TPU v7x, 128 devices: a whole 4x4x4 slice. The times are simulated.
128 devices in a mesh: tm: 32 (over y, x, core), panel: 4 (over z).
Axes of the slice: x: 4, y: 4, z: 4, core: 2. Of those that a mesh axis runs over, the one named last changes fastest.
Arguments:
- observed: bfloat16 [16384, 4096], P('tm', 'panel'), may hold values from -12 to 12
- present: int32 [128, 4096], P('tm', 'panel'), may hold values 0 or 1
- loadings: bfloat16 [4096, 256], P('panel'), may hold values from -0.09375 to 0.09375
- noise_var: float32 [4096], P('panel'), may hold values from 1 to 4
- decay_rate: float32 [256], replicated, may hold values from 6.1035157e-06 to 0.03
- panel_of_block: int32 [32], P('panel'), may hold values from 0 to 18
Outputs:
- smoothed: float32 [16384, 256], P('tm')
- loading_moment: float32 [256, 4096], P('tm', 'panel')
- state_moment: float32 [256, 256], replicated
- panel_var: float32 [19], replicated
All inputs are finite; a program needn't handle non-finite values. No bound on the sum of `present` on one device may be relied on, other than what follows from the above.
Results may differ from a plain program's by a relative error of at most 0.00055.
Values sent between devices are 32-bit elements; how exact they have to be, the bound alone decides.
No kernel may reach another device: no remote copies, remote signals or barrier semaphores. Data moves between devices by JAX's collectives and lax.ppermute only.
A program may use at most 128 MiB of HBM per device.

v0:
```python
import math

import jax
import jax.numpy as jnp
from jax import lax
from jax.experimental import pallas as pl
from jax.experimental.pallas import tpu as pltpu
from jax.sharding import Mesh
from jax.sharding import PartitionSpec as P


SER_BLOCK = 128
PANELS = 19
LEVELS = 7
BLOCK = 128
TM = ("tm_0", "tm_1", "tm_2")
F32 = jnp.float32
BF16 = jnp.bfloat16
HIGH = lax.Precision.HIGHEST
VMEM = pl.BlockSpec(memory_space=pltpu.VMEM)
SMEM = pl.BlockSpec(memory_space=pltpu.SMEM)


def split(x):
    hi = x.astype(BF16)
    return hi, (x - hi.astype(F32)).astype(BF16)


def dot(a, b, dims=((1,), (0,))):
    return lax.dot_general(a, b, (dims, ((), ())), preferred_element_type=F32)


def dot3(a, b, dims=((1,), (0,))):
    return dot(a[0], b[0], dims) + (dot(a[0], b[1], dims) + dot(a[1], b[0], dims))


def grid_iota(n, axis):
    return lax.broadcasted_iota(jnp.int32, (n, n), axis)


def eye(n):
    return (grid_iota(n, 0) == grid_iota(n, 1)).astype(F32)


def pack(sym):
    n = sym.shape[0] // 2
    first, corner, second = sym[:n, :n], sym[:n, n:], sym[n:, n:]
    mixed = jnp.where(grid_iota(n, 0) >= grid_iota(n, 1), first, second)
    diag = jnp.sum(second * eye(n), axis=0, keepdims=True)
    return corner, mixed, jnp.broadcast_to(diag, (8, n))


def store_packed(ref, sym):
    n = sym.shape[0] // 2
    corner, mixed, diag = pack(sym)
    ref[0:n, :] = corner
    ref[n : 2 * n, :] = mixed
    ref[2 * n : 2 * n + 8, :] = diag


def unpack(packed):
    n = packed.shape[1]
    corner, mixed, diag = packed[:n], packed[n : 2 * n], packed[2 * n : 2 * n + 1]
    turned = mixed.T
    row, col = grid_iota(n, 0), grid_iota(n, 1)
    first = jnp.where(row >= col, mixed, turned)
    second = jnp.where(row == col, diag, jnp.where(row < col, mixed, turned))
    return jnp.concatenate(
        [jnp.concatenate([first, corner], axis=1), jnp.concatenate([corner.T, second], axis=1)],
        axis=0,
    )


def gram_kernel(place, present_in, noise_in, loads_in, decay_in, turned, decay, o0, o1, o2, o3,
                present, noise, loads, sems):
    copies = [
        pltpu.make_async_copy(present_in, present, sems.at[0]),
        pltpu.make_async_copy(noise_in, noise, sems.at[1]),
        pltpu.make_async_copy(loads_in, loads, sems.at[2]),
        pltpu.make_async_copy(decay_in, decay, sems.at[3]),
    ]
    for c in copies:
        c.start()
    for c in copies:
        c.wait()
    coef = loads[...]
    flipped = coef.astype(F32).T
    turned[...] = flipped.astype(BF16)
    inv_noise = 1.0 / noise[...]
    for k, out in enumerate((o0, o1, o2, o3)):
        b = lax.rem(place[3] + k, 4)
        weight = present[pl.ds(b, 1), :].astype(F32) * inv_noise
        hi, lo = split(flipped * weight)
        store_packed(out, dot(hi, coef) + dot(lo, coef))


def project_kernel(place, present, noise, loads, observed, *outs):
    coef = loads[...]
    inv_noise = 1.0 / noise[...]
    for k in range(len(outs)):
        b = lax.rem(place[3] + k, len(outs))
        weight = present[pl.ds(b, 1), :].astype(F32) * inv_noise
        rows = observed[pl.ds(pl.multiple_of(b * BLOCK, BLOCK), BLOCK), :].astype(F32)
        hi, lo = split(rows * weight)
        outs[k][...] = dot(hi, coef) + dot(lo, coef)


def inverse_kernel(decay, g0, g1, g2, g3, out, guess):
    gram = unpack((g0[...] + g1[...]) + (g2[...] + g3[...]))
    n = gram.shape[0]
    ident = eye(n)
    whole = ident + gram
    size = jnp.max(jnp.sum(jnp.abs(gram), axis=1, keepdims=True))
    frob = jnp.sqrt(jnp.max(jnp.sum(jnp.sum(gram * gram, axis=1, keepdims=True), axis=0, keepdims=True)))
    top = 1.0 + jnp.minimum(size, frob) * 1.001
    scale = 2.0 / (1.0 + top)
    start = (top - 1.0) / (top + 1.0)
    guess[...] = (2.0 * scale) * ident - (scale * scale) * whole

    def improve(x):
        rest = 2.0 * ident - jnp.dot(whole, x, precision=HIGH, preferred_element_type=F32)
        return jnp.dot(x, rest, precision=HIGH, preferred_element_type=F32)

    def body(err):
        guess[...] = improve(guess[...])
        return err * err

    lax.while_loop(lambda err: err > 1e-4, body, start * start)
    inverse = improve(guess[...])
    gain = jnp.dot(gram, inverse, precision=HIGH, preferred_element_type=F32)
    gain = 0.5 * (gain + gain.T)
    rho = 1.0 - decay[...]
    root = jnp.sqrt(rho)
    root_down = jnp.sum(ident * root, axis=1, keepdims=True)
    store_packed(out, ident * (1.0 - rho) + gain * root * root_down)


def shifted(rows, offset, ahead):
    n = rows.shape[0]
    at = lax.broadcasted_iota(jnp.int32, rows.shape, 0)
    if ahead:
        return jnp.where(at >= offset, pltpu.roll(rows, offset, 0), 0.0)
    return jnp.where(at < n - offset, pltpu.roll(rows, n - offset, 0), 0.0)


def end_kernel(decay, packed, p0, p1, p2, p3, total, out, err_ref):
    n = decay.shape[1]
    half = n // 2
    proj = (p0[...] + p1[...]) + (p2[...] + p3[...])
    total[...] = proj
    out[0 : n + 8, :] = packed[...]
    err = unpack(packed[...])
    z = proj * lax.rsqrt(1.0 - decay[...])
    v = z - dot3(split(z), split(err))
    err_ref[...] = err
    rows = BLOCK
    for level in range(LEVELS):
        pair = split(err_ref[...])
        v = v + shifted(v - dot3(split(v), pair), 1 << level, True)
        if level + 1 < LEVELS:
            err_ref[...] = 2.0 * err_ref[...] - dot3(pair, pair)
    out[n + 8 : n + 16, :] = jnp.broadcast_to(v[rows - 1 :, :half], (8, half))
    out[n + 16 :, :] = jnp.broadcast_to(v[rows - 1 :, half:], (8, half))


def powers_kernel(place, e0, e1, e2, e3, his, los, tops, ends, whole, errs):
    nb = 4
    n = 2 * e0.shape[1]
    half = n // 2
    for k, e in enumerate((e0, e1, e2, e3)):
        b = lax.rem(place[3] + nb - k, nb)
        errs[b] = unpack(e[0 : n + 8, :])
        ends[b, :, 0:half] = e[n + 8 : n + 16, :]
        ends[b, :, half:] = e[n + 16 :, :]
    for level in range(LEVELS):
        for b in range(nb):
            err = errs[b]
            pair = split(err)
            his[level * nb + b] = pair[0]
            los[level * nb + b] = pair[1]
            errs[b] = 2.0 * err - dot3(pair, pair)
    total, end = errs[0], ends[0]
    tops[0] = total
    for b in range(1, nb):
        err = errs[b]
        tops[b] = err
        pair = split(err)
        end = end - dot3(split(end), pair) + ends[b]
        total = total + err - dot3(split(total), pair)
    whole[0:n, :] = total
    whole[n:, :] = end


def join(maps):
    n = maps[0].shape[1]
    total, end = maps[0][:n], maps[0][n:]
    for m in maps[1:]:
        err = m[:n]
        pair = split(err)
        end = end - dot3(split(end), pair) + m[n:]
        total = total + err - dot3(split(total), pair)
    return total, end


def store_map(total, end, core, out, half):
    n = total.shape[1]
    h = n // 2
    out[0:n, :] = total
    out[n:, :] = end
    half[0:h, :] = out[pl.ds(pl.multiple_of(core * h, h), h), :]
    half[h:, :] = end


def pair_kernel(place, mine, other, out, half):
    own, far = mine[...], other[...]
    first = place[2] == 0
    total, end = join([jnp.where(first, own, far), jnp.where(first, far, own)])
    store_map(total, end, place[2], out, half)


def ordered(place, refs, scratch):
    for k, r in enumerate(refs):
        scratch[lax.rem(place + len(refs) - k, len(refs))] = r[...]


def ordered_maps(place, core, own, halves, maps):
    n = own.shape[1]
    h = n // 2
    maps[place] = own[...]
    for k, (mine, other) in enumerate(halves):
        at = lax.rem(place + 3 - k, 4)
        maps[at, pl.ds(pl.multiple_of(core * h, h), h), :] = mine[0:h, :]
        maps[at, pl.ds(pl.multiple_of((1 - core) * h, h), h), :] = other[0:h, :]
        maps[at, n:, :] = mine[h:, :]


def group_kernel(place, own, m1, m2, m3, o1, o2, o3, out, half, maps):
    ordered_maps(place[1], place[2], own, ((m1, o1), (m2, o2), (m3, o3)), maps)
    total, end = join([maps[k] for k in range(4)])
    store_map(total, end, place[2], out, half)


def advance(state, m):
    n = state.shape[1]
    return state - dot3(split(state), split(m[:n])) + m[n:]


def retreat(state, err):
    return state - dot3(split(state), split(err), ((1,), (1,)))


def scan_rows(values, his, los, nb, ahead):
    for level in range(LEVELS):
        for b in range(nb):
            v = values[b]
            pair = (his[level * nb + b], los[level * nb + b])
            values[b] = v + shifted(v - dot3(split(v), pair), 1 << level, ahead)


def forward_kernel(place, decay, own, m1, m2, m3, o1, o2, o3, xs, other, p0, p1, p2, p3,
                   ends, his, los, tops,
                   past, change, firsts, first, ys, values, states):
    nb = 4
    root_inv = lax.rsqrt(1.0 - decay[...])
    ordered(place[3], (p0, p1, p2, p3), values)
    ordered_maps(place[0], place[2], own, ((m1, o1), (m2, o2), (m3, o3)), ys)
    n = decay.shape[1]
    state = jnp.zeros((8, n), F32)
    state = lax.fori_loop(0, place[0], lambda k, s: advance(s, ys[k]), state)
    state = lax.fori_loop(0, place[1], lambda k, s: advance(s, xs[k]), state)
    state = jnp.where(place[2] == 0, state, advance(state, other[...]))
    at = lax.broadcasted_iota(jnp.int32, (BLOCK, n), 0)
    rho = 1.0 - decay[...]
    for b in range(nb):
        states[b] = state
        if b + 1 < nb:
            state = state - dot3(split(state), split(tops[b])) + ends[b]
    for b in range(nb):
        z = values[b] * root_inv
        z = z + jnp.where(at == 0, states[b][0:1], 0.0)
        values[b] = z - dot3(split(z), (his[b], los[b]))
    scan_rows(values, his, los, nb, True)
    for b in range(nb):
        v = values[b]
        before = jnp.where(at == 0, states[b][0:1], pltpu.roll(v, 1, 0)) * rho
        past[b] = before
        change[b] = v - before
        values[b] = v - before
    scan_rows(values, his, los, nb, False)
    back = jnp.zeros((8, n), F32)
    for b in reversed(range(nb)):
        lead = jnp.broadcast_to(values[b][0:1], (8, n))
        firsts[b] = lead
        back = back - dot3(split(back), split(tops[b])) + lead
    first[...] = back


def pair_back_kernel(place, own, far, mine, other, out):
    n = mine.shape[1]
    lead = place[2] == 0
    early_q = jnp.where(lead, own[...], far[...])
    late_q = jnp.where(lead, far[...], own[...])
    early = jnp.where(lead, mine[0:n, :], other[0:n, :])
    out[...] = early_q + retreat(late_q, early)


def group_back_kernel(place, q0, q1, q2, q3, xs, out, qs):
    n = xs.shape[2]
    ordered(place[1], (q0, q1, q2, q3), qs)
    q = qs[3]
    for k in (2, 1, 0):
        q = qs[k] + retreat(q, xs[k, 0:n, :])
    out[...] = q


def smooth_kernel(place, decay, gy0, gy1, gy2, gy3, gxs, far, ys, xs, other,
                  past, change, firsts, his, los, tops,
                  smoothed, high, low, quarter, gys, values, states, moment):
    nb = 4
    nseg = 4
    ordered(place[0], (gy0, gy1, gy2, gy3), gys)
    n = decay.shape[1]
    back = jnp.zeros((8, n), F32)

    def over(gs, ms):
        def step(k, s):
            j = nseg - 1 - k
            return gs[j] + retreat(s, ms[j, 0:n, :])

        return step

    back = lax.fori_loop(0, nseg - 1 - place[0], over(gys, ys), back)
    back = lax.fori_loop(0, nseg - 1 - place[1], over(gxs, xs), back)
    back = jnp.where(place[2] == 0, far[...] + retreat(back, other[0:n, :]), back)
    at = lax.broadcasted_iota(jnp.int32, (BLOCK, n), 0)
    for b in reversed(range(nb)):
        states[b] = back
        if b:
            back = back - dot3(split(back), split(tops[b])) + firsts[b]
    for b in range(nb):
        s = states[b]
        step = s - dot3(split(s), (his[b], los[b]))
        values[b] = change[b] + jnp.where(at == BLOCK - 1, step[0:1], 0.0)
    scan_rows(values, his, los, nb, False)
    root_inv = lax.rsqrt(1.0 - decay[...])
    for b in range(nb):
        smoothed[b * BLOCK : (b + 1) * BLOCK, :] = (values[b] + past[b]) * root_inv
    pair = split(smoothed[...])
    high[...], low[...] = pair
    moment[...] = dot3(pair, pair, ((0,), (0,))) * (1.0 / (128 * BLOCK))
    quarter[...] = moment[pl.ds(pl.multiple_of(place[3] * 64, 64), 64), :]


def errors_kernel(panel_of, high, low, observed, present, turned, sums_out):
    nb = 4
    n, series = turned.shape
    coef = turned[...]
    weight = present[...].astype(F32)
    squares = jnp.zeros((1, series), F32)
    for b in range(nb):
        part = slice(b * BLOCK, (b + 1) * BLOCK)
        miss = observed[part, :].astype(F32) - (dot(high[part, :], coef) + dot(low[part, :], coef))
        squares = squares + jnp.sum(miss * miss, axis=0, keepdims=True) * weight[b : b + 1]
    counts = float(BLOCK) * jnp.sum(weight, axis=0, keepdims=True)
    lane = lax.broadcasted_iota(jnp.int32, (8, n), 1)
    line = lax.broadcasted_iota(jnp.int32, (8, n), 0)
    sums = jnp.zeros((8, n), F32)
    for j in range(series // SER_BLOCK):
        part = slice(j * SER_BLOCK, (j + 1) * SER_BLOCK)
        sq = jnp.sum(squares[:, part], axis=1, keepdims=True)
        ct = jnp.sum(counts[:, part], axis=1, keepdims=True)
        here = lane == panel_of[j]
        sums = sums + jnp.where(here & (line == 0), sq, 0.0) + jnp.where(here & (line == 1), ct, 0.0)
    sums_out[...] = sums


def moment_kernel(place, high, low, observed, present, own_part, far_part, moment):
    nb = 4
    weight = present[...].astype(F32)
    kept = jnp.concatenate(
        [
            (observed[b * BLOCK : (b + 1) * BLOCK, :].astype(F32) * weight[b : b + 1]).astype(BF16)
            for b in range(nb)
        ],
        axis=0,
    )
    both = ((0,), (0,))
    scale = 1.0 / math.sqrt(128 * BLOCK)
    moment[...] = (dot(high[...], kept, both) + dot(low[...], kept, both)) * scale
    for i in range(16):
        own_part[i] = moment[pl.ds(pl.multiple_of((2 * i + place[2]) * 8, 8), 8), :]
        far_part[i] = moment[pl.ds(pl.multiple_of((2 * i + 1 - place[2]) * 8, 8), 8), :]


def add_kernel(a, b, out):
    out[...] = a[...] + b[...]


def small_kernel(q, q_far, s, s_far, out):
    out[0:64, :] = q[...] + q_far[...]
    out[64:72, :] = s[...] + s_far[...]


def sum_kernel(a, b, c, d, out):
    out[...] = (a[...] + b[...]) + (c[...] + d[...])


def finish_kernel(place, s0, s1, s2, s3, out, var):
    sums = jnp.zeros((8, s0.shape[1]), F32)
    for k, s in enumerate((s0, s1, s2, s3)):
        at = lax.rem(place[3] + 4 - k, 4)
        out[pl.ds(pl.multiple_of(at * 64, 64), 64), :] = s[0:64, :]
        sums = sums + s[64:72, :]
    var[...] = jnp.broadcast_to(sums[0:1] / jnp.maximum(sums[1:2], 1.0), var.shape)


def call(kernel, outs, scratch, *args, smem=1, far=0, sems=0, mib=12):
    shapes = [jax.ShapeDtypeStruct(s, d) for s, d in outs]
    specs = [SMEM] * smem + [pl.BlockSpec(memory_space=pltpu.HBM)] * far
    specs += [VMEM] * (len(args) - smem - far)
    made = pl.pallas_call(
        kernel,
        out_shape=shapes,
        in_specs=specs,
        out_specs=[VMEM] * len(outs),
        scratch_shapes=[pltpu.VMEM(s, d) for s, d in scratch]
        + ([pltpu.SemaphoreType.DMA((sems,))] if sems else []),
        compiler_params=pltpu.CompilerParams(vmem_limit_bytes=mib << 20),
    )
    return made(*args)


def from_peers(arrays, axis):
    n = lax.axis_size(axis)
    out = [arrays[0]]
    for k in range(1, n):
        out.append(lax.ppermute(arrays[k], axis, [(i, (i + k) % n) for i in range(n)]))
    return out


def gather(array, axis):
    return from_peers([array] * lax.axis_size(axis), axis)


def swap(array, axis):
    return lax.ppermute(array, axis, [(0, 1), (1, 0)])


def step(observed, present, loadings, noise_var, decay_rate, panel_of_block):
    time_rows, series = observed.shape
    width = loadings.shape[1]
    nb = time_rows // BLOCK
    half = width // 2
    ay, ax, ac = TM
    iy, ix, ic, iz = (lax.axis_index(a) for a in (ay, ax, ac, "panel"))
    scalar = lambda *v: jnp.stack([jnp.int32(i) for i in v])
    place = scalar(iy, ix, ic, iz)
    noise = noise_var.reshape(1, series)
    packed = ((width + 8, half), F32)
    packed_end = ((width + 24, half), F32)
    map_shape = ((width + 8, width), F32)
    half_shape = ((half + 8, width), F32)
    vec = ((8, width), F32)
    vecs4 = ((4, 8, width), F32)
    maps4 = ((4, width + 8, width), F32)
    rows2 = ((BLOCK, width), F32)
    rows3 = ((nb, BLOCK, width), F32)
    square = ((width, width), F32)
    squares4 = ((nb, width, width), F32)
    powers = ((LEVELS * nb, width, width), BF16)

    turned, decay, *grams = call(
        gram_kernel, [((width, series), BF16), ((1, width), F32)] + [packed] * nb,
        [(present.shape, jnp.int32), ((1, series), F32), ((series, width), BF16)],
        place, present, noise, loadings, decay_rate.reshape(1, width), far=4, sems=4,
    )
    projs = call(project_kernel, [rows2] * nb, [], place, present, noise, loadings, observed)
    grams = from_peers(grams, "panel")
    projs = from_peers(projs, "panel")
    (err,) = call(inverse_kernel, [packed], [square], decay, *grams, smem=0)
    proj, err_end = call(end_kernel, [rows2, packed_end], [square], decay, err, *projs, smem=0)
    errs = gather(err_end, "panel")
    his, los, tops, ends, seg = call(
        powers_kernel,
        [powers, powers, squares4, vecs4, map_shape],
        [squares4],
        place, *errs,
    )
    seg, proj = lax.optimization_barrier((seg, proj))
    seg_far = swap(seg, ac)
    projs = gather(proj, "panel")
    pair, pair_half = call(pair_kernel, [map_shape, half_shape], [], place, seg, seg_far)
    near = gather(pair_half, ax)[1:]
    group, group_half, xs = call(
        group_kernel, [map_shape, half_shape, maps4], [],
        place, pair, *near, *[swap(m, ac) for m in near],
    )
    near = gather(group_half, ay)[1:]
    past, change, firsts, first, ys = call(
        forward_kernel,
        [rows3, rows3, vecs4, vec, maps4],
        [rows3, vecs4],
        place, decay, group, *near, *[swap(m, ac) for m in near],
        xs, seg_far, *projs, ends, his, los, tops,
    )
    first_far = swap(first, ac)
    (pair_first,) = call(pair_back_kernel, [vec], [], place, first, first_far, seg, seg_far)
    group_first, gxs = call(
        group_back_kernel, [vec, vecs4], [], place, *gather(pair_first, ax), xs
    )
    flat = ((time_rows, width), BF16)
    smoothed, high, low, quarter = call(
        smooth_kernel,
        [((time_rows, width), F32), flat, flat, ((64, width), F32)],
        [vecs4, rows3, vecs4, square],
        place, decay, *gather(group_first, ay), gxs, first_far, ys, xs, seg_far,
        past, change, firsts, his, los, tops,
    )
    quarter_far = swap(quarter, ac)
    (sums,) = call(errors_kernel, [vec], [], panel_of_block, high, low, observed, present, turned)
    small_shape = ((72, width), F32)
    (small,) = call(small_kernel, [small_shape], [], quarter, quarter_far, sums, swap(sums, ac), smem=0)
    (small,) = call(sum_kernel, [small_shape], [], *gather(small, ax), smem=0)
    part = ((16, 8, series), F32)
    own_part, far_part = call(
        moment_kernel, [part, part], [((width, series), F32)], place, high, low, observed, present
    )
    (own_part,) = call(add_kernel, [part], [], own_part, swap(far_part, ac), smem=0)
    arrived = lax.all_to_all(own_part, (ay, ax), 0, 0, tiled=True)
    loading_moment = arrived.sum(axis=0)
    (small,) = call(sum_kernel, [small_shape], [], *gather(small, ay), smem=0)
    state_moment, var = call(finish_kernel, [square, vec], [], place, *gather(small, "panel"))
    return smoothed, loading_moment, state_moment, var[0, :PANELS]


def solution(mesh):
    finer = Mesh(
        mesh.devices.reshape(4, 4, 2, mesh.shape["panel"]), ("tm_0", "tm_1", "tm_2", "panel")
    )
    in_specs = (P(TM, "panel"), P(TM, "panel"), P("panel", None), P("panel"), P(), P("panel"))
    out_specs = (P(TM, None), P(TM, "panel"), P(), P())
    return jax.shard_map(step, mesh=finer, in_specs=in_specs, out_specs=out_specs, check_vma=False)
```

profile of v0, /device:TPU:1, one launch (start us, length us, event | category | flops | bytes accessed | tf_op | source)
XLA Modules:
  0.0 150.4 jit_solution(1946886438240856108)
XLA Ops:
  0.7 1.0 copy-done.2
  3.8 2.1 %shard_map.93 = (bf16[256,1024]{1,0:T(8,128)(2,1)S(1)}, f32[1,256]{1,0:T(1,128)S(1)}, f32[264,128]{1,0:T(8,128)S(1)}, f32[264,128]{1,0:T(8,128)S(1)}, f32[264,128]{1,0:T(8,128)S(1)}, /*index=5*/f32[264,128]{1,0:T(8,128)S(1)}) custom-call(s32[4]{0:T(128)S(1)} %pad_add_fusion.place, s32[4,1024]{1,0:T(4,128)S(1)} %copy-done.3, f32[1,1024]{1,0:T(1,128)S(1)} %bitcast.8, ...), custom_call_target="tpu_custom_call" | custom-call | tf_op jit(solution)/shard_map/pallas_call | solution.py:430
  5.9 2.5 %collective-permute-start = (f32[264,128]{1,0:T(8,128)S(1)}, f32[264,128]{1,0:T(8,128)S(1)}, u32[]{:S(2)}, u32[]{:S(2)}) collective-permute-start(f32[264,128]{1,0:T(8,128)S(1)} %get-tuple-element.45), channel_id=1, source_target_pairs={{0,1},{1,2},{2,3},{3,0},{4,5},{5,6},{6,7},{7,4},{8,9},{9,10},{10,1... | collective-permute-start | bytes 405512 | tf_op jit(solution)/shard_map/ppermute | solution.py:437
  8.4 3.3 %collective-permute-start.1 = (f32[264,128]{1,0:T(8,128)S(1)}, f32[264,128]{1,0:T(8,128)S(1)}, u32[]{:S(2)}, u32[]{:S(2)}) collective-permute-start(f32[264,128]{1,0:T(8,128)S(1)} %get-tuple-element.46), channel_id=1, source_target_pairs={{0,2},{1,3},{2,0},{3,1},{4,6},{5,7},{6,4},{7,5},{8,10},{9,11},{10,... | collective-permute-start | bytes 405512 | tf_op jit(solution)/shard_map/ppermute | solution.py:437
  11.7 0.7 collective-permute-start.2
  12.5 1.2 copy-done
  13.7 1.3 shard_map.95
  15.0 0.8 collective-permute-start.3
  16.3 2.0 %collective-permute-start.5 = (f32[128,256]{1,0:T(8,128)S(1)}, f32[128,256]{1,0:T(8,128)S(1)}, u32[]{:S(2)}, u32[]{:S(2)}) collective-permute-start(f32[128,256]{1,0:T(8,128)S(1)} %get-tuple-element.51), channel_id=1, source_target_pairs={{0,3},{1,0},{2,1},{3,2},{4,7},{5,4},{6,5},{7,6},{8,11},{9,8},{10,9... | collective-permute-start | bytes 393224 | tf_op jit(solution)/shard_map/ppermute | solution.py:437
  18.3 4.1 %shard_map.94.packed = f32[264,128]{1,0:T(8,128)S(1)} custom-call(f32[1,256]{1,0:T(1,128)S(1)} %get-tuple-element.43.decay, f32[264,128]{1,0:T(8,128)S(1)} %get-tuple-element.44.g0, f32[264,128]{1,0:T(8,128)S(1)} %collective-permute-done.g1, f32[264,128]{1,0:T(8,128)S(1)} %collective-permute-done.1.g2, f32[264,128]{1,0:T(8,128)S(1)} %collective-permute-done.2.g3), custom_call_target="tpu_custom_call" | custom-call | tf_op jit(solution)/shard_map/pallas_call | solution.py:430
  22.5 0.8 collective-permute-done.4.p2
  23.3 2.9 %shard_map.96 = (f32[128,256]{1,0:T(8,128)S(1)}, f32[280,128]{1,0:T(8,128)S(1)}) custom-call(f32[1,256]{1,0:T(1,128)S(1)} %get-tuple-element.43.decay, f32[264,128]{1,0:T(8,128)S(1)} %shard_map.94.packed, f32[128,256]{1,0:T(8,128)S(1)} %get-tuple-element.48.p0, f32[128,256]{1,0:T(8,128)S(1)} %collective-permute-done.3.p1, ...), custom_call_target="tpu_custom_call" | custom-call | tf_op jit(solution)/shard_map/pallas_call | solution.py:430
  26.1 3.4 %collective-permute-start.8 = (f32[280,128]{1,0:T(8,128)S(1)}, f32[280,128]{1,0:T(8,128)S(1)}, u32[]{:S(2)}, u32[]{:S(2)}) collective-permute-start(f32[280,128]{1,0:T(8,128)S(1)} %get-tuple-element.52.e0), channel_id=1, source_target_pairs={{0,3},{1,0},{2,1},{3,2},{4,7},{5,4},{6,5},{7,6},{8,11},{9,8},{10,9... | collective-permute-start | bytes 430088 | tf_op jit(solution)/shard_map/ppermute | solution.py:437
  30.3 3.3 %collective-permute-done.8.e3 = f32[280,128]{1,0:T(8,128)S(1)} collective-permute-done((f32[280,128]{1,0:T(8,128)S(1)}, f32[280,128]{1,0:T(8,128)S(1)}, u32[]{:S(2)}, u32[]{:S(2)}) %collective-permute-start.8) | collective-permute-done | bytes 143392 | tf_op jit(solution)/shard_map/ppermute | solution.py:437
  33.6 1.6 %collective-permute-done.7.e2 = f32[280,128]{1,0:T(8,128)S(1)} collective-permute-done((f32[280,128]{1,0:T(8,128)S(1)}, f32[280,128]{1,0:T(8,128)S(1)}, u32[]{:S(2)}, u32[]{:S(2)}) %collective-permute-start.7) | collective-permute-done | bytes 143392 | tf_op jit(solution)/shard_map/ppermute | solution.py:437
  35.1 3.7 %collective-permute-done.6.e1 = f32[280,128]{1,0:T(8,128)S(1)} collective-permute-done((f32[280,128]{1,0:T(8,128)S(1)}, f32[280,128]{1,0:T(8,128)S(1)}, u32[]{:S(2)}, u32[]{:S(2)}) %collective-permute-start.6) | collective-permute-done | bytes 143392 | tf_op jit(solution)/shard_map/ppermute | solution.py:437
  38.9 5.3 %shard_map.97 = (bf16[28,256,256]{2,1,0:T(8,128)(2,1)S(1)}, bf16[28,256,256]{2,1,0:T(8,128)(2,1)S(1)}, f32[4,256,256]{2,1,0:T(8,128)S(1)}, f32[4,8,256]{2,1,0:T(8,128)S(1)}, f32[264,256]{1,0:T(8,128)S(1)}) custom-call(s32[4]{0:T(128)S(1)} %pad_add_fusion.place, f32[280,128]{1,0:T(8,128)S(1)} %get-tuple-element.52.e0, ...), custom_call_target="tpu_custom_call" | custom-call | tf_op jit(solution)/shard_map/pallas_call | solution.py:430
  44.1 1.3 collective-permute-start.9
  45.4 1.2 collective-permute-done.9.other
  46.6 0.9 shard_map.98
  47.4 2.5 %collective-permute-start.12 = (f32[136,256]{1,0:T(8,128)S(1)}, f32[136,256]{1,0:T(8,128)S(1)}, u32[]{:S(2)}, u32[]{:S(2)}) collective-permute-start(f32[136,256]{1,0:T(8,128)S(1)} %get-tuple-element.57), channel_id=1, source_target_pairs={{0,24},{8,0},{16,8},{24,16},{1,25},{9,1},{17,9},{25,17},{2,26},{10... | collective-permute-start | bytes 417800 | tf_op jit(solution)/shard_map/ppermute | solution.py:437
  51.1 2.2 %collective-permute-done.12.m3 = f32[136,256]{1,0:T(8,128)S(1)} collective-permute-done((f32[136,256]{1,0:T(8,128)S(1)}, f32[136,256]{1,0:T(8,128)S(1)}, u32[]{:S(2)}, u32[]{:S(2)}) %collective-permute-start.12) | collective-permute-done | bytes 139296 | tf_op jit(solution)/shard_map/ppermute | solution.py:437
  53.3 3.5 %collective-permute-start.15 = (f32[136,256]{1,0:T(8,128)S(1)}, f32[136,256]{1,0:T(8,128)S(1)}, u32[]{:S(2)}, u32[]{:S(2)}) collective-permute-start(f32[136,256]{1,0:T(8,128)S(1)} %collective-permute-done.12.m3), channel_id=1, source_target_pairs={{0,4},{4,0},{1,5},{5,1},{2,6},{6,2},{3,7},{7,3},{8,12},{12,8},{9,1... | collective-permute-start | bytes 417800 | tf_op jit(solution)/shard_map/ppermute | solution.py:446
  56.9 1.8 %collective-permute-start.14 = (f32[136,256]{1,0:T(8,128)S(1)}, f32[136,256]{1,0:T(8,128)S(1)}, u32[]{:S(2)}, u32[]{:S(2)}) collective-permute-start(f32[136,256]{1,0:T(8,128)S(1)} %collective-permute-done.11.m2), channel_id=1, source_target_pairs={{0,4},{4,0},{1,5},{5,1},{2,6},{6,2},{3,7},{7,3},{8,12},{12,8},{9,1... | collective-permute-start | bytes 417800 | tf_op jit(solution)/shard_map/ppermute | solution.py:446
  58.7 1.4 collective-permute-done.10.m1
  60.6 1.0 collective-permute-done.13.o1
  61.5 1.5 %shard_map.99 = (f32[264,256]{1,0:T(8,128)S(1)}, f32[136,256]{1,0:T(8,128)S(1)}, f32[4,264,256]{2,1,0:T(8,128)S(1)}) custom-call(s32[4]{0:T(128)S(1)} %pad_add_fusion.place, f32[264,256]{1,0:T(8,128)S(1)} %get-tuple-element.56.own, f32[136,256]{1,0:T(8,128)S(1)} %collective-permute-done.10.m1, f32[136,256]{1,0:T(8,128)S(1)} %collective-permute-done.11.m2, ...), custom_call_target="tpu_custom_call" | custom-call | tf_op jit(solution)/shard_map/pallas_call | solution.py:430
  63.1 2.8 %collective-permute-start.18 = (f32[136,256]{1,0:T(8,128)S(1)}, f32[136,256]{1,0:T(8,128)S(1)}, u32[]{:S(2)}, u32[]{:S(2)}) collective-permute-start(f32[136,256]{1,0:T(8,128)S(1)} %get-tuple-element.59), channel_id=1, source_target_pairs={{0,96},{32,0},{64,32},{96,64},{1,97},{33,1},{65,33},{97,65},{2,98}... | collective-permute-start | bytes 417800 | tf_op jit(solution)/shard_map/ppermute | solution.py:437
  67.5 3.9 %collective-permute-done.18.m3 = f32[136,256]{1,0:T(8,128)S(1)} collective-permute-done((f32[136,256]{1,0:T(8,128)S(1)}, f32[136,256]{1,0:T(8,128)S(1)}, u32[]{:S(2)}, u32[]{:S(2)}) %collective-permute-start.18) | collective-permute-done | bytes 139296 | tf_op jit(solution)/shard_map/ppermute | solution.py:437
  71.4 1.3 collective-permute-start.21
  72.7 1.9 %collective-permute-start.20 = (f32[136,256]{1,0:T(8,128)S(1)}, f32[136,256]{1,0:T(8,128)S(1)}, u32[]{:S(2)}, u32[]{:S(2)}) collective-permute-start(f32[136,256]{1,0:T(8,128)S(1)} %collective-permute-done.17.m2), channel_id=1, source_target_pairs={{0,4},{4,0},{1,5},{5,1},{2,6},{6,2},{3,7},{7,3},{8,12},{12,8},{9,1... | collective-permute-start | bytes 417800 | tf_op jit(solution)/shard_map/ppermute | solution.py:446
  74.6 1.3 collective-permute-done.16.m1
  76.7 0.9 collective-permute-start.22
  77.6 5.4 %collective-permute-done.23.p2 = f32[128,256]{1,0:T(8,128)S(1)} collective-permute-done((f32[128,256]{1,0:T(8,128)S(1)}, f32[128,256]{1,0:T(8,128)S(1)}, u32[]{:S(2)}, u32[]{:S(2)}) %collective-permute-start.23) | collective-permute-done | bytes 131104 | tf_op jit(solution)/shard_map/ppermute | solution.py:437
  83.0 3.2 %collective-permute-done.22.p1 = f32[128,256]{1,0:T(8,128)S(1)} collective-permute-done((f32[128,256]{1,0:T(8,128)S(1)}, f32[128,256]{1,0:T(8,128)S(1)}, u32[]{:S(2)}, u32[]{:S(2)}) %collective-permute-start.22) | collective-permute-done | bytes 131104 | tf_op jit(solution)/shard_map/ppermute | solution.py:437
  86.2 5.5 %shard_map.100 = (f32[4,128,256]{2,1,0:T(8,128)S(1)}, f32[4,128,256]{2,1,0:T(8,128)S(1)}, f32[4,8,256]{2,1,0:T(8,128)S(1)}, f32[8,256]{1,0:T(8,128)S(1)}, f32[4,264,256]{2,1,0:T(8,128)S(1)}) custom-call(s32[4]{0:T(128)S(1)} %pad_add_fusion.place, f32[1,256]{1,0:T(1,128)S(1)} %get-tuple-element.43.decay, f32[264,256]{1,0:T(8,128)S(1)} %get-tuple-element.58.own, ...), custom_call_target="tpu_custom_call" | custom-call | tf_op jit(solution)/shard_map/pallas_call | solution.py:430
  92.2 0.8 collective-permute-done.25.far
  93.8 0.8 collective-permute-start.28
  94.8 0.8 collective-permute-start.26
  95.5 0.8 collective-permute-done.28.q3
  96.4 2.3 %collective-permute-done.27.q2 = f32[8,256]{1,0:T(8,128)S(1)} collective-permute-done((f32[8,256]{1,0:T(8,128)S(1)}, f32[8,256]{1,0:T(8,128)S(1)}, u32[]{:S(2)}, u32[]{:S(2)}) %collective-permute-start.27) | collective-permute-done | bytes 8224 | tf_op jit(solution)/shard_map/ppermute | solution.py:437
  98.8 1.3 shard_map.102
  100.0 0.9 collective-permute-start.31
  101.6 0.9 collective-permute-done.31.gy3
  102.6 2.4 %collective-permute-done.30.gy2 = f32[8,256]{1,0:T(8,128)S(1)} collective-permute-done((f32[8,256]{1,0:T(8,128)S(1)}, f32[8,256]{1,0:T(8,128)S(1)}, u32[]{:S(2)}, u32[]{:S(2)}) %collective-permute-start.30) | collective-permute-done | bytes 8224 | tf_op jit(solution)/shard_map/ppermute | solution.py:437
  105.0 5.7 %shard_map.103 = (f32[512,256]{1,0:T(8,128)}, bf16[512,256]{1,0:T(8,128)(2,1)S(1)}, bf16[512,256]{1,0:T(8,128)(2,1)S(1)}, f32[64,256]{1,0:T(8,128)S(1)}) custom-call(s32[4]{0:T(128)S(1)} %pad_add_fusion.place, f32[1,256]{1,0:T(1,128)S(1)} %get-tuple-element.43.decay, f32[8,256]{1,0:T(8,128)S(1)} %get-tuple-element.67.gy0, ...), custom_call_target="tpu_custom_call" | custom-call | tf_op jit(solution)/shard_map/pallas_call | solution.py:430
  110.7 1.3 shard_map.104
  112.1 3.3 %collective-permute-start.32 = (f32[16,8,1024]{2,1,0:T(8,128)S(1)}, f32[16,8,1024]{2,1,0:T(8,128)S(1)}, u32[]{:S(2)}, u32[]{:S(2)}) collective-permute-start(f32[16,8,1024]{2,1,0:T(8,128)S(1)} %get-tuple-element.77), channel_id=1, source_target_pairs={{0,4},{4,0},{1,5},{5,1},{2,6},{6,2},{3,7},{7,3},{8,12},{12,8},{9,1... | collective-permute-start | bytes 1572872 | tf_op jit(solution)/shard_map/ppermute | solution.py:446
  115.5 1.4 collective-permute-done.32.b
  116.9 0.9 shard_map.105
  117.8 3.6 %all-to-all-start = ((f32[16,8,1024]{2,1,0:T(8,128)}), f32[16,8,1024]{2,1,0:T(8,128)S(1)}, u32[]{:S(2)}, u32[]{:S(2)}) async-start(f32[16,8,1024]{2,1,0:T(8,128)} %shard_map.105), calls=%async_computation | async-start | bytes 1048576 | tf_op jit(solution)/shard_map/all_to_all | solution.py:529
  121.4 1.4 shard_map.106.s
  123.3 0.8 collective-permute-done.34.s_far
  124.1 3.2 %collective-permute-start.37 = (f32[72,256]{1,0:T(8,128)S(1)}, f32[72,256]{1,0:T(8,128)S(1)}, u32[]{:S(2)}, u32[]{:S(2)}) collective-permute-start(f32[72,256]{1,0:T(8,128)S(1)} %shard_map.107.a), channel_id=1, source_target_pairs={{0,24},{8,0},{16,8},{24,16},{1,25},{9,1},{17,9},{25,17},{2,26},{10... | collective-permute-start | bytes 221192 | tf_op jit(solution)/shard_map/ppermute | solution.py:437
  128.4 1.9 %collective-permute-done.37.d = f32[72,256]{1,0:T(8,128)S(1)} collective-permute-done((f32[72,256]{1,0:T(8,128)S(1)}, f32[72,256]{1,0:T(8,128)S(1)}, u32[]{:S(2)}, u32[]{:S(2)}) %collective-permute-start.37) | collective-permute-done | bytes 73760 | tf_op jit(solution)/shard_map/ppermute | solution.py:437
  130.3 1.6 %collective-permute-done.36.c = f32[72,256]{1,0:T(8,128)S(1)} collective-permute-done((f32[72,256]{1,0:T(8,128)S(1)}, f32[72,256]{1,0:T(8,128)S(1)}, u32[]{:S(2)}, u32[]{:S(2)}) %collective-permute-start.36) | collective-permute-done | bytes 73760 | tf_op jit(solution)/shard_map/ppermute | solution.py:437
  132.0 2.1 %collective-permute-done.35.b = f32[72,256]{1,0:T(8,128)S(1)} collective-permute-done((f32[72,256]{1,0:T(8,128)S(1)}, f32[72,256]{1,0:T(8,128)S(1)}, u32[]{:S(2)}, u32[]{:S(2)}) %collective-permute-start.35) | collective-permute-done | bytes 73760 | tf_op jit(solution)/shard_map/ppermute | solution.py:437
  134.1 2.5 %collective-permute-start.40 = (f32[72,256]{1,0:T(8,128)S(1)}, f32[72,256]{1,0:T(8,128)S(1)}, u32[]{:S(2)}, u32[]{:S(2)}) collective-permute-start(f32[72,256]{1,0:T(8,128)S(1)} %shard_map.108.a), channel_id=1, source_target_pairs={{0,96},{32,0},{64,32},{96,64},{1,97},{33,1},{65,33},{97,65},{2,98}... | collective-permute-start | bytes 221192 | tf_op jit(solution)/shard_map/ppermute | solution.py:437
  138.0 3.4 %collective-permute-done.39.c = f32[72,256]{1,0:T(8,128)S(1)} collective-permute-done((f32[72,256]{1,0:T(8,128)S(1)}, f32[72,256]{1,0:T(8,128)S(1)}, u32[]{:S(2)}, u32[]{:S(2)}) %collective-permute-start.39) | collective-permute-done | bytes 73760 | tf_op jit(solution)/shard_map/ppermute | solution.py:437
  142.7 0.9 collective-permute-start.41
  143.6 1.7 %collective-permute-done.43.s3 = f32[72,256]{1,0:T(8,128)S(1)} collective-permute-done((f32[72,256]{1,0:T(8,128)S(1)}, f32[72,256]{1,0:T(8,128)S(1)}, u32[]{:S(2)}, u32[]{:S(2)}) %collective-permute-start.43) | collective-permute-done | bytes 73760 | tf_op jit(solution)/shard_map/ppermute | solution.py:437
  145.4 1.9 %collective-permute-done.42.s2 = f32[72,256]{1,0:T(8,128)S(1)} collective-permute-done((f32[72,256]{1,0:T(8,128)S(1)}, f32[72,256]{1,0:T(8,128)S(1)}, u32[]{:S(2)}, u32[]{:S(2)}) %collective-permute-start.42) | collective-permute-done | bytes 73760 | tf_op jit(solution)/shard_map/ppermute | solution.py:437
  147.2 0.8 collective-permute-done.41.s1
  148.0 1.3 shard_map.110
  (63 shorter events, 15.5 us)
Async XLA Ops:
  0.7 1.0 copy-start.2
  1.8 0.7 copy-start.3
  2.5 0.7 copy-start.5
  3.2 0.7 copy-start.6
  5.9 10.4 %collective-permute-start = (f32[264,128]{1,0:T(8,128)S(1)}, f32[264,128]{1,0:T(8,128)S(1)}, u32[]{:S(2)}, u32[]{:S(2)}) collective-permute-start(f32[264,128]{1,0:T(8,128)S(1)} %get-tuple-element.45), channel_id=1, source_target_pairs={{0,1},{1,2},{2,3},{3,0},{4,5},{5,6},{6,7},{7,4},{8,9},{9,10},{10,1... | collective-permute-start | bytes 405512 | tf_op jit(solution)/shard_map/ppermute | solution.py:437
  8.4 9.9 %collective-permute-start.1 = (f32[264,128]{1,0:T(8,128)S(1)}, f32[264,128]{1,0:T(8,128)S(1)}, u32[]{:S(2)}, u32[]{:S(2)}) collective-permute-start(f32[264,128]{1,0:T(8,128)S(1)} %get-tuple-element.46), channel_id=1, source_target_pairs={{0,2},{1,3},{2,0},{3,1},{4,6},{5,7},{6,4},{7,5},{8,10},{9,11},{10,... | collective-permute-start | bytes 405512 | tf_op jit(solution)/shard_map/ppermute | solution.py:437
  11.7 6.6 %collective-permute-start.2 = (f32[264,128]{1,0:T(8,128)S(1)}, f32[264,128]{1,0:T(8,128)S(1)}, u32[]{:S(2)}, u32[]{:S(2)}) collective-permute-start(f32[264,128]{1,0:T(8,128)S(1)} %get-tuple-element.47), channel_id=1, source_target_pairs={{0,3},{1,0},{2,1},{3,2},{4,7},{5,4},{6,5},{7,6},{8,11},{9,8},{10,9... | collective-permute-start | bytes 405512 | tf_op jit(solution)/shard_map/ppermute | solution.py:437
  12.5 1.2 copy-start
  15.0 7.5 %collective-permute-start.3 = (f32[128,256]{1,0:T(8,128)S(1)}, f32[128,256]{1,0:T(8,128)S(1)}, u32[]{:S(2)}, u32[]{:S(2)}) collective-permute-start(f32[128,256]{1,0:T(8,128)S(1)} %get-tuple-element.49), channel_id=1, source_target_pairs={{0,1},{1,2},{2,3},{3,0},{4,5},{5,6},{6,7},{7,4},{8,9},{9,10},{10,1... | collective-permute-start | bytes 393224 | tf_op jit(solution)/shard_map/ppermute | solution.py:437
  15.8 7.4 %collective-permute-start.4 = (f32[128,256]{1,0:T(8,128)S(1)}, f32[128,256]{1,0:T(8,128)S(1)}, u32[]{:S(2)}, u32[]{:S(2)}) collective-permute-start(f32[128,256]{1,0:T(8,128)S(1)} %get-tuple-element.50), channel_id=1, source_target_pairs={{0,2},{1,3},{2,0},{3,1},{4,6},{5,7},{6,4},{7,5},{8,10},{9,11},{10,... | collective-permute-start | bytes 393224 | tf_op jit(solution)/shard_map/ppermute | solution.py:437
  16.3 7.0 %collective-permute-start.5 = (f32[128,256]{1,0:T(8,128)S(1)}, f32[128,256]{1,0:T(8,128)S(1)}, u32[]{:S(2)}, u32[]{:S(2)}) collective-permute-start(f32[128,256]{1,0:T(8,128)S(1)} %get-tuple-element.51), channel_id=1, source_target_pairs={{0,3},{1,0},{2,1},{3,2},{4,7},{5,4},{6,5},{7,6},{8,11},{9,8},{10,9... | collective-permute-start | bytes 393224 | tf_op jit(solution)/shard_map/ppermute | solution.py:437
  26.1 7.4 %collective-permute-start.8 = (f32[280,128]{1,0:T(8,128)S(1)}, f32[280,128]{1,0:T(8,128)S(1)}, u32[]{:S(2)}, u32[]{:S(2)}) collective-permute-start(f32[280,128]{1,0:T(8,128)S(1)} %get-tuple-element.52.e0), channel_id=1, source_target_pairs={{0,3},{1,0},{2,1},{3,2},{4,7},{5,4},{6,5},{7,6},{8,11},{9,8},{10,9... | collective-permute-start | bytes 430088 | tf_op jit(solution)/shard_map/ppermute | solution.py:437
  29.6 5.6 %collective-permute-start.7 = (f32[280,128]{1,0:T(8,128)S(1)}, f32[280,128]{1,0:T(8,128)S(1)}, u32[]{:S(2)}, u32[]{:S(2)}) collective-permute-start(f32[280,128]{1,0:T(8,128)S(1)} %get-tuple-element.52.e0), channel_id=1, source_target_pairs={{0,2},{1,3},{2,0},{3,1},{4,6},{5,7},{6,4},{7,5},{8,10},{9,11},{10,... | collective-permute-start | bytes 430088 | tf_op jit(solution)/shard_map/ppermute | solution.py:437
  29.6 9.3 %collective-permute-start.6 = (f32[280,128]{1,0:T(8,128)S(1)}, f32[280,128]{1,0:T(8,128)S(1)}, u32[]{:S(2)}, u32[]{:S(2)}) collective-permute-start(f32[280,128]{1,0:T(8,128)S(1)} %get-tuple-element.52.e0), channel_id=1, source_target_pairs={{0,1},{1,2},{2,3},{3,0},{4,5},{5,6},{6,7},{7,4},{8,9},{9,10},{10,1... | collective-permute-start | bytes 430088 | tf_op jit(solution)/shard_map/ppermute | solution.py:437
  44.1 2.4 %collective-permute-start.9 = (f32[264,256]{1,0:T(8,128)S(1)}, f32[264,256]{1,0:T(8,128)S(1)}, u32[]{:S(2)}, u32[]{:S(2)}) collective-permute-start(f32[264,256]{1,0:T(8,128)S(1)} %get-tuple-element.55.mine), channel_id=1, source_target_pairs={{0,4},{4,0},{1,5},{5,1},{2,6},{6,2},{3,7},{7,3},{8,12},{12,8},{9,1... | collective-permute-start | bytes 811016 | tf_op jit(solution)/shard_map/ppermute | solution.py:446
  47.4 5.9 %collective-permute-start.12 = (f32[136,256]{1,0:T(8,128)S(1)}, f32[136,256]{1,0:T(8,128)S(1)}, u32[]{:S(2)}, u32[]{:S(2)}) collective-permute-start(f32[136,256]{1,0:T(8,128)S(1)} %get-tuple-element.57), channel_id=1, source_target_pairs={{0,24},{8,0},{16,8},{24,16},{1,25},{9,1},{17,9},{25,17},{2,26},{10... | collective-permute-start | bytes 417800 | tf_op jit(solution)/shard_map/ppermute | solution.py:437
  50.0 6.9 %collective-permute-start.11 = (f32[136,256]{1,0:T(8,128)S(1)}, f32[136,256]{1,0:T(8,128)S(1)}, u32[]{:S(2)}, u32[]{:S(2)}) collective-permute-start(f32[136,256]{1,0:T(8,128)S(1)} %get-tuple-element.57), channel_id=1, source_target_pairs={{0,16},{8,24},{16,0},{24,8},{1,17},{9,25},{17,1},{25,9},{2,18},{10... | collective-permute-start | bytes 417800 | tf_op jit(solution)/shard_map/ppermute | solution.py:437
  50.5 9.5 %collective-permute-start.10 = (f32[136,256]{1,0:T(8,128)S(1)}, f32[136,256]{1,0:T(8,128)S(1)}, u32[]{:S(2)}, u32[]{:S(2)}) collective-permute-start(f32[136,256]{1,0:T(8,128)S(1)} %get-tuple-element.57), channel_id=1, source_target_pairs={{0,8},{8,16},{16,24},{24,0},{1,9},{9,17},{17,25},{25,1},{2,10},{10... | collective-permute-start | bytes 417800 | tf_op jit(solution)/shard_map/ppermute | solution.py:437
  53.3 7.2 %collective-permute-start.15 = (f32[136,256]{1,0:T(8,128)S(1)}, f32[136,256]{1,0:T(8,128)S(1)}, u32[]{:S(2)}, u32[]{:S(2)}) collective-permute-start(f32[136,256]{1,0:T(8,128)S(1)} %collective-permute-done.12.m3), channel_id=1, source_target_pairs={{0,4},{4,0},{1,5},{5,1},{2,6},{6,2},{3,7},{7,3},{8,12},{12,8},{9,1... | collective-permute-start | bytes 417800 | tf_op jit(solution)/shard_map/ppermute | solution.py:446
  56.9 3.7 %collective-permute-start.14 = (f32[136,256]{1,0:T(8,128)S(1)}, f32[136,256]{1,0:T(8,128)S(1)}, u32[]{:S(2)}, u32[]{:S(2)}) collective-permute-start(f32[136,256]{1,0:T(8,128)S(1)} %collective-permute-done.11.m2), channel_id=1, source_target_pairs={{0,4},{4,0},{1,5},{5,1},{2,6},{6,2},{3,7},{7,3},{8,12},{12,8},{9,1... | collective-permute-start | bytes 417800 | tf_op jit(solution)/shard_map/ppermute | solution.py:446
  60.1 1.5 collective-permute-start.13
  63.1 8.3 %collective-permute-start.18 = (f32[136,256]{1,0:T(8,128)S(1)}, f32[136,256]{1,0:T(8,128)S(1)}, u32[]{:S(2)}, u32[]{:S(2)}) collective-permute-start(f32[136,256]{1,0:T(8,128)S(1)} %get-tuple-element.59), channel_id=1, source_target_pairs={{0,96},{32,0},{64,32},{96,64},{1,97},{33,1},{65,33},{97,65},{2,98}... | collective-permute-start | bytes 417800 | tf_op jit(solution)/shard_map/ppermute | solution.py:437
  65.9 6.9 %collective-permute-start.17 = (f32[136,256]{1,0:T(8,128)S(1)}, f32[136,256]{1,0:T(8,128)S(1)}, u32[]{:S(2)}, u32[]{:S(2)}) collective-permute-start(f32[136,256]{1,0:T(8,128)S(1)} %get-tuple-element.59), channel_id=1, source_target_pairs={{0,64},{32,96},{64,0},{96,32},{1,65},{33,97},{65,1},{97,33},{2,66}... | collective-permute-start | bytes 417800 | tf_op jit(solution)/shard_map/ppermute | solution.py:437
  66.2 9.7 %collective-permute-start.16 = (f32[136,256]{1,0:T(8,128)S(1)}, f32[136,256]{1,0:T(8,128)S(1)}, u32[]{:S(2)}, u32[]{:S(2)}) collective-permute-start(f32[136,256]{1,0:T(8,128)S(1)} %get-tuple-element.59), channel_id=1, source_target_pairs={{0,32},{32,64},{64,96},{96,0},{1,33},{33,65},{65,97},{97,1},{2,34}... | collective-permute-start | bytes 417800 | tf_op jit(solution)/shard_map/ppermute | solution.py:437
  66.9 9.8 %collective-permute-start.24 = (f32[128,256]{1,0:T(8,128)S(1)}, f32[128,256]{1,0:T(8,128)S(1)}, u32[]{:S(2)}, u32[]{:S(2)}) collective-permute-start(f32[128,256]{1,0:T(8,128)S(1)} %get-tuple-element.61.p0), channel_id=1, source_target_pairs={{0,3},{1,0},{2,1},{3,2},{4,7},{5,4},{6,5},{7,6},{8,11},{9,8},{10,9... | collective-permute-start | bytes 393224 | tf_op jit(solution)/shard_map/ppermute | solution.py:437
  71.4 14.8 %collective-permute-start.21 = (f32[136,256]{1,0:T(8,128)S(1)}, f32[136,256]{1,0:T(8,128)S(1)}, u32[]{:S(2)}, u32[]{:S(2)}) collective-permute-start(f32[136,256]{1,0:T(8,128)S(1)} %collective-permute-done.18.m3), channel_id=1, source_target_pairs={{0,4},{4,0},{1,5},{5,1},{2,6},{6,2},{3,7},{7,3},{8,12},{12,8},{9,1... | collective-permute-start | bytes 417800 | tf_op jit(solution)/shard_map/ppermute | solution.py:446
  72.7 13.5 %collective-permute-start.20 = (f32[136,256]{1,0:T(8,128)S(1)}, f32[136,256]{1,0:T(8,128)S(1)}, u32[]{:S(2)}, u32[]{:S(2)}) collective-permute-start(f32[136,256]{1,0:T(8,128)S(1)} %collective-permute-done.17.m2), channel_id=1, source_target_pairs={{0,4},{4,0},{1,5},{5,1},{2,6},{6,2},{3,7},{7,3},{8,12},{12,8},{9,1... | collective-permute-start | bytes 417800 | tf_op jit(solution)/shard_map/ppermute | solution.py:446
  75.9 10.3 %collective-permute-start.19 = (f32[136,256]{1,0:T(8,128)S(1)}, f32[136,256]{1,0:T(8,128)S(1)}, u32[]{:S(2)}, u32[]{:S(2)}) collective-permute-start(f32[136,256]{1,0:T(8,128)S(1)} %collective-permute-done.16.m1), channel_id=1, source_target_pairs={{0,4},{4,0},{1,5},{5,1},{2,6},{6,2},{3,7},{7,3},{8,12},{12,8},{9,1... | collective-permute-start | bytes 417800 | tf_op jit(solution)/shard_map/ppermute | solution.py:446
  76.4 6.6 %collective-permute-start.23 = (f32[128,256]{1,0:T(8,128)S(1)}, f32[128,256]{1,0:T(8,128)S(1)}, u32[]{:S(2)}, u32[]{:S(2)}) collective-permute-start(f32[128,256]{1,0:T(8,128)S(1)} %get-tuple-element.61.p0), channel_id=1, source_target_pairs={{0,2},{1,3},{2,0},{3,1},{4,6},{5,7},{6,4},{7,5},{8,10},{9,11},{10,... | collective-permute-start | bytes 393224 | tf_op jit(solution)/shard_map/ppermute | solution.py:437
  76.7 9.5 %collective-permute-start.22 = (f32[128,256]{1,0:T(8,128)S(1)}, f32[128,256]{1,0:T(8,128)S(1)}, u32[]{:S(2)}, u32[]{:S(2)}) collective-permute-start(f32[128,256]{1,0:T(8,128)S(1)} %get-tuple-element.61.p0), channel_id=1, source_target_pairs={{0,1},{1,2},{2,3},{3,0},{4,5},{5,6},{6,7},{7,4},{8,9},{9,10},{10,1... | collective-permute-start | bytes 393224 | tf_op jit(solution)/shard_map/ppermute | solution.py:437
  91.7 1.3 collective-permute-start.25
  93.8 2.6 %collective-permute-start.28 = (f32[8,256]{1,0:T(8,128)S(1)}, f32[8,256]{1,0:T(8,128)S(1)}, u32[]{:S(2)}, u32[]{:S(2)}) collective-permute-start(f32[8,256]{1,0:T(8,128)S(1)} %shard_map.101.q0), channel_id=1, source_target_pairs={{0,24},{8,0},{16,8},{24,16},{1,25},{9,1},{17,9},{25,17},{2,26},{10... | collective-permute-start | bytes 24584 | tf_op jit(solution)/shard_map/ppermute | solution.py:437
  94.6 4.0 %collective-permute-start.27 = (f32[8,256]{1,0:T(8,128)S(1)}, f32[8,256]{1,0:T(8,128)S(1)}, u32[]{:S(2)}, u32[]{:S(2)}) collective-permute-start(f32[8,256]{1,0:T(8,128)S(1)} %shard_map.101.q0), channel_id=1, source_target_pairs={{0,16},{8,24},{16,0},{24,8},{1,17},{9,25},{17,1},{25,9},{2,18},{10... | collective-permute-start | bytes 24584 | tf_op jit(solution)/shard_map/ppermute | solution.py:437
  94.8 4.0 %collective-permute-start.26 = (f32[8,256]{1,0:T(8,128)S(1)}, f32[8,256]{1,0:T(8,128)S(1)}, u32[]{:S(2)}, u32[]{:S(2)}) collective-permute-start(f32[8,256]{1,0:T(8,128)S(1)} %shard_map.101.q0), channel_id=1, source_target_pairs={{0,8},{8,16},{16,24},{24,0},{1,9},{9,17},{17,25},{25,1},{2,10},{10... | collective-permute-start | bytes 24584 | tf_op jit(solution)/shard_map/ppermute | solution.py:437
  100.0 2.5 %collective-permute-start.31 = (f32[8,256]{1,0:T(8,128)S(1)}, f32[8,256]{1,0:T(8,128)S(1)}, u32[]{:S(2)}, u32[]{:S(2)}) collective-permute-start(f32[8,256]{1,0:T(8,128)S(1)} %get-tuple-element.67.gy0), channel_id=1, source_target_pairs={{0,96},{32,0},{64,32},{96,64},{1,97},{33,1},{65,33},{97,65},{2,98}... | collective-permute-start | bytes 24584 | tf_op jit(solution)/shard_map/ppermute | solution.py:437
  100.9 4.0 %collective-permute-start.30 = (f32[8,256]{1,0:T(8,128)S(1)}, f32[8,256]{1,0:T(8,128)S(1)}, u32[]{:S(2)}, u32[]{:S(2)}) collective-permute-start(f32[8,256]{1,0:T(8,128)S(1)} %get-tuple-element.67.gy0), channel_id=1, source_target_pairs={{0,64},{32,96},{64,0},{96,32},{1,65},{33,97},{65,1},{97,33},{2,66}... | collective-permute-start | bytes 24584 | tf_op jit(solution)/shard_map/ppermute | solution.py:437
  100.9 4.1 %collective-permute-start.29 = (f32[8,256]{1,0:T(8,128)S(1)}, f32[8,256]{1,0:T(8,128)S(1)}, u32[]{:S(2)}, u32[]{:S(2)}) collective-permute-start(f32[8,256]{1,0:T(8,128)S(1)} %get-tuple-element.67.gy0), channel_id=1, source_target_pairs={{0,32},{32,64},{64,96},{96,0},{1,33},{33,65},{65,97},{97,1},{2,34}... | collective-permute-start | bytes 24584 | tf_op jit(solution)/shard_map/ppermute | solution.py:437
  105.0 5.7 %copy-start.1 = (bf16[512,1024]{1,0:T(8,128)(2,1)S(1)}, bf16[512,1024]{1,0:T(8,128)(2,1)}, u32[]{:S(2)}) copy-start(bf16[512,1024]{1,0:T(8,128)(2,1)} %observed.5) | copy-start | bytes 3145732
  105.0 5.7 %copy-start.4 = (s32[4,1024]{1,0:T(4,128)S(1)}, s32[4,1024]{1,0:T(4,128)}, u32[]{:S(2)}) copy-start(s32[4,1024]{1,0:T(4,128)} %present.5) | copy-start | bytes 49156
  110.7 10.7 %copy-start.7 = (s32[8]{0:T(128)S(1)}, s32[8]{0:T(128)}, u32[]{:S(2)}) copy-start(s32[8]{0:T(128)} %panel_of.1) | copy-start | bytes 100
  112.1 4.9 %collective-permute-start.32 = (f32[16,8,1024]{2,1,0:T(8,128)S(1)}, f32[16,8,1024]{2,1,0:T(8,128)S(1)}, u32[]{:S(2)}, u32[]{:S(2)}) collective-permute-start(f32[16,8,1024]{2,1,0:T(8,128)S(1)} %get-tuple-element.77), channel_id=1, source_target_pairs={{0,4},{4,0},{1,5},{5,1},{2,6},{6,2},{3,7},{7,3},{8,12},{12,8},{9,1... | collective-permute-start | bytes 1572872 | tf_op jit(solution)/shard_map/ppermute | solution.py:446
  115.4 8.7 %collective-permute-start.33 = (f32[64,256]{1,0:T(8,128)S(1)}, f32[64,256]{1,0:T(8,128)S(1)}, u32[]{:S(2)}, u32[]{:S(2)}) collective-permute-start(f32[64,256]{1,0:T(8,128)S(1)} %get-tuple-element.78.q), channel_id=1, source_target_pairs={{0,4},{4,0},{1,5},{5,1},{2,6},{6,2},{3,7},{7,3},{8,12},{12,8},{9,1... | collective-permute-start | bytes 196616 | tf_op jit(solution)/shard_map/ppermute | solution.py:446
  117.8 32.0 %all-to-all-start = ((f32[16,8,1024]{2,1,0:T(8,128)}), f32[16,8,1024]{2,1,0:T(8,128)S(1)}, u32[]{:S(2)}, u32[]{:S(2)}) async-start(f32[16,8,1024]{2,1,0:T(8,128)} %shard_map.105), calls=%async_computation | async-start | bytes 1048576 | tf_op jit(solution)/shard_map/all_to_all | solution.py:529
  122.8 1.3 collective-permute-start.34
  124.1 6.2 %collective-permute-start.37 = (f32[72,256]{1,0:T(8,128)S(1)}, f32[72,256]{1,0:T(8,128)S(1)}, u32[]{:S(2)}, u32[]{:S(2)}) collective-permute-start(f32[72,256]{1,0:T(8,128)S(1)} %shard_map.107.a), channel_id=1, source_target_pairs={{0,24},{8,0},{16,8},{24,16},{1,25},{9,1},{17,9},{25,17},{2,26},{10... | collective-permute-start | bytes 221192 | tf_op jit(solution)/shard_map/ppermute | solution.py:437
  127.3 4.7 %collective-permute-start.36 = (f32[72,256]{1,0:T(8,128)S(1)}, f32[72,256]{1,0:T(8,128)S(1)}, u32[]{:S(2)}, u32[]{:S(2)}) collective-permute-start(f32[72,256]{1,0:T(8,128)S(1)} %shard_map.107.a), channel_id=1, source_target_pairs={{0,16},{8,24},{16,0},{24,8},{1,17},{9,25},{17,1},{25,9},{2,18},{10... | collective-permute-start | bytes 221192 | tf_op jit(solution)/shard_map/ppermute | solution.py:437
  127.9 6.2 %collective-permute-start.35 = (f32[72,256]{1,0:T(8,128)S(1)}, f32[72,256]{1,0:T(8,128)S(1)}, u32[]{:S(2)}, u32[]{:S(2)}) collective-permute-start(f32[72,256]{1,0:T(8,128)S(1)} %shard_map.107.a), channel_id=1, source_target_pairs={{0,8},{8,16},{16,24},{24,0},{1,9},{9,17},{17,25},{25,1},{2,10},{10... | collective-permute-start | bytes 221192 | tf_op jit(solution)/shard_map/ppermute | solution.py:437
  134.1 3.9 %collective-permute-start.40 = (f32[72,256]{1,0:T(8,128)S(1)}, f32[72,256]{1,0:T(8,128)S(1)}, u32[]{:S(2)}, u32[]{:S(2)}) collective-permute-start(f32[72,256]{1,0:T(8,128)S(1)} %shard_map.108.a), channel_id=1, source_target_pairs={{0,96},{32,0},{64,32},{96,64},{1,97},{33,1},{65,33},{97,65},{2,98}... | collective-permute-start | bytes 221192 | tf_op jit(solution)/shard_map/ppermute | solution.py:437
  136.6 4.8 %collective-permute-start.39 = (f32[72,256]{1,0:T(8,128)S(1)}, f32[72,256]{1,0:T(8,128)S(1)}, u32[]{:S(2)}, u32[]{:S(2)}) collective-permute-start(f32[72,256]{1,0:T(8,128)S(1)} %shard_map.108.a), channel_id=1, source_target_pairs={{0,64},{32,96},{64,0},{96,32},{1,65},{33,97},{65,1},{97,33},{2,66}... | collective-permute-start | bytes 221192 | tf_op jit(solution)/shard_map/ppermute | solution.py:437
  137.1 4.9 %collective-permute-start.38 = (f32[72,256]{1,0:T(8,128)S(1)}, f32[72,256]{1,0:T(8,128)S(1)}, u32[]{:S(2)}, u32[]{:S(2)}) collective-permute-start(f32[72,256]{1,0:T(8,128)S(1)} %shard_map.108.a), channel_id=1, source_target_pairs={{0,32},{32,64},{64,96},{96,0},{1,33},{33,65},{65,97},{97,1},{2,34}... | collective-permute-start | bytes 221192 | tf_op jit(solution)/shard_map/ppermute | solution.py:437
  142.1 3.3 %collective-permute-start.43 = (f32[72,256]{1,0:T(8,128)S(1)}, f32[72,256]{1,0:T(8,128)S(1)}, u32[]{:S(2)}, u32[]{:S(2)}) collective-permute-start(f32[72,256]{1,0:T(8,128)S(1)} %shard_map.109.s0), channel_id=1, source_target_pairs={{0,3},{1,0},{2,1},{3,2},{4,7},{5,4},{6,5},{7,6},{8,11},{9,8},{10,9... | collective-permute-start | bytes 221192 | tf_op jit(solution)/shard_map/ppermute | solution.py:437
  142.5 4.7 %collective-permute-start.42 = (f32[72,256]{1,0:T(8,128)S(1)}, f32[72,256]{1,0:T(8,128)S(1)}, u32[]{:S(2)}, u32[]{:S(2)}) collective-permute-start(f32[72,256]{1,0:T(8,128)S(1)} %shard_map.109.s0), channel_id=1, source_target_pairs={{0,2},{1,3},{2,0},{3,1},{4,6},{5,7},{6,4},{7,5},{8,10},{9,11},{10,... | collective-permute-start | bytes 221192 | tf_op jit(solution)/shard_map/ppermute | solution.py:437
  142.7 5.2 %collective-permute-start.41 = (f32[72,256]{1,0:T(8,128)S(1)}, f32[72,256]{1,0:T(8,128)S(1)}, u32[]{:S(2)}, u32[]{:S(2)}) collective-permute-start(f32[72,256]{1,0:T(8,128)S(1)} %shard_map.109.s0), channel_id=1, source_target_pairs={{0,1},{1,2},{2,3},{3,0},{4,5},{5,6},{6,7},{7,4},{8,9},{9,10},{10,1... | collective-permute-start | bytes 221192 | tf_op jit(solution)/shard_map/ppermute | solution.py:437
where the time goes:
time: 153 us; the launch traced here: 150 us
  starting transfers between devices  54.9 us (36%)
  waiting for transfers between devices  53 us (35%)
  Pallas kernels  36.2 us (24%)
  local copies, waits for them, and re-layouts  4.87 us (3%)
    ppermute x33, waiting for transfers between devices, from_peers(): lax.ppermute(arrays[k], axis, [(i, (i + k) % n) for i in range(n)])  47.7 us
    pallas_call x18, Pallas kernels, call(): return made(*args)  36.2 us
    ppermute x33, starting transfers between devices, from_peers(): lax.ppermute(arrays[k], axis, [(i, (i + k) % n) for i in range(n)])  36.1 us
    ppermute x11, starting transfers between devices, swap(): return lax.ppermute(array, axis, [(0, 1), (1, 0)])  15.2 us
    ppermute x11, waiting for transfers between devices, swap(): return lax.ppermute(array, axis, [(0, 1), (1, 0)])  5.28 us
    unnamed x16, local copies, waits for them, and re-layouts  4.36 us
    all_to_all x1, starting transfers between devices, step(): arrived = lax.all_to_all(own_part, (ay, ax), 0, 0, tiled=True)  3.57 us
  transfers between devices with their start and end apart: 45, of which 30 were waited for; matrix products, arithmetic and copies ran while one was open for 0% of the time, Pallas kernels for 6%

commit v1 on v0

--- a/solution.py
+++ b/solution.py
@@ -71,41 +71,37 @@
     )
 
 
-def gram_kernel(place, present_in, noise_in, loads_in, decay_in, turned, decay, o0, o1, o2, o3,
-                present, noise, loads, sems):
-    copies = [
-        pltpu.make_async_copy(present_in, present, sems.at[0]),
-        pltpu.make_async_copy(noise_in, noise, sems.at[1]),
-        pltpu.make_async_copy(loads_in, loads, sems.at[2]),
-        pltpu.make_async_copy(decay_in, decay, sems.at[3]),
-    ]
-    for c in copies:
-        c.start()
-    for c in copies:
-        c.wait()
+def gram_kernel(place, present, noise, loads, *outs):
     coef = loads[...]
     flipped = coef.astype(F32).T
-    turned[...] = flipped.astype(BF16)
     inv_noise = 1.0 / noise[...]
-    for k, out in enumerate((o0, o1, o2, o3)):
-        b = lax.rem(place[3] + k, 4)
-        weight = present[pl.ds(b, 1), :].astype(F32) * inv_noise
-        hi, lo = split(flipped * weight)
+    for k, out in enumerate(outs):
+        b = lax.rem(place[3] + k, len(outs))
+        hi, lo = split(flipped * (present[pl.ds(b, 1), :].astype(F32) * inv_noise))
         store_packed(out, dot(hi, coef) + dot(lo, coef))
 
 
-def project_kernel(place, present, noise, loads, observed, *outs):
+def project_kernel(place, present, noise, loads, decay, observed, table, *outs):
     coef = loads[...]
     inv_noise = 1.0 / noise[...]
+    table[0:4, :] = present[...].astype(F32)
+    table[4:5, 0 : decay.shape[1]] = decay[...]
     for k in range(len(outs)):
         b = lax.rem(place[3] + k, len(outs))
-        weight = present[pl.ds(b, 1), :].astype(F32) * inv_noise
         rows = observed[pl.ds(pl.multiple_of(b * BLOCK, BLOCK), BLOCK), :].astype(F32)
-        hi, lo = split(rows * weight)
+        hi, lo = split(rows * (present[pl.ds(b, 1), :].astype(F32) * inv_noise))
         outs[k][...] = dot(hi, coef) + dot(lo, coef)
 
 
-def inverse_kernel(decay, g0, g1, g2, g3, out, guess):
+def turn_kernel(loads, out):
+    out[...] = loads[...].astype(F32).T.astype(BF16)
+
+
+def decay_of(table, n):
+    return table[4:5, 0:n]
+
+
+def inverse_kernel(table, g0, g1, g2, g3, out, guess):
     gram = unpack((g0[...] + g1[...]) + (g2[...] + g3[...]))
     n = gram.shape[0]
     ident = eye(n)
@@ -125,11 +121,18 @@
         guess[...] = improve(guess[...])
         return err * err
 
-    lax.while_loop(lambda err: err > 1e-4, body, start * start)
+    def quick(err):
+        x = guess[...]
+        pair = split(x)
+        guess[...] = 2.0 * x - dot3(pair, split(dot3(split(whole), pair)))
+        return err * err
+
+    err = lax.while_loop(lambda e: (e > 1e-4) & (top < 8.0), quick, start * start)
+    lax.while_loop(lambda e: e > 1e-4, body, err)
     inverse = improve(guess[...])
     gain = jnp.dot(gram, inverse, precision=HIGH, preferred_element_type=F32)
     gain = 0.5 * (gain + gain.T)
-    rho = 1.0 - decay[...]
+    rho = 1.0 - decay_of(table, n)
     root = jnp.sqrt(rho)
     root_down = jnp.sum(ident * root, axis=1, keepdims=True)
     store_packed(out, ident * (1.0 - rho) + gain * root * root_down)
@@ -143,52 +146,51 @@
     return jnp.where(at < n - offset, pltpu.roll(rows, n - offset, 0), 0.0)
 
 
-def end_kernel(decay, packed, p0, p1, p2, p3, total, out, err_ref):
-    n = decay.shape[1]
-    half = n // 2
+def end_kernel(table, packed, p0, p1, p2, p3, total, out, err_ref):
     proj = (p0[...] + p1[...]) + (p2[...] + p3[...])
     total[...] = proj
-    out[0 : n + 8, :] = packed[...]
-    err = unpack(packed[...])
-    z = proj * lax.rsqrt(1.0 - decay[...])
-    v = z - dot3(split(z), split(err))
-    err_ref[...] = err
-    rows = BLOCK
+    z = proj * lax.rsqrt(1.0 - decay_of(table, proj.shape[1]))
+    err_ref[...] = unpack(packed[...])
+    v = z - dot3(split(z), split(err_ref[...]))
     for level in range(LEVELS):
         pair = split(err_ref[...])
         v = v + shifted(v - dot3(split(v), pair), 1 << level, True)
         if level + 1 < LEVELS:
             err_ref[...] = 2.0 * err_ref[...] - dot3(pair, pair)
-    out[n + 8 : n + 16, :] = jnp.broadcast_to(v[rows - 1 :, :half], (8, half))
-    out[n + 16 :, :] = jnp.broadcast_to(v[rows - 1 :, half:], (8, half))
-
-
-def powers_kernel(place, e0, e1, e2, e3, his, los, tops, ends, whole, errs):
+    out[...] = jnp.broadcast_to(v[BLOCK - 1 :], out.shape)
+
+
+def powers_kernel(place, e0, e1, e2, e3, his, los, tops, whole, errs):
     nb = 4
-    n = 2 * e0.shape[1]
-    half = n // 2
     for k, e in enumerate((e0, e1, e2, e3)):
-        b = lax.rem(place[3] + nb - k, nb)
-        errs[b] = unpack(e[0 : n + 8, :])
-        ends[b, :, 0:half] = e[n + 8 : n + 16, :]
-        ends[b, :, half:] = e[n + 16 :, :]
-    for level in range(LEVELS):
+        errs[lax.rem(place[3] + nb - k, nb)] = unpack(e[...])
+
+    def square(level, carry):
         for b in range(nb):
             err = errs[b]
             pair = split(err)
             his[level * nb + b] = pair[0]
             los[level * nb + b] = pair[1]
             errs[b] = 2.0 * err - dot3(pair, pair)
-    total, end = errs[0], ends[0]
+        return carry
+
+    lax.fori_loop(0, LEVELS, square, 0)
+    total = errs[0]
     tops[0] = total
     for b in range(1, nb):
         err = errs[b]
         tops[b] = err
-        pair = split(err)
-        end = end - dot3(split(end), pair) + ends[b]
-        total = total + err - dot3(split(total), pair)
-    whole[0:n, :] = total
-    whole[n:, :] = end
+        total = total + err - dot3(split(total), split(err))
+    whole[...] = total
+
+
+def segment_end_kernel(place, tops, v0, v1, v2, v3, ends, out):
+    nb = 4
+    ordered(place[3], (v0, v1, v2, v3), ends)
+    end = ends[0]
+    for b in range(1, nb):
+        end = end - dot3(split(end), split(tops[b])) + ends[b]
+    out[...] = end
 
 
 def join(maps):
@@ -211,10 +213,15 @@
     half[h:, :] = end
 
 
-def pair_kernel(place, mine, other, out, half):
-    own, far = mine[...], other[...]
+def pair_kernel(place, mine, other, v_mine, v_other, out, half):
+    own, far, v_own, v_far = mine[...], other[...], v_mine[...], v_other[...]
     first = place[2] == 0
-    total, end = join([jnp.where(first, own, far), jnp.where(first, far, own)])
+    total = jnp.where(first, own, far)
+    err = jnp.where(first, far, own)
+    pair = split(err)
+    end = jnp.where(first, v_own, v_far)
+    end = end - dot3(split(end), pair) + jnp.where(first, v_far, v_own)
+    total = total + err - dot3(split(total), pair)
     store_map(total, end, place[2], out, half)
 
 
@@ -257,20 +264,21 @@
             values[b] = v + shifted(v - dot3(split(v), pair), 1 << level, ahead)
 
 
-def forward_kernel(place, decay, own, m1, m2, m3, o1, o2, o3, xs, other, p0, p1, p2, p3,
+def forward_kernel(place, table, own, m1, m2, m3, o1, o2, o3, xs, other, v_other, p0, p1, p2, p3,
                    ends, his, los, tops,
                    past, change, firsts, first, ys, values, states):
     nb = 4
-    root_inv = lax.rsqrt(1.0 - decay[...])
+    n = own.shape[1]
+    rho = 1.0 - decay_of(table, n)
+    root_inv = lax.rsqrt(rho)
     ordered(place[3], (p0, p1, p2, p3), values)
     ordered_maps(place[0], place[2], own, ((m1, o1), (m2, o2), (m3, o3)), ys)
-    n = decay.shape[1]
     state = jnp.zeros((8, n), F32)
     state = lax.fori_loop(0, place[0], lambda k, s: advance(s, ys[k]), state)
     state = lax.fori_loop(0, place[1], lambda k, s: advance(s, xs[k]), state)
-    state = jnp.where(place[2] == 0, state, advance(state, other[...]))
+    over = state - dot3(split(state), split(other[...])) + v_other[...]
+    state = jnp.where(place[2] == 0, state, over)
     at = lax.broadcasted_iota(jnp.int32, (BLOCK, n), 0)
-    rho = 1.0 - decay[...]
     for b in range(nb):
         states[b] = state
         if b + 1 < nb:
@@ -296,11 +304,10 @@
 
 
 def pair_back_kernel(place, own, far, mine, other, out):
-    n = mine.shape[1]
     lead = place[2] == 0
     early_q = jnp.where(lead, own[...], far[...])
     late_q = jnp.where(lead, far[...], own[...])
-    early = jnp.where(lead, mine[0:n, :], other[0:n, :])
+    early = jnp.where(lead, mine[...], other[...])
     out[...] = early_q + retreat(late_q, early)
 
 
@@ -313,13 +320,13 @@
     out[...] = q
 
 
-def smooth_kernel(place, decay, gy0, gy1, gy2, gy3, gxs, far, ys, xs, other,
+def smooth_kernel(place, table, gy0, gy1, gy2, gy3, gxs, far, ys, xs, other,
                   past, change, firsts, his, los, tops,
-                  smoothed, high, low, quarter, gys, values, states, moment):
+                  smoothed, high, low, keep, give, gys, values, states, moment):
     nb = 4
     nseg = 4
     ordered(place[0], (gy0, gy1, gy2, gy3), gys)
-    n = decay.shape[1]
+    n = gy0.shape[1]
     back = jnp.zeros((8, n), F32)
 
     def over(gs, ms):
@@ -331,7 +338,7 @@
 
     back = lax.fori_loop(0, nseg - 1 - place[0], over(gys, ys), back)
     back = lax.fori_loop(0, nseg - 1 - place[1], over(gxs, xs), back)
-    back = jnp.where(place[2] == 0, far[...] + retreat(back, other[0:n, :]), back)
+    back = jnp.where(place[2] == 0, far[...] + retreat(back, other[...]), back)
     at = lax.broadcasted_iota(jnp.int32, (BLOCK, n), 0)
     for b in reversed(range(nb)):
         states[b] = back
@@ -342,20 +349,23 @@
         step = s - dot3(split(s), (his[b], los[b]))
         values[b] = change[b] + jnp.where(at == BLOCK - 1, step[0:1], 0.0)
     scan_rows(values, his, los, nb, False)
-    root_inv = lax.rsqrt(1.0 - decay[...])
+    root_inv = lax.rsqrt(1.0 - decay_of(table, n))
     for b in range(nb):
         smoothed[b * BLOCK : (b + 1) * BLOCK, :] = (values[b] + past[b]) * root_inv
     pair = split(smoothed[...])
     high[...], low[...] = pair
-    moment[...] = dot3(pair, pair, ((0,), (0,))) * (1.0 / (128 * BLOCK))
-    quarter[...] = moment[pl.ds(pl.multiple_of(place[3] * 64, 64), 64), :]
-
-
-def errors_kernel(panel_of, high, low, observed, present, turned, sums_out):
+    store_packed(moment, dot3(pair, pair, ((0,), (0,))) * (1.0 / (128 * BLOCK)))
+    rows = keep.shape[0]
+    keep[...] = moment[pl.ds(pl.multiple_of(place[2] * BLOCK, BLOCK), rows), :]
+    give[...] = moment[pl.ds(pl.multiple_of((1 - place[2]) * BLOCK, BLOCK), rows), :]
+
+
+def errors_kernel(panel_of, table, high, low, observed, turned, sums_out):
     nb = 4
-    n, series = turned.shape
+    n = sums_out.shape[1]
+    series = turned.shape[1]
     coef = turned[...]
-    weight = present[...].astype(F32)
+    weight = table[0:4, :]
     squares = jnp.zeros((1, series), F32)
     for b in range(nb):
         part = slice(b * BLOCK, (b + 1) * BLOCK)
@@ -374,9 +384,9 @@
     sums_out[...] = sums
 
 
-def moment_kernel(place, high, low, observed, present, own_part, far_part, moment):
+def moment_kernel(place, table, high, low, observed, own_part, far_part, moment):
     nb = 4
-    weight = present[...].astype(F32)
+    weight = table[0:4, :]
     kept = jnp.concatenate(
         [
             (observed[b * BLOCK : (b + 1) * BLOCK, :].astype(F32) * weight[b : b + 1]).astype(BF16)
@@ -388,43 +398,60 @@
     scale = 1.0 / math.sqrt(128 * BLOCK)
     moment[...] = (dot(high[...], kept, both) + dot(low[...], kept, both)) * scale
     for i in range(16):
-        own_part[i] = moment[pl.ds(pl.multiple_of((2 * i + place[2]) * 8, 8), 8), :]
-        far_part[i] = moment[pl.ds(pl.multiple_of((2 * i + 1 - place[2]) * 8, 8), 8), :]
+        own = moment[pl.ds(pl.multiple_of((2 * i + place[2]) * 8, 8), 8), :]
+        far = moment[pl.ds(pl.multiple_of((2 * i + 1 - place[2]) * 8, 8), 8), :]
+        for j in range(8):
+            own_part[i, 8 * j : 8 * j + 8, :] = own[:, j * 128 : (j + 1) * 128]
+            far_part[i, 8 * j : 8 * j + 8, :] = far[:, j * 128 : (j + 1) * 128]
 
 
 def add_kernel(a, b, out):
     out[...] = a[...] + b[...]
 
 
-def small_kernel(q, q_far, s, s_far, out):
-    out[0:64, :] = q[...] + q_far[...]
-    out[64:72, :] = s[...] + s_far[...]
+def small_kernel(keep, given, s, s_far, out):
+    n = keep.shape[0]
+    out[0:n, :] = keep[...] + given[...]
+    out[n:, :] = s[...] + s_far[...]
+
+
+def collect_kernel(arrived, out):
+    total = jnp.sum(arrived[...], axis=0)
+    for j in range(8):
+        out[:, j * 128 : (j + 1) * 128] = total[8 * j : 8 * j + 8]
+
+
+def variance_kernel(s0, s1, s2, s3, out):
+    sums = (s0[...] + s1[...]) + (s2[...] + s3[...])
+    out[...] = sums[0:1] / jnp.maximum(sums[1:2], 1.0)
+
+
+def last_sum_kernel(a, b, c, d, state, sums):
+    n = state.shape[0]
+    total = (a[...] + b[...]) + (c[...] + d[...])
+    state[...] = total[:n]
+    sums[...] = total[n:]
 
 
 def sum_kernel(a, b, c, d, out):
     out[...] = (a[...] + b[...]) + (c[...] + d[...])
 
 
-def finish_kernel(place, s0, s1, s2, s3, out, var):
-    sums = jnp.zeros((8, s0.shape[1]), F32)
-    for k, s in enumerate((s0, s1, s2, s3)):
-        at = lax.rem(place[3] + 4 - k, 4)
-        out[pl.ds(pl.multiple_of(at * 64, 64), 64), :] = s[0:64, :]
-        sums = sums + s[64:72, :]
-    var[...] = jnp.broadcast_to(sums[0:1] / jnp.maximum(sums[1:2], 1.0), var.shape)
-
-
-def call(kernel, outs, scratch, *args, smem=1, far=0, sems=0, mib=12):
+def finish_kernel(place, mine, other, out):
+    first = jnp.where(place[2] == 0, mine[...], other[...])
+    second = jnp.where(place[2] == 0, other[...], mine[...])
+    out[...] = unpack(jnp.concatenate([first[0:BLOCK], second], axis=0))
+
+
+def call(kernel, outs, scratch, *args, smem=1, mib=12):
     shapes = [jax.ShapeDtypeStruct(s, d) for s, d in outs]
-    specs = [SMEM] * smem + [pl.BlockSpec(memory_space=pltpu.HBM)] * far
-    specs += [VMEM] * (len(args) - smem - far)
+    specs = [SMEM] * smem + [VMEM] * (len(args) - smem)
     made = pl.pallas_call(
         kernel,
         out_shape=shapes,
         in_specs=specs,
         out_specs=[VMEM] * len(outs),
-        scratch_shapes=[pltpu.VMEM(s, d) for s, d in scratch]
-        + ([pltpu.SemaphoreType.DMA((sems,))] if sems else []),
+        scratch_shapes=[pltpu.VMEM(s, d) for s, d in scratch],
         compiler_params=pltpu.CompilerParams(vmem_limit_bytes=mib << 20),
     )
     return made(*args)
@@ -455,9 +482,7 @@
     iy, ix, ic, iz = (lax.axis_index(a) for a in (ay, ax, ac, "panel"))
     scalar = lambda *v: jnp.stack([jnp.int32(i) for i in v])
     place = scalar(iy, ix, ic, iz)
-    noise = noise_var.reshape(1, series)
     packed = ((width + 8, half), F32)
-    packed_end = ((width + 24, half), F32)
     map_shape = ((width + 8, width), F32)
     half_shape = ((half + 8, width), F32)
     vec = ((8, width), F32)
@@ -469,27 +494,28 @@
     squares4 = ((nb, width, width), F32)
     powers = ((LEVELS * nb, width, width), BF16)
 
-    turned, decay, *grams = call(
-        gram_kernel, [((width, series), BF16), ((1, width), F32)] + [packed] * nb,
-        [(present.shape, jnp.int32), ((1, series), F32), ((series, width), BF16)],
-        place, present, noise, loadings, decay_rate.reshape(1, width), far=4, sems=4,
-    )
-    projs = call(project_kernel, [rows2] * nb, [], place, present, noise, loadings, observed)
+    noise = noise_var.reshape(1, series)
+    grams = call(gram_kernel, [packed] * nb, [], place, present, noise, loadings)
+    table, *projs = call(
+        project_kernel, [((8, series), F32)] + [rows2] * nb, [],
+        place, present, noise, loadings, decay_rate.reshape(1, width), observed,
+    )
     grams = from_peers(grams, "panel")
     projs = from_peers(projs, "panel")
-    (err,) = call(inverse_kernel, [packed], [square], decay, *grams, smem=0)
-    proj, err_end = call(end_kernel, [rows2, packed_end], [square], decay, err, *projs, smem=0)
-    errs = gather(err_end, "panel")
-    his, los, tops, ends, seg = call(
-        powers_kernel,
-        [powers, powers, squares4, vecs4, map_shape],
-        [squares4],
-        place, *errs,
+    (err,) = call(inverse_kernel, [packed], [square], table, *grams, smem=0)
+    errs = gather(err, "panel")
+    proj, end = call(end_kernel, [rows2, vec], [square], table, err, *projs, smem=0)
+    ends = gather(end, "panel")
+    his, los, tops, seg = call(
+        powers_kernel, [powers, powers, squares4, square], [squares4], place, *errs
     )
     seg, proj = lax.optimization_barrier((seg, proj))
     seg_far = swap(seg, ac)
+    ends, seg_end = call(segment_end_kernel, [vecs4, vec], [], place, tops, *ends)
+    end_far = swap(seg_end, ac)
     projs = gather(proj, "panel")
-    pair, pair_half = call(pair_kernel, [map_shape, half_shape], [], place, seg, seg_far)
+    pair, pair_half = call(pair_kernel, [map_shape, half_shape], [], place, seg, seg_far, seg_end, end_far)
+    (turned,) = call(turn_kernel, [((width, series), BF16)], [], loadings, smem=0)
     near = gather(pair_half, ax)[1:]
     group, group_half, xs = call(
         group_kernel, [map_shape, half_shape, maps4], [],
@@ -500,8 +526,8 @@
         forward_kernel,
         [rows3, rows3, vecs4, vec, maps4],
         [rows3, vecs4],
-        place, decay, group, *near, *[swap(m, ac) for m in near],
-        xs, seg_far, *projs, ends, his, los, tops,
+        place, table, group, *near, *[swap(m, ac) for m in near],
+        xs, seg_far, end_far, *projs, ends, his, los, tops,
     )
     first_far = swap(first, ac)
     (pair_first,) = call(pair_back_kernel, [vec], [], place, first, first_far, seg, seg_far)
@@ -509,27 +535,32 @@
         group_back_kernel, [vec, vecs4], [], place, *gather(pair_first, ax), xs
     )
     flat = ((time_rows, width), BF16)
-    smoothed, high, low, quarter = call(
+    piece = ((BLOCK + 8, half), F32)
+    smoothed, high, low, keep, give = call(
         smooth_kernel,
-        [((time_rows, width), F32), flat, flat, ((64, width), F32)],
-        [vecs4, rows3, vecs4, square],
-        place, decay, *gather(group_first, ay), gxs, first_far, ys, xs, seg_far,
+        [((time_rows, width), F32), flat, flat, piece, piece],
+        [vecs4, rows3, vecs4, packed],
+        place, table, *gather(group_first, ay), gxs, first_far, ys, xs, seg_far,
         past, change, firsts, his, los, tops,
     )
-    quarter_far = swap(quarter, ac)
-    (sums,) = call(errors_kernel, [vec], [], panel_of_block, high, low, observed, present, turned)
-    small_shape = ((72, width), F32)
-    (small,) = call(small_kernel, [small_shape], [], quarter, quarter_far, sums, swap(sums, ac), smem=0)
-    (small,) = call(sum_kernel, [small_shape], [], *gather(small, ax), smem=0)
-    part = ((16, 8, series), F32)
+    given = swap(give, ac)
+    line = ((8, half), F32)
+    (sums,) = call(errors_kernel, [line], [], panel_of_block, table, high, low, observed, turned)
+    tall = ((BLOCK + 16, half), F32)
+    (small,) = call(small_kernel, [tall], [], keep, given, sums, swap(sums, ac), smem=0)
+    smalls = gather(small, ax)
+    part = ((16, 64, half), F32)
     own_part, far_part = call(
-        moment_kernel, [part, part], [((width, series), F32)], place, high, low, observed, present
-    )
-    (own_part,) = call(add_kernel, [part], [], own_part, swap(far_part, ac), smem=0)
-    arrived = lax.all_to_all(own_part, (ay, ax), 0, 0, tiled=True)
-    loading_moment = arrived.sum(axis=0)
-    (small,) = call(sum_kernel, [small_shape], [], *gather(small, ay), smem=0)
-    state_moment, var = call(finish_kernel, [square, vec], [], place, *gather(small, "panel"))
+        moment_kernel, [part, part], [((width, series), F32)], place, table, high, low, observed
+    )
+    (spread,) = call(add_kernel, [part], [], own_part, swap(far_part, ac), smem=0)
+    arrived = lax.all_to_all(spread, (ay, ax), 0, 0, tiled=True)
+    (small,) = call(sum_kernel, [tall], [], *smalls, smem=0)
+    smalls = gather(small, ay)
+    state, sums = call(last_sum_kernel, [piece, line], [], *smalls, smem=0)
+    (state_moment,) = call(finish_kernel, [square], [], place, state, swap(state, ac))
+    (var,) = call(variance_kernel, [((1, half), F32)], [], *gather(sums, "panel"), smem=0)
+    (loading_moment,) = call(collect_kernel, [((8, series), F32)], [], arrived, smem=0)
     return smoothed, loading_moment, state_moment, var[0, :PANELS]
 
 

time: 153 us -> 161 us (1.052)
  starting transfers between devices: 54.9 us -> 76.8 us
  waiting for transfers between devices: 53 us -> 38.5 us
  Pallas kernels: 36.2 us -> 38.1 us
    ppermute x33 -> x36, starting transfers between devices: 36.1 us -> 53.7 us  [from_peers(): lax.ppermute(arrays[k], axis, [(i, (i + k) % n) for i in range(n)])]
    ppermute x33 -> x36, waiting for transfers between devices: 47.7 us -> 32.4 us  [from_peers(): lax.ppermute(arrays[k], axis, [(i, (i + k) % n) for i in range(n)])]
    ppermute x11 -> x13, starting transfers between devices: 15.2 us -> 18.9 us  [swap(): return lax.ppermute(array, axis, [(0, 1), (1, 0)])]
    pallas_call x18 -> x22, Pallas kernels: 36.2 us -> 38.1 us  [call(): return made(*args)]
    ppermute x11 -> x13, waiting for transfers between devices: 5.28 us -> 6.07 us  [swap(): return lax.ppermute(array, axis, [(0, 1), (1, 0)])]
  transfers between devices with their start and end apart: 45 -> 50, of which waited for: 30 -> 26; matrix products, arithmetic and copies ran while one was open for 0% -> 0% of each run, Pallas kernels for 6% -> 7%
where the time goes in v1:
time: 161 us; the launch traced here: 159 us
  starting transfers between devices  76.8 us (48%)
  waiting for transfers between devices  38.5 us (24%)
  Pallas kernels  38.1 us (24%)
  local copies, waits for them, and re-layouts  4.87 us (3%)
    ppermute x36, starting transfers between devices, from_peers(): lax.ppermute(arrays[k], axis, [(i, (i + k) % n) for i in range(n)])  53.7 us
    pallas_call x22, Pallas kernels, call(): return made(*args)  38.1 us
    ppermute x36, waiting for transfers between devices, from_peers(): lax.ppermute(arrays[k], axis, [(i, (i + k) % n) for i in range(n)])  32.4 us
    ppermute x13, starting transfers between devices, swap(): return lax.ppermute(array, axis, [(0, 1), (1, 0)])  18.9 us
    ppermute x13, waiting for transfers between devices, swap(): return lax.ppermute(array, axis, [(0, 1), (1, 0)])  6.07 us
    unnamed x16, local copies, waits for them, and re-layouts  4.36 us
    all_to_all x1, starting transfers between devices, step(): arrived = lax.all_to_all(spread, (ay, ax), 0, 0, tiled=True)  4.2 us
  transfers between devices with their start and end apart: 50, of which 26 were waited for; matrix products, arithmetic and copies ran while one was open for 0% of the time, Pallas kernels for 7%

profile of v1, /device:TPU:1, one launch (start us, length us, event | category | flops | bytes accessed | tf_op | source)
XLA Modules:
  0.0 159.2 jit_solution(14842582309956080060)
XLA Ops:
  3.2 1.9 %shard_map.94 = (f32[264,128]{1,0:T(8,128)S(1)}, f32[264,128]{1,0:T(8,128)S(1)}, f32[264,128]{1,0:T(8,128)S(1)}, f32[264,128]{1,0:T(8,128)S(1)}) custom-call(s32[4]{0:T(128)S(1)} %pad_add_fusion.place, s32[4,1024]{1,0:T(4,128)S(1)} %copy-done.4, f32[1,1024]{1,0:T(1,128)S(1)} %bitcast.8, bf16[1024,256]{1,0:T(8,128)(2,1)S(1)} %copy-done.2), custom_call_target="tpu_custom_call" | custom-call | tf_op jit(solution)/shard_map/pallas_call | solution.py:457
  5.1 2.5 %collective-permute-start = (f32[264,128]{1,0:T(8,128)S(1)}, f32[264,128]{1,0:T(8,128)S(1)}, u32[]{:S(2)}, u32[]{:S(2)}) collective-permute-start(f32[264,128]{1,0:T(8,128)S(1)} %get-tuple-element.46), channel_id=1, source_target_pairs={{0,1},{1,2},{2,3},{3,0},{4,5},{5,6},{6,7},{7,4},{8,9},{9,10},{10,1... | collective-permute-start | bytes 405512 | tf_op jit(solution)/shard_map/ppermute | solution.py:464
  7.6 3.3 %collective-permute-start.1 = (f32[264,128]{1,0:T(8,128)S(1)}, f32[264,128]{1,0:T(8,128)S(1)}, u32[]{:S(2)}, u32[]{:S(2)}) collective-permute-start(f32[264,128]{1,0:T(8,128)S(1)} %get-tuple-element.47), channel_id=1, source_target_pairs={{0,2},{1,3},{2,0},{3,1},{4,6},{5,7},{6,4},{7,5},{8,10},{9,11},{10,... | collective-permute-start | bytes 405512 | tf_op jit(solution)/shard_map/ppermute | solution.py:464
  11.7 1.2 copy-done
  13.6 1.3 shard_map.93
  15.7 1.1 collective-permute-done.1.g2
  16.9 3.3 %shard_map.95.e0.packed = f32[264,128]{1,0:T(8,128)S(1)} custom-call(f32[8,1024]{1,0:T(8,128)S(1)} %get-tuple-element.44.table, f32[264,128]{1,0:T(8,128)S(1)} %get-tuple-element.45.g0, f32[264,128]{1,0:T(8,128)S(1)} %collective-permute-done.g1, f32[264,128]{1,0:T(8,128)S(1)} %collective-permute-done.1.g2, f32[264,128]{1,0:T(8,128)S(1)} %collective-permute-done.2.g3), custom_call_target="tpu_custom_call" | custom-call | tf_op jit(solution)/shard_map/pallas_call | solution.py:457
  20.2 1.7 %collective-permute-start.3 = (f32[264,128]{1,0:T(8,128)S(1)}, f32[264,128]{1,0:T(8,128)S(1)}, u32[]{:S(2)}, u32[]{:S(2)}) collective-permute-start(f32[264,128]{1,0:T(8,128)S(1)} %shard_map.95.e0.packed), channel_id=1, source_target_pairs={{0,1},{1,2},{2,3},{3,0},{4,5},{5,6},{6,7},{7,4},{8,9},{9,10},{10,1... | collective-permute-start | bytes 405512 | tf_op jit(solution)/shard_map/ppermute | solution.py:464
  21.9 1.9 %collective-permute-start.4 = (f32[264,128]{1,0:T(8,128)S(1)}, f32[264,128]{1,0:T(8,128)S(1)}, u32[]{:S(2)}, u32[]{:S(2)}) collective-permute-start(f32[264,128]{1,0:T(8,128)S(1)} %shard_map.95.e0.packed), channel_id=1, source_target_pairs={{0,2},{1,3},{2,0},{3,1},{4,6},{5,7},{6,4},{7,5},{8,10},{9,11},{10,... | collective-permute-start | bytes 405512 | tf_op jit(solution)/shard_map/ppermute | solution.py:464
  25.3 2.4 %collective-permute-start.8 = (f32[128,256]{1,0:T(8,128)S(1)}, f32[128,256]{1,0:T(8,128)S(1)}, u32[]{:S(2)}, u32[]{:S(2)}) collective-permute-start(f32[128,256]{1,0:T(8,128)S(1)} %get-tuple-element.53), channel_id=1, source_target_pairs={{0,3},{1,0},{2,1},{3,2},{4,7},{5,4},{6,5},{7,6},{8,11},{9,8},{10,9... | collective-permute-start | bytes 393224 | tf_op jit(solution)/shard_map/ppermute | solution.py:464
  27.7 4.5 %collective-permute-done.7.p2 = f32[128,256]{1,0:T(8,128)S(1)} collective-permute-done((f32[128,256]{1,0:T(8,128)S(1)}, f32[128,256]{1,0:T(8,128)S(1)}, u32[]{:S(2)}, u32[]{:S(2)}) %collective-permute-start.7) | collective-permute-done | bytes 131104 | tf_op jit(solution)/shard_map/ppermute | solution.py:464
  32.2 1.5 collective-permute-done.8.p3
  33.7 2.9 %shard_map.97 = (f32[128,256]{1,0:T(8,128)S(1)}, f32[8,256]{1,0:T(8,128)S(1)}) custom-call(f32[8,1024]{1,0:T(8,128)S(1)} %get-tuple-element.44.table, f32[264,128]{1,0:T(8,128)S(1)} %shard_map.95.e0.packed, f32[128,256]{1,0:T(8,128)S(1)} %get-tuple-element.50.p0, f32[128,256]{1,0:T(8,128)S(1)} %collective-permute-done.6.p1, ...), custom_call_target="tpu_custom_call" | custom-call | tf_op jit(solution)/shard_map/pallas_call | solution.py:457
  36.6 5.9 %shard_map.96 = (bf16[28,256,256]{2,1,0:T(8,128)(2,1)S(1)}, bf16[28,256,256]{2,1,0:T(8,128)(2,1)S(1)}, f32[4,256,256]{2,1,0:T(8,128)S(1)}, f32[256,256]{1,0:T(8,128)S(1)}) custom-call(s32[4]{0:T(128)S(1)} %pad_add_fusion.place, f32[264,128]{1,0:T(8,128)S(1)} %shard_map.95.e0.packed, f32[264,128]{1,0:T(8,128)S(1)} %collective-permute-done.3.e1, ...), custom_call_target="tpu_custom_call" | custom-call | tf_op jit(solution)/shard_map/pallas_call | solution.py:457
  42.6 3.3 %collective-permute-start.9 = (f32[256,256]{1,0:T(8,128)S(1)}, f32[256,256]{1,0:T(8,128)S(1)}, u32[]{:S(2)}, u32[]{:S(2)}) collective-permute-start(f32[256,256]{1,0:T(8,128)S(1)} %get-tuple-element.55.mine), channel_id=1, source_target_pairs={{0,4},{4,0},{1,5},{5,1},{2,6},{6,2},{3,7},{7,3},{8,12},{12,8},{9,1... | collective-permute-start | bytes 786440 | tf_op jit(solution)/shard_map/ppermute | solution.py:473
  46.9 2.5 %collective-permute-start.11 = (f32[8,256]{1,0:T(8,128)S(1)}, f32[8,256]{1,0:T(8,128)S(1)}, u32[]{:S(2)}, u32[]{:S(2)}) collective-permute-start(f32[8,256]{1,0:T(8,128)S(1)} %get-tuple-element.57.v0), channel_id=1, source_target_pairs={{0,2},{1,3},{2,0},{3,1},{4,6},{5,7},{6,4},{7,5},{8,10},{9,11},{10,... | collective-permute-start | bytes 24584 | tf_op jit(solution)/shard_map/ppermute | solution.py:464
  49.6 1.3 collective-permute-done.11.v2
  51.0 1.1 collective-permute-done.12.v3
  52.0 1.1 shard_map.98
  53.1 1.6 %collective-permute-start.13 = (f32[8,256]{1,0:T(8,128)S(1)}, f32[8,256]{1,0:T(8,128)S(1)}, u32[]{:S(2)}, u32[]{:S(2)}) collective-permute-start(f32[8,256]{1,0:T(8,128)S(1)} %get-tuple-element.58.v_mine), channel_id=1, source_target_pairs={{0,4},{4,0},{1,5},{5,1},{2,6},{6,2},{3,7},{7,3},{8,12},{12,8},{9,1... | collective-permute-start | bytes 24584 | tf_op jit(solution)/shard_map/ppermute | solution.py:473
  56.5 1.3 collective-permute-start.14
  57.8 2.5 %collective-permute-start.15 = (f32[136,256]{1,0:T(8,128)S(1)}, f32[136,256]{1,0:T(8,128)S(1)}, u32[]{:S(2)}, u32[]{:S(2)}) collective-permute-start(f32[136,256]{1,0:T(8,128)S(1)} %get-tuple-element.60), channel_id=1, source_target_pairs={{0,16},{8,24},{16,0},{24,8},{1,17},{9,25},{17,1},{25,9},{2,18},{10... | collective-permute-start | bytes 417800 | tf_op jit(solution)/shard_map/ppermute | solution.py:464
  60.2 1.1 collective-permute-start.16
  61.4 1.3 collective-permute-done.14.m1
  62.7 1.2 collective-permute-start.17
  63.9 2.8 %collective-permute-done.15.m2 = f32[136,256]{1,0:T(8,128)S(1)} collective-permute-done((f32[136,256]{1,0:T(8,128)S(1)}, f32[136,256]{1,0:T(8,128)S(1)}, u32[]{:S(2)}, u32[]{:S(2)}) %collective-permute-start.15) | collective-permute-done | bytes 139296 | tf_op jit(solution)/shard_map/ppermute | solution.py:464
  66.6 1.2 collective-permute-start.18
  69.2 1.5 shard_map.100
  70.7 1.4 collective-permute-start.20
  72.1 2.6 %collective-permute-start.21 = (f32[136,256]{1,0:T(8,128)S(1)}, f32[136,256]{1,0:T(8,128)S(1)}, u32[]{:S(2)}, u32[]{:S(2)}) collective-permute-start(f32[136,256]{1,0:T(8,128)S(1)} %get-tuple-element.62), channel_id=1, source_target_pairs={{0,64},{32,96},{64,0},{96,32},{1,65},{33,97},{65,1},{97,33},{2,66}... | collective-permute-start | bytes 417800 | tf_op jit(solution)/shard_map/ppermute | solution.py:464
  74.7 1.1 collective-permute-start.22
  75.8 1.4 collective-permute-done.20.m1
  78.1 3.1 %collective-permute-done.21.m2 = f32[136,256]{1,0:T(8,128)S(1)} collective-permute-done((f32[136,256]{1,0:T(8,128)S(1)}, f32[136,256]{1,0:T(8,128)S(1)}, u32[]{:S(2)}, u32[]{:S(2)}) %collective-permute-start.21) | collective-permute-done | bytes 139296 | tf_op jit(solution)/shard_map/ppermute | solution.py:464
  82.3 1.2 collective-permute-start.27
  84.5 3.9 %collective-permute-done.27.p2 = f32[128,256]{1,0:T(8,128)S(1)} collective-permute-done((f32[128,256]{1,0:T(8,128)S(1)}, f32[128,256]{1,0:T(8,128)S(1)}, u32[]{:S(2)}, u32[]{:S(2)}) %collective-permute-start.27) | collective-permute-done | bytes 131104 | tf_op jit(solution)/shard_map/ppermute | solution.py:464
  88.4 1.9 %collective-permute-done.28.p3 = f32[128,256]{1,0:T(8,128)S(1)} collective-permute-done((f32[128,256]{1,0:T(8,128)S(1)}, f32[128,256]{1,0:T(8,128)S(1)}, u32[]{:S(2)}, u32[]{:S(2)}) %collective-permute-start.28) | collective-permute-done | bytes 131104 | tf_op jit(solution)/shard_map/ppermute | solution.py:464
  90.3 5.6 %shard_map.101 = (f32[4,128,256]{2,1,0:T(8,128)S(1)}, f32[4,128,256]{2,1,0:T(8,128)S(1)}, f32[4,8,256]{2,1,0:T(8,128)S(1)}, f32[8,256]{1,0:T(8,128)S(1)}, f32[4,264,256]{2,1,0:T(8,128)S(1)}) custom-call(s32[4]{0:T(128)S(1)} %pad_add_fusion.place, f32[8,1024]{1,0:T(8,128)S(1)} %get-tuple-element.44.table, f32[264,256]{1,0:T(8,128)S(1)} %get-tuple-element.61.own, ...), custom_call_target="tpu_custom_call" | custom-call | tf_op jit(solution)/shard_map/pallas_call | solution.py:457
  95.9 1.4 collective-permute-start.29
  99.8 2.5 %collective-permute-start.31 = (f32[8,256]{1,0:T(8,128)S(1)}, f32[8,256]{1,0:T(8,128)S(1)}, u32[]{:S(2)}, u32[]{:S(2)}) collective-permute-start(f32[8,256]{1,0:T(8,128)S(1)} %shard_map.102.q0), channel_id=1, source_target_pairs={{0,16},{8,24},{16,0},{24,8},{1,17},{9,25},{17,1},{25,9},{2,18},{10... | collective-permute-start | bytes 24584 | tf_op jit(solution)/shard_map/ppermute | solution.py:464
  102.3 1.1 collective-permute-start.32
  103.8 1.3 collective-permute-done.32.q3
  105.1 1.3 shard_map.103
  106.3 1.2 collective-permute-start.33
  107.6 2.5 %collective-permute-start.34 = (f32[8,256]{1,0:T(8,128)S(1)}, f32[8,256]{1,0:T(8,128)S(1)}, u32[]{:S(2)}, u32[]{:S(2)}) collective-permute-start(f32[8,256]{1,0:T(8,128)S(1)} %get-tuple-element.69.gy0), channel_id=1, source_target_pairs={{0,64},{32,96},{64,0},{96,32},{1,65},{33,97},{65,1},{97,33},{2,66}... | collective-permute-start | bytes 24584 | tf_op jit(solution)/shard_map/ppermute | solution.py:464
  110.0 1.1 collective-permute-start.35
  112.6 5.8 %shard_map.104 = (f32[512,256]{1,0:T(8,128)}, bf16[512,256]{1,0:T(8,128)(2,1)S(1)}, bf16[512,256]{1,0:T(8,128)(2,1)S(1)}, f32[136,128]{1,0:T(8,128)S(1)}, f32[136,128]{1,0:T(8,128)S(1)}) custom-call(s32[4]{0:T(128)S(1)} %pad_add_fusion.place, f32[8,1024]{1,0:T(8,128)S(1)} %get-tuple-element.44.table, f32[8,256]{1,0:T(8,128)S(1)} %get-tuple-element.69.gy0, ...), custom_call_target="tpu_custom_call" | custom-call | tf_op jit(solution)/shard_map/pallas_call | solution.py:457
  118.4 1.3 shard_map.105
  119.8 3.5 %collective-permute-start.36 = (f32[16,64,128]{2,1,0:T(8,128)S(1)}, f32[16,64,128]{2,1,0:T(8,128)S(1)}, u32[]{:S(2)}, u32[]{:S(2)}) collective-permute-start(f32[16,64,128]{2,1,0:T(8,128)S(1)} %get-tuple-element.79), channel_id=1, source_target_pairs={{0,4},{4,0},{1,5},{5,1},{2,6},{6,2},{3,7},{7,3},{8,12},{12,8},{9,1... | collective-permute-start | bytes 1572872 | tf_op jit(solution)/shard_map/ppermute | solution.py:473
  123.3 1.5 collective-permute-done.36.b
  125.7 4.2 %all-to-all-start = ((f32[16,64,128]{2,1,0:T(8,128)}), f32[16,64,128]{2,1,0:T(8,128)S(1)}, u32[]{:S(2)}, u32[]{:S(2)}) async-start(f32[16,64,128]{2,1,0:T(8,128)} %shard_map.106), calls=%async_computation | async-start | bytes 1048576 | tf_op jit(solution)/shard_map/all_to_all | solution.py:557
  130.8 1.4 shard_map.109.s
  132.3 1.1 collective-permute-done.38.s_far
  133.5 1.6 %collective-permute-start.39 = (f32[144,128]{1,0:T(8,128)S(1)}, f32[144,128]{1,0:T(8,128)S(1)}, u32[]{:S(2)}, u32[]{:S(2)}) collective-permute-start(f32[144,128]{1,0:T(8,128)S(1)} %shard_map.110.a), channel_id=1, source_target_pairs={{0,8},{8,16},{16,24},{24,0},{1,9},{9,17},{17,25},{25,1},{2,10},{10... | collective-permute-start | bytes 221192 | tf_op jit(solution)/shard_map/ppermute | solution.py:464
  135.1 2.4 %collective-permute-start.40 = (f32[144,128]{1,0:T(8,128)S(1)}, f32[144,128]{1,0:T(8,128)S(1)}, u32[]{:S(2)}, u32[]{:S(2)}) collective-permute-start(f32[144,128]{1,0:T(8,128)S(1)} %shard_map.110.a), channel_id=1, source_target_pairs={{0,16},{8,24},{16,0},{24,8},{1,17},{9,25},{17,1},{25,9},{2,18},{10... | collective-permute-start | bytes 221192 | tf_op jit(solution)/shard_map/ppermute | solution.py:464
  137.5 1.2 collective-permute-start.41
  138.7 1.8 %collective-permute-done.39.b = f32[144,128]{1,0:T(8,128)S(1)} collective-permute-done((f32[144,128]{1,0:T(8,128)S(1)}, f32[144,128]{1,0:T(8,128)S(1)}, u32[]{:S(2)}, u32[]{:S(2)}) %collective-permute-start.39) | collective-permute-done | bytes 73760 | tf_op jit(solution)/shard_map/ppermute | solution.py:464
  140.4 1.2 collective-permute-done.40.c
  141.7 1.3 collective-permute-start.42
  142.9 2.4 %collective-permute-start.43 = (f32[144,128]{1,0:T(8,128)S(1)}, f32[144,128]{1,0:T(8,128)S(1)}, u32[]{:S(2)}, u32[]{:S(2)}) collective-permute-start(f32[144,128]{1,0:T(8,128)S(1)} %shard_map.111.a), channel_id=1, source_target_pairs={{0,64},{32,96},{64,0},{96,32},{1,65},{33,97},{65,1},{97,33},{2,66}... | collective-permute-start | bytes 221192 | tf_op jit(solution)/shard_map/ppermute | solution.py:464
  145.3 1.2 collective-permute-start.44
  146.5 1.4 collective-permute-done.43.c
  149.6 2.9 %collective-permute-start.47 = (f32[8,128]{1,0:T(8,128)S(1)}, f32[8,128]{1,0:T(8,128)S(1)}, u32[]{:S(2)}, u32[]{:S(2)}) collective-permute-start(f32[8,128]{1,0:T(8,128)S(1)} %get-tuple-element.83.s0), channel_id=1, source_target_pairs={{0,2},{1,3},{2,0},{3,1},{4,6},{5,7},{6,4},{7,5},{8,10},{9,11},{10,... | collective-permute-start | bytes 12296 | tf_op jit(solution)/shard_map/ppermute | solution.py:464
  152.5 3.8 %collective-permute-start.45 = (f32[136,128]{1,0:T(8,128)S(1)}, f32[136,128]{1,0:T(8,128)S(1)}, u32[]{:S(2)}, u32[]{:S(2)}) collective-permute-start(f32[136,128]{1,0:T(8,128)S(1)} %get-tuple-element.82.mine), channel_id=1, source_target_pairs={{0,4},{4,0},{1,5},{5,1},{2,6},{6,2},{3,7},{7,3},{8,12},{12,8},{9,1... | collective-permute-start | bytes 208904 | tf_op jit(solution)/shard_map/ppermute | solution.py:473
  157.2 1.3 shard_map.113
  (76 shorter events, 23.2 us)
Async XLA Ops:
  0.7 1.0 copy-start.2
  1.8 0.7 copy-start.4
  2.5 0.7 copy-start.5
  5.1 10.6 %collective-permute-start = (f32[264,128]{1,0:T(8,128)S(1)}, f32[264,128]{1,0:T(8,128)S(1)}, u32[]{:S(2)}, u32[]{:S(2)}) collective-permute-start(f32[264,128]{1,0:T(8,128)S(1)} %get-tuple-element.46), channel_id=1, source_target_pairs={{0,1},{1,2},{2,3},{3,0},{4,5},{5,6},{6,7},{7,4},{8,9},{9,10},{10,1... | collective-permute-start | bytes 405512 | tf_op jit(solution)/shard_map/ppermute | solution.py:464
  7.6 9.2 %collective-permute-start.1 = (f32[264,128]{1,0:T(8,128)S(1)}, f32[264,128]{1,0:T(8,128)S(1)}, u32[]{:S(2)}, u32[]{:S(2)}) collective-permute-start(f32[264,128]{1,0:T(8,128)S(1)} %get-tuple-element.47), channel_id=1, source_target_pairs={{0,2},{1,3},{2,0},{3,1},{4,6},{5,7},{6,4},{7,5},{8,10},{9,11},{10,... | collective-permute-start | bytes 405512 | tf_op jit(solution)/shard_map/ppermute | solution.py:464
  10.9 5.9 %collective-permute-start.2 = (f32[264,128]{1,0:T(8,128)S(1)}, f32[264,128]{1,0:T(8,128)S(1)}, u32[]{:S(2)}, u32[]{:S(2)}) collective-permute-start(f32[264,128]{1,0:T(8,128)S(1)} %get-tuple-element.48), channel_id=1, source_target_pairs={{0,3},{1,0},{2,1},{3,2},{4,7},{5,4},{6,5},{7,6},{8,11},{9,8},{10,9... | collective-permute-start | bytes 405512 | tf_op jit(solution)/shard_map/ppermute | solution.py:464
  11.7 1.2 copy-start
  12.9 0.7 copy-start.6
  14.9 10.4 %collective-permute-start.6 = (f32[128,256]{1,0:T(8,128)S(1)}, f32[128,256]{1,0:T(8,128)S(1)}, u32[]{:S(2)}, u32[]{:S(2)}) collective-permute-start(f32[128,256]{1,0:T(8,128)S(1)} %get-tuple-element.51), channel_id=1, source_target_pairs={{0,1},{1,2},{2,3},{3,0},{4,5},{5,6},{6,7},{7,4},{8,9},{9,10},{10,1... | collective-permute-start | bytes 393224 | tf_op jit(solution)/shard_map/ppermute | solution.py:464
  20.2 16.5 %collective-permute-start.3 = (f32[264,128]{1,0:T(8,128)S(1)}, f32[264,128]{1,0:T(8,128)S(1)}, u32[]{:S(2)}, u32[]{:S(2)}) collective-permute-start(f32[264,128]{1,0:T(8,128)S(1)} %shard_map.95.e0.packed), channel_id=1, source_target_pairs={{0,1},{1,2},{2,3},{3,0},{4,5},{5,6},{6,7},{7,4},{8,9},{9,10},{10,1... | collective-permute-start | bytes 405512 | tf_op jit(solution)/shard_map/ppermute | solution.py:464
  21.9 14.8 %collective-permute-start.4 = (f32[264,128]{1,0:T(8,128)S(1)}, f32[264,128]{1,0:T(8,128)S(1)}, u32[]{:S(2)}, u32[]{:S(2)}) collective-permute-start(f32[264,128]{1,0:T(8,128)S(1)} %shard_map.95.e0.packed), channel_id=1, source_target_pairs={{0,2},{1,3},{2,0},{3,1},{4,6},{5,7},{6,4},{7,5},{8,10},{9,11},{10,... | collective-permute-start | bytes 405512 | tf_op jit(solution)/shard_map/ppermute | solution.py:464
  23.8 12.8 %collective-permute-start.5 = (f32[264,128]{1,0:T(8,128)S(1)}, f32[264,128]{1,0:T(8,128)S(1)}, u32[]{:S(2)}, u32[]{:S(2)}) collective-permute-start(f32[264,128]{1,0:T(8,128)S(1)} %shard_map.95.e0.packed), channel_id=1, source_target_pairs={{0,3},{1,0},{2,1},{3,2},{4,7},{5,4},{6,5},{7,6},{8,11},{9,8},{10,9... | collective-permute-start | bytes 405512 | tf_op jit(solution)/shard_map/ppermute | solution.py:464
  24.4 7.9 %collective-permute-start.7 = (f32[128,256]{1,0:T(8,128)S(1)}, f32[128,256]{1,0:T(8,128)S(1)}, u32[]{:S(2)}, u32[]{:S(2)}) collective-permute-start(f32[128,256]{1,0:T(8,128)S(1)} %get-tuple-element.52), channel_id=1, source_target_pairs={{0,2},{1,3},{2,0},{3,1},{4,6},{5,7},{6,4},{7,5},{8,10},{9,11},{10,... | collective-permute-start | bytes 393224 | tf_op jit(solution)/shard_map/ppermute | solution.py:464
  25.3 8.4 %collective-permute-start.8 = (f32[128,256]{1,0:T(8,128)S(1)}, f32[128,256]{1,0:T(8,128)S(1)}, u32[]{:S(2)}, u32[]{:S(2)}) collective-permute-start(f32[128,256]{1,0:T(8,128)S(1)} %get-tuple-element.53), channel_id=1, source_target_pairs={{0,3},{1,0},{2,1},{3,2},{4,7},{5,4},{6,5},{7,6},{8,11},{9,8},{10,9... | collective-permute-start | bytes 393224 | tf_op jit(solution)/shard_map/ppermute | solution.py:464
  42.6 13.0 %collective-permute-start.9 = (f32[256,256]{1,0:T(8,128)S(1)}, f32[256,256]{1,0:T(8,128)S(1)}, u32[]{:S(2)}, u32[]{:S(2)}) collective-permute-start(f32[256,256]{1,0:T(8,128)S(1)} %get-tuple-element.55.mine), channel_id=1, source_target_pairs={{0,4},{4,0},{1,5},{5,1},{2,6},{6,2},{3,7},{7,3},{8,12},{12,8},{9,1... | collective-permute-start | bytes 786440 | tf_op jit(solution)/shard_map/ppermute | solution.py:473
  45.9 3.7 %collective-permute-start.10 = (f32[8,256]{1,0:T(8,128)S(1)}, f32[8,256]{1,0:T(8,128)S(1)}, u32[]{:S(2)}, u32[]{:S(2)}) collective-permute-start(f32[8,256]{1,0:T(8,128)S(1)} %get-tuple-element.57.v0), channel_id=1, source_target_pairs={{0,1},{1,2},{2,3},{3,0},{4,5},{5,6},{6,7},{7,4},{8,9},{9,10},{10,1... | collective-permute-start | bytes 24584 | tf_op jit(solution)/shard_map/ppermute | solution.py:464
  46.9 4.1 %collective-permute-start.11 = (f32[8,256]{1,0:T(8,128)S(1)}, f32[8,256]{1,0:T(8,128)S(1)}, u32[]{:S(2)}, u32[]{:S(2)}) collective-permute-start(f32[8,256]{1,0:T(8,128)S(1)} %get-tuple-element.57.v0), channel_id=1, source_target_pairs={{0,2},{1,3},{2,0},{3,1},{4,6},{5,7},{6,4},{7,5},{8,10},{9,11},{10,... | collective-permute-start | bytes 24584 | tf_op jit(solution)/shard_map/ppermute | solution.py:464
  49.4 2.7 %collective-permute-start.12 = (f32[8,256]{1,0:T(8,128)S(1)}, f32[8,256]{1,0:T(8,128)S(1)}, u32[]{:S(2)}, u32[]{:S(2)}) collective-permute-start(f32[8,256]{1,0:T(8,128)S(1)} %get-tuple-element.57.v0), channel_id=1, source_target_pairs={{0,3},{1,0},{2,1},{3,2},{4,7},{5,4},{6,5},{7,6},{8,11},{9,8},{10,9... | collective-permute-start | bytes 24584 | tf_op jit(solution)/shard_map/ppermute | solution.py:464
  53.1 2.5 %collective-permute-start.13 = (f32[8,256]{1,0:T(8,128)S(1)}, f32[8,256]{1,0:T(8,128)S(1)}, u32[]{:S(2)}, u32[]{:S(2)}) collective-permute-start(f32[8,256]{1,0:T(8,128)S(1)} %get-tuple-element.58.v_mine), channel_id=1, source_target_pairs={{0,4},{4,0},{1,5},{5,1},{2,6},{6,2},{3,7},{7,3},{8,12},{12,8},{9,1... | collective-permute-start | bytes 24584 | tf_op jit(solution)/shard_map/ppermute | solution.py:473
  56.5 6.2 %collective-permute-start.14 = (f32[136,256]{1,0:T(8,128)S(1)}, f32[136,256]{1,0:T(8,128)S(1)}, u32[]{:S(2)}, u32[]{:S(2)}) collective-permute-start(f32[136,256]{1,0:T(8,128)S(1)} %get-tuple-element.60), channel_id=1, source_target_pairs={{0,8},{8,16},{16,24},{24,0},{1,9},{9,17},{17,25},{25,1},{2,10},{10... | collective-permute-start | bytes 417800 | tf_op jit(solution)/shard_map/ppermute | solution.py:464
  57.8 8.9 %collective-permute-start.15 = (f32[136,256]{1,0:T(8,128)S(1)}, f32[136,256]{1,0:T(8,128)S(1)}, u32[]{:S(2)}, u32[]{:S(2)}) collective-permute-start(f32[136,256]{1,0:T(8,128)S(1)} %get-tuple-element.60), channel_id=1, source_target_pairs={{0,16},{8,24},{16,0},{24,8},{1,17},{9,25},{17,1},{25,9},{2,18},{10... | collective-permute-start | bytes 417800 | tf_op jit(solution)/shard_map/ppermute | solution.py:464
  60.2 7.6 %collective-permute-start.16 = (f32[136,256]{1,0:T(8,128)S(1)}, f32[136,256]{1,0:T(8,128)S(1)}, u32[]{:S(2)}, u32[]{:S(2)}) collective-permute-start(f32[136,256]{1,0:T(8,128)S(1)} %get-tuple-element.60), channel_id=1, source_target_pairs={{0,24},{8,0},{16,8},{24,16},{1,25},{9,1},{17,9},{25,17},{2,26},{10... | collective-permute-start | bytes 417800 | tf_op jit(solution)/shard_map/ppermute | solution.py:464
  62.7 5.2 %collective-permute-start.17 = (f32[136,256]{1,0:T(8,128)S(1)}, f32[136,256]{1,0:T(8,128)S(1)}, u32[]{:S(2)}, u32[]{:S(2)}) collective-permute-start(f32[136,256]{1,0:T(8,128)S(1)} %collective-permute-done.14.m1), channel_id=1, source_target_pairs={{0,4},{4,0},{1,5},{5,1},{2,6},{6,2},{3,7},{7,3},{8,12},{12,8},{9,1... | collective-permute-start | bytes 417800 | tf_op jit(solution)/shard_map/ppermute | solution.py:473
  66.6 2.2 %collective-permute-start.18 = (f32[136,256]{1,0:T(8,128)S(1)}, f32[136,256]{1,0:T(8,128)S(1)}, u32[]{:S(2)}, u32[]{:S(2)}) collective-permute-start(f32[136,256]{1,0:T(8,128)S(1)} %collective-permute-done.15.m2), channel_id=1, source_target_pairs={{0,4},{4,0},{1,5},{5,1},{2,6},{6,2},{3,7},{7,3},{8,12},{12,8},{9,1... | collective-permute-start | bytes 417800 | tf_op jit(solution)/shard_map/ppermute | solution.py:473
  67.8 1.4 collective-permute-start.19
  70.7 6.4 %collective-permute-start.20 = (f32[136,256]{1,0:T(8,128)S(1)}, f32[136,256]{1,0:T(8,128)S(1)}, u32[]{:S(2)}, u32[]{:S(2)}) collective-permute-start(f32[136,256]{1,0:T(8,128)S(1)} %get-tuple-element.62), channel_id=1, source_target_pairs={{0,32},{32,64},{64,96},{96,0},{1,33},{33,65},{65,97},{97,1},{2,34}... | collective-permute-start | bytes 417800 | tf_op jit(solution)/shard_map/ppermute | solution.py:464
  72.1 9.2 %collective-permute-start.21 = (f32[136,256]{1,0:T(8,128)S(1)}, f32[136,256]{1,0:T(8,128)S(1)}, u32[]{:S(2)}, u32[]{:S(2)}) collective-permute-start(f32[136,256]{1,0:T(8,128)S(1)} %get-tuple-element.62), channel_id=1, source_target_pairs={{0,64},{32,96},{64,0},{96,32},{1,65},{33,97},{65,1},{97,33},{2,66}... | collective-permute-start | bytes 417800 | tf_op jit(solution)/shard_map/ppermute | solution.py:464
  74.7 7.6 %collective-permute-start.22 = (f32[136,256]{1,0:T(8,128)S(1)}, f32[136,256]{1,0:T(8,128)S(1)}, u32[]{:S(2)}, u32[]{:S(2)}) collective-permute-start(f32[136,256]{1,0:T(8,128)S(1)} %get-tuple-element.62), channel_id=1, source_target_pairs={{0,96},{32,0},{64,32},{96,64},{1,97},{33,1},{65,33},{97,65},{2,98}... | collective-permute-start | bytes 417800 | tf_op jit(solution)/shard_map/ppermute | solution.py:464
  75.8 7.8 %collective-permute-start.26 = (f32[128,256]{1,0:T(8,128)S(1)}, f32[128,256]{1,0:T(8,128)S(1)}, u32[]{:S(2)}, u32[]{:S(2)}) collective-permute-start(f32[128,256]{1,0:T(8,128)S(1)} %get-tuple-element.64.p0), channel_id=1, source_target_pairs={{0,1},{1,2},{2,3},{3,0},{4,5},{5,6},{6,7},{7,4},{8,9},{9,10},{10,1... | collective-permute-start | bytes 393224 | tf_op jit(solution)/shard_map/ppermute | solution.py:464
  77.1 13.1 %collective-permute-start.23 = (f32[136,256]{1,0:T(8,128)S(1)}, f32[136,256]{1,0:T(8,128)S(1)}, u32[]{:S(2)}, u32[]{:S(2)}) collective-permute-start(f32[136,256]{1,0:T(8,128)S(1)} %collective-permute-done.20.m1), channel_id=1, source_target_pairs={{0,4},{4,0},{1,5},{5,1},{2,6},{6,2},{3,7},{7,3},{8,12},{12,8},{9,1... | collective-permute-start | bytes 417800 | tf_op jit(solution)/shard_map/ppermute | solution.py:473
  81.3 9.0 %collective-permute-start.24 = (f32[136,256]{1,0:T(8,128)S(1)}, f32[136,256]{1,0:T(8,128)S(1)}, u32[]{:S(2)}, u32[]{:S(2)}) collective-permute-start(f32[136,256]{1,0:T(8,128)S(1)} %collective-permute-done.21.m2), channel_id=1, source_target_pairs={{0,4},{4,0},{1,5},{5,1},{2,6},{6,2},{3,7},{7,3},{8,12},{12,8},{9,1... | collective-permute-start | bytes 417800 | tf_op jit(solution)/shard_map/ppermute | solution.py:473
  82.3 8.0 %collective-permute-start.25 = (f32[136,256]{1,0:T(8,128)S(1)}, f32[136,256]{1,0:T(8,128)S(1)}, u32[]{:S(2)}, u32[]{:S(2)}) collective-permute-start(f32[136,256]{1,0:T(8,128)S(1)} %collective-permute-done.22.m3), channel_id=1, source_target_pairs={{0,4},{4,0},{1,5},{5,1},{2,6},{6,2},{3,7},{7,3},{8,12},{12,8},{9,1... | collective-permute-start | bytes 417800 | tf_op jit(solution)/shard_map/ppermute | solution.py:473
  82.3 6.1 %collective-permute-start.27 = (f32[128,256]{1,0:T(8,128)S(1)}, f32[128,256]{1,0:T(8,128)S(1)}, u32[]{:S(2)}, u32[]{:S(2)}) collective-permute-start(f32[128,256]{1,0:T(8,128)S(1)} %get-tuple-element.64.p0), channel_id=1, source_target_pairs={{0,2},{1,3},{2,0},{3,1},{4,6},{5,7},{6,4},{7,5},{8,10},{9,11},{10,... | collective-permute-start | bytes 393224 | tf_op jit(solution)/shard_map/ppermute | solution.py:464
  83.5 6.7 %collective-permute-start.28 = (f32[128,256]{1,0:T(8,128)S(1)}, f32[128,256]{1,0:T(8,128)S(1)}, u32[]{:S(2)}, u32[]{:S(2)}) collective-permute-start(f32[128,256]{1,0:T(8,128)S(1)} %get-tuple-element.64.p0), channel_id=1, source_target_pairs={{0,3},{1,0},{2,1},{3,2},{4,7},{5,4},{6,5},{7,6},{8,11},{9,8},{10,9... | collective-permute-start | bytes 393224 | tf_op jit(solution)/shard_map/ppermute | solution.py:464
  95.9 2.2 %collective-permute-start.29 = (f32[8,256]{1,0:T(8,128)S(1)}, f32[8,256]{1,0:T(8,128)S(1)}, u32[]{:S(2)}, u32[]{:S(2)}) collective-permute-start(f32[8,256]{1,0:T(8,128)S(1)} %get-tuple-element.68.own), channel_id=1, source_target_pairs={{0,4},{4,0},{1,5},{5,1},{2,6},{6,2},{3,7},{7,3},{8,12},{12,8},{9,1... | collective-permute-start | bytes 24584 | tf_op jit(solution)/shard_map/ppermute | solution.py:473
  98.8 4.5 %collective-permute-start.30 = (f32[8,256]{1,0:T(8,128)S(1)}, f32[8,256]{1,0:T(8,128)S(1)}, u32[]{:S(2)}, u32[]{:S(2)}) collective-permute-start(f32[8,256]{1,0:T(8,128)S(1)} %shard_map.102.q0), channel_id=1, source_target_pairs={{0,8},{8,16},{16,24},{24,0},{1,9},{9,17},{17,25},{25,1},{2,10},{10... | collective-permute-start | bytes 24584 | tf_op jit(solution)/shard_map/ppermute | solution.py:464
  99.8 4.0 %collective-permute-start.31 = (f32[8,256]{1,0:T(8,128)S(1)}, f32[8,256]{1,0:T(8,128)S(1)}, u32[]{:S(2)}, u32[]{:S(2)}) collective-permute-start(f32[8,256]{1,0:T(8,128)S(1)} %shard_map.102.q0), channel_id=1, source_target_pairs={{0,16},{8,24},{16,0},{24,8},{1,17},{9,25},{17,1},{25,9},{2,18},{10... | collective-permute-start | bytes 24584 | tf_op jit(solution)/shard_map/ppermute | solution.py:464
  102.3 2.8 %collective-permute-start.32 = (f32[8,256]{1,0:T(8,128)S(1)}, f32[8,256]{1,0:T(8,128)S(1)}, u32[]{:S(2)}, u32[]{:S(2)}) collective-permute-start(f32[8,256]{1,0:T(8,128)S(1)} %shard_map.102.q0), channel_id=1, source_target_pairs={{0,24},{8,0},{16,8},{24,16},{1,25},{9,1},{17,9},{25,17},{2,26},{10... | collective-permute-start | bytes 24584 | tf_op jit(solution)/shard_map/ppermute | solution.py:464
  106.3 4.8 %collective-permute-start.33 = (f32[8,256]{1,0:T(8,128)S(1)}, f32[8,256]{1,0:T(8,128)S(1)}, u32[]{:S(2)}, u32[]{:S(2)}) collective-permute-start(f32[8,256]{1,0:T(8,128)S(1)} %get-tuple-element.69.gy0), channel_id=1, source_target_pairs={{0,32},{32,64},{64,96},{96,0},{1,33},{33,65},{65,97},{97,1},{2,34}... | collective-permute-start | bytes 24584 | tf_op jit(solution)/shard_map/ppermute | solution.py:464
  107.6 4.0 %collective-permute-start.34 = (f32[8,256]{1,0:T(8,128)S(1)}, f32[8,256]{1,0:T(8,128)S(1)}, u32[]{:S(2)}, u32[]{:S(2)}) collective-permute-start(f32[8,256]{1,0:T(8,128)S(1)} %get-tuple-element.69.gy0), channel_id=1, source_target_pairs={{0,64},{32,96},{64,0},{96,32},{1,65},{33,97},{65,1},{97,33},{2,66}... | collective-permute-start | bytes 24584 | tf_op jit(solution)/shard_map/ppermute | solution.py:464
  110.0 2.6 %collective-permute-start.35 = (f32[8,256]{1,0:T(8,128)S(1)}, f32[8,256]{1,0:T(8,128)S(1)}, u32[]{:S(2)}, u32[]{:S(2)}) collective-permute-start(f32[8,256]{1,0:T(8,128)S(1)} %get-tuple-element.69.gy0), channel_id=1, source_target_pairs={{0,96},{32,0},{64,32},{96,64},{1,97},{33,1},{65,33},{97,65},{2,98}... | collective-permute-start | bytes 24584 | tf_op jit(solution)/shard_map/ppermute | solution.py:464
  112.6 5.8 %copy-start.1 = (bf16[512,1024]{1,0:T(8,128)(2,1)S(1)}, bf16[512,1024]{1,0:T(8,128)(2,1)}, u32[]{:S(2)}) copy-start(bf16[512,1024]{1,0:T(8,128)(2,1)} %observed.5) | copy-start | bytes 3145732
  118.4 12.2 %copy-start.3 = (bf16[1024,256]{1,0:T(8,128)(2,1)S(1)}, bf16[1024,256]{1,0:T(8,128)(2,1)}, u32[]{:S(2)}) copy-start(bf16[1024,256]{1,0:T(8,128)(2,1)} %loads.5) | copy-start | bytes 1572868
  118.4 12.4 %copy-start.7 = (s32[8]{0:T(128)S(1)}, s32[8]{0:T(128)}, u32[]{:S(2)}) copy-start(s32[8]{0:T(128)} %panel_of.1) | copy-start | bytes 100
  119.8 5.0 %collective-permute-start.36 = (f32[16,64,128]{2,1,0:T(8,128)S(1)}, f32[16,64,128]{2,1,0:T(8,128)S(1)}, u32[]{:S(2)}, u32[]{:S(2)}) collective-permute-start(f32[16,64,128]{2,1,0:T(8,128)S(1)} %get-tuple-element.79), channel_id=1, source_target_pairs={{0,4},{4,0},{1,5},{5,1},{2,6},{6,2},{3,7},{7,3},{8,12},{12,8},{9,1... | collective-permute-start | bytes 1572872 | tf_op jit(solution)/shard_map/ppermute | solution.py:473
  125.7 32.9 %all-to-all-start = ((f32[16,64,128]{2,1,0:T(8,128)}), f32[16,64,128]{2,1,0:T(8,128)S(1)}, u32[]{:S(2)}, u32[]{:S(2)}) async-start(f32[16,64,128]{2,1,0:T(8,128)} %shard_map.106), calls=%async_computation | async-start | bytes 1048576 | tf_op jit(solution)/shard_map/all_to_all | solution.py:557
  129.9 3.6 %collective-permute-start.37 = (f32[136,128]{1,0:T(8,128)S(1)}, f32[136,128]{1,0:T(8,128)S(1)}, u32[]{:S(2)}, u32[]{:S(2)}) collective-permute-start(f32[136,128]{1,0:T(8,128)S(1)} %get-tuple-element.81), channel_id=1, source_target_pairs={{0,4},{4,0},{1,5},{5,1},{2,6},{6,2},{3,7},{7,3},{8,12},{12,8},{9,1... | collective-permute-start | bytes 208904 | tf_op jit(solution)/shard_map/ppermute | solution.py:473
  132.2 1.2 collective-permute-start.38
  133.5 7.0 %collective-permute-start.39 = (f32[144,128]{1,0:T(8,128)S(1)}, f32[144,128]{1,0:T(8,128)S(1)}, u32[]{:S(2)}, u32[]{:S(2)}) collective-permute-start(f32[144,128]{1,0:T(8,128)S(1)} %shard_map.110.a), channel_id=1, source_target_pairs={{0,8},{8,16},{16,24},{24,0},{1,9},{9,17},{17,25},{25,1},{2,10},{10... | collective-permute-start | bytes 221192 | tf_op jit(solution)/shard_map/ppermute | solution.py:464
  135.1 6.5 %collective-permute-start.40 = (f32[144,128]{1,0:T(8,128)S(1)}, f32[144,128]{1,0:T(8,128)S(1)}, u32[]{:S(2)}, u32[]{:S(2)}) collective-permute-start(f32[144,128]{1,0:T(8,128)S(1)} %shard_map.110.a), channel_id=1, source_target_pairs={{0,16},{8,24},{16,0},{24,8},{1,17},{9,25},{17,1},{25,9},{2,18},{10... | collective-permute-start | bytes 221192 | tf_op jit(solution)/shard_map/ppermute | solution.py:464
  137.5 4.2 %collective-permute-start.41 = (f32[144,128]{1,0:T(8,128)S(1)}, f32[144,128]{1,0:T(8,128)S(1)}, u32[]{:S(2)}, u32[]{:S(2)}) collective-permute-start(f32[144,128]{1,0:T(8,128)S(1)} %shard_map.110.a), channel_id=1, source_target_pairs={{0,24},{8,0},{16,8},{24,16},{1,25},{9,1},{17,9},{25,17},{2,26},{10... | collective-permute-start | bytes 221192 | tf_op jit(solution)/shard_map/ppermute | solution.py:464
  141.7 4.8 %collective-permute-start.42 = (f32[144,128]{1,0:T(8,128)S(1)}, f32[144,128]{1,0:T(8,128)S(1)}, u32[]{:S(2)}, u32[]{:S(2)}) collective-permute-start(f32[144,128]{1,0:T(8,128)S(1)} %shard_map.111.a), channel_id=1, source_target_pairs={{0,32},{32,64},{64,96},{96,0},{1,33},{33,65},{65,97},{97,1},{2,34}... | collective-permute-start | bytes 221192 | tf_op jit(solution)/shard_map/ppermute | solution.py:464
  142.9 5.0 %collective-permute-start.43 = (f32[144,128]{1,0:T(8,128)S(1)}, f32[144,128]{1,0:T(8,128)S(1)}, u32[]{:S(2)}, u32[]{:S(2)}) collective-permute-start(f32[144,128]{1,0:T(8,128)S(1)} %shard_map.111.a), channel_id=1, source_target_pairs={{0,64},{32,96},{64,0},{96,32},{1,65},{33,97},{65,1},{97,33},{2,66}... | collective-permute-start | bytes 221192 | tf_op jit(solution)/shard_map/ppermute | solution.py:464
  145.3 3.6 %collective-permute-start.44 = (f32[144,128]{1,0:T(8,128)S(1)}, f32[144,128]{1,0:T(8,128)S(1)}, u32[]{:S(2)}, u32[]{:S(2)}) collective-permute-start(f32[144,128]{1,0:T(8,128)S(1)} %shard_map.111.a), channel_id=1, source_target_pairs={{0,96},{32,0},{64,32},{96,64},{1,97},{33,1},{65,33},{97,65},{2,98}... | collective-permute-start | bytes 221192 | tf_op jit(solution)/shard_map/ppermute | solution.py:464
  148.9 7.4 %collective-permute-start.46 = (f32[8,128]{1,0:T(8,128)S(1)}, f32[8,128]{1,0:T(8,128)S(1)}, u32[]{:S(2)}, u32[]{:S(2)}) collective-permute-start(f32[8,128]{1,0:T(8,128)S(1)} %get-tuple-element.83.s0), channel_id=1, source_target_pairs={{0,1},{1,2},{2,3},{3,0},{4,5},{5,6},{6,7},{7,4},{8,9},{9,10},{10,1... | collective-permute-start | bytes 12296 | tf_op jit(solution)/shard_map/ppermute | solution.py:464
  149.6 6.6 %collective-permute-start.47 = (f32[8,128]{1,0:T(8,128)S(1)}, f32[8,128]{1,0:T(8,128)S(1)}, u32[]{:S(2)}, u32[]{:S(2)}) collective-permute-start(f32[8,128]{1,0:T(8,128)S(1)} %get-tuple-element.83.s0), channel_id=1, source_target_pairs={{0,2},{1,3},{2,0},{3,1},{4,6},{5,7},{6,4},{7,5},{8,10},{9,11},{10,... | collective-permute-start | bytes 12296 | tf_op jit(solution)/shard_map/ppermute | solution.py:464
  152.5 3.8 %collective-permute-start.48 = (f32[8,128]{1,0:T(8,128)S(1)}, f32[8,128]{1,0:T(8,128)S(1)}, u32[]{:S(2)}, u32[]{:S(2)}) collective-permute-start(f32[8,128]{1,0:T(8,128)S(1)} %get-tuple-element.83.s0), channel_id=1, source_target_pairs={{0,3},{1,0},{2,1},{3,2},{4,7},{5,4},{6,5},{7,6},{8,11},{9,8},{10,9... | collective-permute-start | bytes 12296 | tf_op jit(solution)/shard_map/ppermute | solution.py:464
  152.5 4.7 %collective-permute-start.45 = (f32[136,128]{1,0:T(8,128)S(1)}, f32[136,128]{1,0:T(8,128)S(1)}, u32[]{:S(2)}, u32[]{:S(2)}) collective-permute-start(f32[136,128]{1,0:T(8,128)S(1)} %get-tuple-element.82.mine), channel_id=1, source_target_pairs={{0,4},{4,0},{1,5},{5,1},{2,6},{6,2},{3,7},{7,3},{8,12},{12,8},{9,1... | collective-permute-start | bytes 208904 | tf_op jit(solution)/shard_map/ppermute | solution.py:473

commit v2 on v1

--- a/solution.py
+++ b/solution.py
@@ -31,6 +31,10 @@
 
 
 def dot3(a, b, dims=((1,), (0,))):
+    rows = a[0].shape[0]
+    if dims[0] == (1,):
+        both = dot(jnp.concatenate(a, axis=0), b[0], dims)
+        return (both[:rows] + both[rows:]) + dot(a[0], b[1], dims)
     return dot(a[0], b[0], dims) + (dot(a[0], b[1], dims) + dot(a[1], b[0], dims))
 
 
@@ -71,25 +75,26 @@
     )
 
 
-def gram_kernel(place, present, noise, loads, *outs):
+def gram_kernel(place, present, both, loads, table, *outs):
     coef = loads[...]
-    flipped = coef.astype(F32).T
-    inv_noise = 1.0 / noise[...]
+    series, n = coef.shape
+    mask = present[...].astype(F32)
+    inv_noise = 1.0 / both[:, 0:series]
+    table[0:4, :] = mask
+    table[4:5, 0:n] = both[:, series:]
+    table[8:12, :] = mask * inv_noise
+    high, low = split(coef.T.astype(F32) * inv_noise)
     for k, out in enumerate(outs):
-        b = lax.rem(place[3] + k, len(outs))
-        hi, lo = split(flipped * (present[pl.ds(b, 1), :].astype(F32) * inv_noise))
-        store_packed(out, dot(hi, coef) + dot(lo, coef))
-
-
-def project_kernel(place, present, noise, loads, decay, observed, table, *outs):
+        kept = table[pl.ds(lax.rem(place[3] + k, len(outs)), 1), :].astype(BF16)
+        store_packed(out, dot(high * kept, coef) + dot(low * kept, coef))
+
+
+def project_kernel(place, table, loads, observed, *outs):
     coef = loads[...]
-    inv_noise = 1.0 / noise[...]
-    table[0:4, :] = present[...].astype(F32)
-    table[4:5, 0 : decay.shape[1]] = decay[...]
     for k in range(len(outs)):
         b = lax.rem(place[3] + k, len(outs))
         rows = observed[pl.ds(pl.multiple_of(b * BLOCK, BLOCK), BLOCK), :].astype(F32)
-        hi, lo = split(rows * (present[pl.ds(b, 1), :].astype(F32) * inv_noise))
+        hi, lo = split(rows * table[pl.ds(8 + b, 1), :])
         outs[k][...] = dot(hi, coef) + dot(lo, coef)
 
 
@@ -128,8 +133,8 @@
         return err * err
 
     err = lax.while_loop(lambda e: (e > 1e-4) & (top < 8.0), quick, start * start)
-    lax.while_loop(lambda e: e > 1e-4, body, err)
-    inverse = improve(guess[...])
+    lax.while_loop(lambda e: e > 0.99e-8, body, err)
+    inverse = guess[...]
     gain = jnp.dot(gram, inverse, precision=HIGH, preferred_element_type=F32)
     gain = 0.5 * (gain + gain.T)
     rho = 1.0 - decay_of(table, n)
@@ -264,8 +269,74 @@
             values[b] = v + shifted(v - dot3(split(v), pair), 1 << level, ahead)
 
 
-def forward_kernel(place, table, own, m1, m2, m3, o1, o2, o3, xs, other, v_other, p0, p1, p2, p3,
-                   ends, his, los, tops,
+def prefix_kernel(place, xs, other, v_other, tops, ends, starts, rests):
+    nb = 4
+    n = other.shape[1]
+
+    def after(total, end, err, v):
+        pair = split(err)
+        return total + err - dot3(split(total), pair), end - dot3(split(end), pair) + v
+
+    starts[0] = jnp.zeros((n + 8, n), F32)
+
+    def into(k, carry):
+        starts[0, 0:n, :], starts[0, n:, :] = after(
+            starts[0, 0:n, :], starts[0, n:, :], xs[k, 0:n, :], xs[k, n:, :]
+        )
+        return carry
+
+    lax.fori_loop(0, place[1], into, 0)
+
+    @pl.when(place[2] == 1)
+    def _():
+        starts[0, 0:n, :], starts[0, n:, :] = after(
+            starts[0, 0:n, :], starts[0, n:, :], other[...], v_other[...]
+        )
+
+    def before(err, total):
+        return total + err - dot3(split(err), split(total))
+
+    rests[nb - 1] = jnp.zeros((n, n), F32)
+
+    def back(k, carry):
+        rests[nb - 1] = before(xs[3 - k, 0:n, :], rests[nb - 1])
+        return carry
+
+    lax.fori_loop(0, 3 - place[1], back, 0)
+
+    @pl.when(place[2] == 0)
+    def _():
+        rests[nb - 1] = before(other[...], rests[nb - 1])
+
+    def blocks(b, carry):
+        starts[b + 1, 0:n, :], starts[b + 1, n:, :] = after(
+            starts[b, 0:n, :], starts[b, n:, :], tops[b], ends[b]
+        )
+        late = nb - 1 - b
+        rests[late - 1] = before(tops[late], rests[late])
+        return carry
+
+    lax.fori_loop(0, nb - 1, blocks, 0)
+
+
+def suffix_kernel(place, qs, xs, far, other, tops, firsts, offsets):
+    nb = 4
+    n = other.shape[1]
+
+    def over(k, s):
+        j = 3 - k
+        return qs[j] + retreat(s, xs[j, 0:n, :])
+
+    back = lax.fori_loop(0, 3 - place[1], over, jnp.zeros((8, n), F32))
+    back = jnp.where(place[2] == 0, far[...] + retreat(back, other[...]), back)
+    for b in reversed(range(nb)):
+        offsets[b] = back
+        if b:
+            back = back - dot3(split(back), split(tops[b])) + firsts[b]
+
+
+def forward_kernel(place, table, own, m1, m2, m3, o1, o2, o3, starts, p0, p1, p2, p3,
+                   his, los, tops,
                    past, change, firsts, first, ys, values, states):
     nb = 4
     n = own.shape[1]
@@ -275,14 +346,9 @@
     ordered_maps(place[0], place[2], own, ((m1, o1), (m2, o2), (m3, o3)), ys)
     state = jnp.zeros((8, n), F32)
     state = lax.fori_loop(0, place[0], lambda k, s: advance(s, ys[k]), state)
-    state = lax.fori_loop(0, place[1], lambda k, s: advance(s, xs[k]), state)
-    over = state - dot3(split(state), split(other[...])) + v_other[...]
-    state = jnp.where(place[2] == 0, state, over)
     at = lax.broadcasted_iota(jnp.int32, (BLOCK, n), 0)
     for b in range(nb):
-        states[b] = state
-        if b + 1 < nb:
-            state = state - dot3(split(state), split(tops[b])) + ends[b]
+        states[b] = advance(state, starts[b])
     for b in range(nb):
         z = values[b] * root_inv
         z = z + jnp.where(at == 0, states[b][0:1], 0.0)
@@ -320,32 +386,23 @@
     out[...] = q
 
 
-def smooth_kernel(place, table, gy0, gy1, gy2, gy3, gxs, far, ys, xs, other,
-                  past, change, firsts, his, los, tops,
-                  smoothed, high, low, keep, give, gys, values, states, moment):
+def smooth_kernel(place, table, gy0, gy1, gy2, gy3, ys, rests, offsets,
+                  past, change, his, los,
+                  smoothed, high, low, keep, give, gys, values, moment):
     nb = 4
     nseg = 4
     ordered(place[0], (gy0, gy1, gy2, gy3), gys)
     n = gy0.shape[1]
     back = jnp.zeros((8, n), F32)
 
-    def over(gs, ms):
-        def step(k, s):
-            j = nseg - 1 - k
-            return gs[j] + retreat(s, ms[j, 0:n, :])
-
-        return step
-
-    back = lax.fori_loop(0, nseg - 1 - place[0], over(gys, ys), back)
-    back = lax.fori_loop(0, nseg - 1 - place[1], over(gxs, xs), back)
-    back = jnp.where(place[2] == 0, far[...] + retreat(back, other[...]), back)
+    def over(k, s):
+        j = nseg - 1 - k
+        return gys[j] + retreat(s, ys[j, 0:n, :])
+
+    back = lax.fori_loop(0, nseg - 1 - place[0], over, back)
     at = lax.broadcasted_iota(jnp.int32, (BLOCK, n), 0)
-    for b in reversed(range(nb)):
-        states[b] = back
-        if b:
-            back = back - dot3(split(back), split(tops[b])) + firsts[b]
     for b in range(nb):
-        s = states[b]
+        s = offsets[b] + retreat(back, rests[b])
         step = s - dot3(split(s), (his[b], los[b]))
         values[b] = change[b] + jnp.where(at == BLOCK - 1, step[0:1], 0.0)
     scan_rows(values, his, los, nb, False)
@@ -494,12 +551,11 @@
     squares4 = ((nb, width, width), F32)
     powers = ((LEVELS * nb, width, width), BF16)
 
-    noise = noise_var.reshape(1, series)
-    grams = call(gram_kernel, [packed] * nb, [], place, present, noise, loadings)
-    table, *projs = call(
-        project_kernel, [((8, series), F32)] + [rows2] * nb, [],
-        place, present, noise, loadings, decay_rate.reshape(1, width), observed,
-    )
+    both = jnp.concatenate([noise_var, decay_rate]).reshape(1, series + width)
+    table, *grams = call(
+        gram_kernel, [((16, series), F32)] + [packed] * nb, [], place, present, both, loadings
+    )
+    projs = call(project_kernel, [rows2] * nb, [], place, table, loadings, observed)
     grams = from_peers(grams, "panel")
     projs = from_peers(projs, "panel")
     (err,) = call(inverse_kernel, [packed], [square], table, *grams, smem=0)
@@ -522,12 +578,15 @@
         place, pair, *near, *[swap(m, ac) for m in near],
     )
     near = gather(group_half, ay)[1:]
+    starts, rests = call(
+        prefix_kernel, [maps4, squares4], [], place, xs, seg_far, end_far, tops, ends
+    )
     past, change, firsts, first, ys = call(
         forward_kernel,
         [rows3, rows3, vecs4, vec, maps4],
         [rows3, vecs4],
         place, table, group, *near, *[swap(m, ac) for m in near],
-        xs, seg_far, end_far, *projs, ends, his, los, tops,
+        starts, *projs, his, los, tops,
     )
     first_far = swap(first, ac)
     (pair_first,) = call(pair_back_kernel, [vec], [], place, first, first_far, seg, seg_far)
@@ -536,12 +595,13 @@
     )
     flat = ((time_rows, width), BF16)
     piece = ((BLOCK + 8, half), F32)
+    firsts_y = gather(group_first, ay)
+    (offsets,) = call(suffix_kernel, [vecs4], [], place, gxs, xs, first_far, seg_far, tops, firsts)
     smoothed, high, low, keep, give = call(
         smooth_kernel,
         [((time_rows, width), F32), flat, flat, piece, piece],
-        [vecs4, rows3, vecs4, packed],
-        place, table, *gather(group_first, ay), gxs, first_far, ys, xs, seg_far,
-        past, change, firsts, his, los, tops,
+        [vecs4, rows3, packed],
+        place, table, *firsts_y, ys, rests, offsets, past, change, his, los,
     )
     given = swap(give, ac)
     line = ((8, half), F32)

time: 161 us -> 160 us (level)
  waiting for transfers between devices: 38.5 us -> 34 us
  Pallas kernels: 38.1 us -> 40.2 us
    ppermute x36, waiting for transfers between devices: 32.4 us -> 28 us  [from_peers(): lax.ppermute(arrays[k], axis, [(i, (i + k) % n) for i in range(n)])]
    pallas_call x22 -> x24, Pallas kernels: 38.1 us -> 40.2 us  [call(): return made(*args)]
    unnamed x16 -> x14, local copies, waits for them, and re-layouts: 4.36 us -> 4.04 us
  transfers between devices with their start and end apart: 50 -> 50, of which waited for: 26 -> 24; matrix products, arithmetic and copies ran while one was open for 0% -> 0% of each run, Pallas kernels for 7% -> 10%
where the time goes in v2:
time: 160 us; the launch traced here: 157 us
  starting transfers between devices  76.9 us (48%)
  Pallas kernels  40.2 us (25%)
  waiting for transfers between devices  34 us (21%)
  local copies, waits for them, and re-layouts  4.56 us (3%)
    ppermute x36, starting transfers between devices, from_peers(): lax.ppermute(arrays[k], axis, [(i, (i + k) % n) for i in range(n)])  53.4 us
    pallas_call x24, Pallas kernels, call(): return made(*args)  40.2 us
    ppermute x36, waiting for transfers between devices, from_peers(): lax.ppermute(arrays[k], axis, [(i, (i + k) % n) for i in range(n)])  28 us
    ppermute x13, starting transfers between devices, swap(): return lax.ppermute(array, axis, [(0, 1), (1, 0)])  18 us
    ppermute x13, waiting for transfers between devices, swap(): return lax.ppermute(array, axis, [(0, 1), (1, 0)])  6.07 us
    all_to_all x1, starting transfers between devices, step(): arrived = lax.all_to_all(spread, (ay, ax), 0, 0, tiled=True)  5.43 us
    unnamed x14, local copies, waits for them, and re-layouts  4.04 us
  transfers between devices with their start and end apart: 50, of which 24 were waited for; matrix products, arithmetic and copies ran while one was open for 0% of the time, Pallas kernels for 10%

profile of v2, /device:TPU:1, one launch (start us, length us, event | category | flops | bytes accessed | tf_op | source)
XLA Modules:
  0.0 157.4 jit_solution(16721692067436642003)
XLA Ops:
  3.2 1.8 %shard_map.93 = (f32[16,1024]{1,0:T(8,128)S(1)}, f32[264,128]{1,0:T(8,128)S(1)}, f32[264,128]{1,0:T(8,128)S(1)}, f32[264,128]{1,0:T(8,128)S(1)}, f32[264,128]{1,0:T(8,128)S(1)}) custom-call(s32[4]{0:T(128)S(1)} %pad_add_fusion.place, s32[4,1024]{1,0:T(4,128)S(1)} %copy-done.5, f32[1,1280]{1,0:T(1,128)S(1)} %reshape.11.both, bf16[1024,256]{1,0:T(8,128)(2,1)S(1)} %copy-done.2), custom_call_target="tpu_custom_call" | custom-call | tf_op jit(solution)/shard_map/pallas_call | solution.py:514
  5.0 2.5 %collective-permute-start = (f32[264,128]{1,0:T(8,128)S(1)}, f32[264,128]{1,0:T(8,128)S(1)}, u32[]{:S(2)}, u32[]{:S(2)}) collective-permute-start(f32[264,128]{1,0:T(8,128)S(1)} %get-tuple-element.48), channel_id=1, source_target_pairs={{0,1},{1,2},{2,3},{3,0},{4,5},{5,6},{6,7},{7,4},{8,9},{9,10},{10,1... | collective-permute-start | bytes 405512 | tf_op jit(solution)/shard_map/ppermute | solution.py:521
  7.6 3.3 %collective-permute-start.1 = (f32[264,128]{1,0:T(8,128)S(1)}, f32[264,128]{1,0:T(8,128)S(1)}, u32[]{:S(2)}, u32[]{:S(2)}) collective-permute-start(f32[264,128]{1,0:T(8,128)S(1)} %get-tuple-element.49), channel_id=1, source_target_pairs={{0,2},{1,3},{2,0},{3,1},{4,6},{5,7},{6,4},{7,5},{8,10},{9,11},{10,... | collective-permute-start | bytes 405512 | tf_op jit(solution)/shard_map/ppermute | solution.py:521
  11.6 1.2 copy-done
  13.9 1.3 shard_map.96
  16.8 3.3 %shard_map.94.e0.packed = f32[264,128]{1,0:T(8,128)S(1)} custom-call(f32[16,1024]{1,0:T(8,128)S(1)} %get-tuple-element.46.table, f32[264,128]{1,0:T(8,128)S(1)} %get-tuple-element.47.g0, f32[264,128]{1,0:T(8,128)S(1)} %collective-permute-done.g1, f32[264,128]{1,0:T(8,128)S(1)} %collective-permute-done.1.g2, f32[264,128]{1,0:T(8,128)S(1)} %collective-permute-done.2.g3), custom_call_target="tpu_custom_call" | custom-call | tf_op jit(solution)/shard_map/pallas_call | solution.py:514
  20.1 1.7 %collective-permute-start.3 = (f32[264,128]{1,0:T(8,128)S(1)}, f32[264,128]{1,0:T(8,128)S(1)}, u32[]{:S(2)}, u32[]{:S(2)}) collective-permute-start(f32[264,128]{1,0:T(8,128)S(1)} %shard_map.94.e0.packed), channel_id=1, source_target_pairs={{0,1},{1,2},{2,3},{3,0},{4,5},{5,6},{6,7},{7,4},{8,9},{9,10},{10,1... | collective-permute-start | bytes 405512 | tf_op jit(solution)/shard_map/ppermute | solution.py:521
  21.8 1.9 %collective-permute-start.4 = (f32[264,128]{1,0:T(8,128)S(1)}, f32[264,128]{1,0:T(8,128)S(1)}, u32[]{:S(2)}, u32[]{:S(2)}) collective-permute-start(f32[264,128]{1,0:T(8,128)S(1)} %shard_map.94.e0.packed), channel_id=1, source_target_pairs={{0,2},{1,3},{2,0},{3,1},{4,6},{5,7},{6,4},{7,5},{8,10},{9,11},{10,... | collective-permute-start | bytes 405512 | tf_op jit(solution)/shard_map/ppermute | solution.py:521
  25.2 2.4 %collective-permute-start.8 = (f32[128,256]{1,0:T(8,128)S(1)}, f32[128,256]{1,0:T(8,128)S(1)}, u32[]{:S(2)}, u32[]{:S(2)}) collective-permute-start(f32[128,256]{1,0:T(8,128)S(1)} %get-tuple-element.55), channel_id=1, source_target_pairs={{0,3},{1,0},{2,1},{3,2},{4,7},{5,4},{6,5},{7,6},{8,11},{9,8},{10,9... | collective-permute-start | bytes 393224 | tf_op jit(solution)/shard_map/ppermute | solution.py:521
  27.6 4.5 %collective-permute-done.7.p2 = f32[128,256]{1,0:T(8,128)S(1)} collective-permute-done((f32[128,256]{1,0:T(8,128)S(1)}, f32[128,256]{1,0:T(8,128)S(1)}, u32[]{:S(2)}, u32[]{:S(2)}) %collective-permute-start.7) | collective-permute-done | bytes 131104 | tf_op jit(solution)/shard_map/ppermute | solution.py:521
  32.1 1.8 %collective-permute-done.8.p3 = f32[128,256]{1,0:T(8,128)S(1)} collective-permute-done((f32[128,256]{1,0:T(8,128)S(1)}, f32[128,256]{1,0:T(8,128)S(1)}, u32[]{:S(2)}, u32[]{:S(2)}) %collective-permute-start.8) | collective-permute-done | bytes 131104 | tf_op jit(solution)/shard_map/ppermute | solution.py:521
  33.9 2.9 %shard_map.97 = (f32[128,256]{1,0:T(8,128)S(1)}, f32[8,256]{1,0:T(8,128)S(1)}) custom-call(f32[16,1024]{1,0:T(8,128)S(1)} %get-tuple-element.46.table, f32[264,128]{1,0:T(8,128)S(1)} %shard_map.94.e0.packed, f32[128,256]{1,0:T(8,128)S(1)} %get-tuple-element.52.p0, f32[128,256]{1,0:T(8,128)S(1)} %collective-permute-done.6.p1, ...), custom_call_target="tpu_custom_call" | custom-call | tf_op jit(solution)/shard_map/pallas_call | solution.py:514
  36.9 5.8 %shard_map.95 = (bf16[28,256,256]{2,1,0:T(8,128)(2,1)S(1)}, bf16[28,256,256]{2,1,0:T(8,128)(2,1)S(1)}, f32[4,256,256]{2,1,0:T(8,128)S(1)}, f32[256,256]{1,0:T(8,128)S(1)}) custom-call(s32[4]{0:T(128)S(1)} %pad_add_fusion.place, f32[264,128]{1,0:T(8,128)S(1)} %shard_map.94.e0.packed, f32[264,128]{1,0:T(8,128)S(1)} %collective-permute-done.3.e1, ...), custom_call_target="tpu_custom_call" | custom-call | tf_op jit(solution)/shard_map/pallas_call | solution.py:514
  42.7 3.0 %collective-permute-start.9 = (f32[256,256]{1,0:T(8,128)S(1)}, f32[256,256]{1,0:T(8,128)S(1)}, u32[]{:S(2)}, u32[]{:S(2)}) collective-permute-start(f32[256,256]{1,0:T(8,128)S(1)} %get-tuple-element.57.mine), channel_id=1, source_target_pairs={{0,4},{4,0},{1,5},{5,1},{2,6},{6,2},{3,7},{7,3},{8,12},{12,8},{9,1... | collective-permute-start | bytes 786440 | tf_op jit(solution)/shard_map/ppermute | solution.py:530
  45.7 1.1 collective-permute-start.10
  46.8 2.3 %collective-permute-start.11 = (f32[8,256]{1,0:T(8,128)S(1)}, f32[8,256]{1,0:T(8,128)S(1)}, u32[]{:S(2)}, u32[]{:S(2)}) collective-permute-start(f32[8,256]{1,0:T(8,128)S(1)} %get-tuple-element.59.v0), channel_id=1, source_target_pairs={{0,2},{1,3},{2,0},{3,1},{4,6},{5,7},{6,4},{7,5},{8,10},{9,11},{10,... | collective-permute-start | bytes 24584 | tf_op jit(solution)/shard_map/ppermute | solution.py:521
  49.5 1.3 collective-permute-done.11.v2
  50.8 1.1 collective-permute-done.12.v3
  52.8 1.6 %collective-permute-start.13 = (f32[8,256]{1,0:T(8,128)S(1)}, f32[8,256]{1,0:T(8,128)S(1)}, u32[]{:S(2)}, u32[]{:S(2)}) collective-permute-start(f32[8,256]{1,0:T(8,128)S(1)} %get-tuple-element.60.v_mine), channel_id=1, source_target_pairs={{0,4},{4,0},{1,5},{5,1},{2,6},{6,2},{3,7},{7,3},{8,12},{12,8},{9,1... | collective-permute-start | bytes 24584 | tf_op jit(solution)/shard_map/ppermute | solution.py:530
  56.1 1.3 collective-permute-start.14
  57.4 2.5 %collective-permute-start.15 = (f32[136,256]{1,0:T(8,128)S(1)}, f32[136,256]{1,0:T(8,128)S(1)}, u32[]{:S(2)}, u32[]{:S(2)}) collective-permute-start(f32[136,256]{1,0:T(8,128)S(1)} %get-tuple-element.62), channel_id=1, source_target_pairs={{0,16},{8,24},{16,0},{24,8},{1,17},{9,25},{17,1},{25,9},{2,18},{10... | collective-permute-start | bytes 417800 | tf_op jit(solution)/shard_map/ppermute | solution.py:521
  59.8 1.2 collective-permute-start.16
  61.0 1.3 collective-permute-done.14.m1
  62.3 1.2 collective-permute-start.17
  63.5 2.8 %collective-permute-done.15.m2 = f32[136,256]{1,0:T(8,128)S(1)} collective-permute-done((f32[136,256]{1,0:T(8,128)S(1)}, f32[136,256]{1,0:T(8,128)S(1)}, u32[]{:S(2)}, u32[]{:S(2)}) %collective-permute-start.15) | collective-permute-done | bytes 139296 | tf_op jit(solution)/shard_map/ppermute | solution.py:521
  66.2 1.2 collective-permute-start.18
  68.8 1.5 shard_map.100
  70.3 1.4 collective-permute-start.20
  71.7 2.6 %collective-permute-start.21 = (f32[136,256]{1,0:T(8,128)S(1)}, f32[136,256]{1,0:T(8,128)S(1)}, u32[]{:S(2)}, u32[]{:S(2)}) collective-permute-start(f32[136,256]{1,0:T(8,128)S(1)} %get-tuple-element.64), channel_id=1, source_target_pairs={{0,64},{32,96},{64,0},{96,32},{1,65},{33,97},{65,1},{97,33},{2,66}... | collective-permute-start | bytes 417800 | tf_op jit(solution)/shard_map/ppermute | solution.py:521
  74.3 1.1 collective-permute-start.22
  75.4 1.4 collective-permute-done.20.m1
  77.7 3.1 %collective-permute-done.21.m2 = f32[136,256]{1,0:T(8,128)S(1)} collective-permute-done((f32[136,256]{1,0:T(8,128)S(1)}, f32[136,256]{1,0:T(8,128)S(1)}, u32[]{:S(2)}, u32[]{:S(2)}) %collective-permute-start.21) | collective-permute-done | bytes 139296 | tf_op jit(solution)/shard_map/ppermute | solution.py:521
  80.8 1.1 collective-permute-start.24
  81.9 1.2 collective-permute-start.27
  83.1 1.1 collective-permute-start.28
  84.2 3.0 %shard_map.101 = (f32[4,264,256]{2,1,0:T(8,128)S(1)}, f32[4,256,256]{2,1,0:T(8,128)S(1)}) custom-call(s32[4]{0:T(128)S(1)} %pad_add_fusion.place, f32[4,264,256]{2,1,0:T(8,128)S(1)} %get-tuple-element.65.xs, f32[256,256]{1,0:T(8,128)S(1)} %collective-permute-done.9.other, f32[8,256]{1,0:T(8,128)S(1)} %collective-permute-done.13.v_other, ...), custom_call_target="tpu_custom_call" | custom-call | tf_op jit(solution)/shard_map/pallas_call | solution.py:514
  87.9 2.1 %collective-permute-done.28.p3 = f32[128,256]{1,0:T(8,128)S(1)} collective-permute-done((f32[128,256]{1,0:T(8,128)S(1)}, f32[128,256]{1,0:T(8,128)S(1)}, u32[]{:S(2)}, u32[]{:S(2)}) %collective-permute-start.28) | collective-permute-done | bytes 131104 | tf_op jit(solution)/shard_map/ppermute | solution.py:521
  90.0 4.8 %shard_map.102 = (f32[4,128,256]{2,1,0:T(8,128)S(1)}, f32[4,128,256]{2,1,0:T(8,128)S(1)}, f32[4,8,256]{2,1,0:T(8,128)S(1)}, f32[8,256]{1,0:T(8,128)S(1)}, f32[4,264,256]{2,1,0:T(8,128)S(1)}) custom-call(s32[4]{0:T(128)S(1)} %pad_add_fusion.place, f32[16,1024]{1,0:T(8,128)S(1)} %get-tuple-element.46.table, f32[264,256]{1,0:T(8,128)S(1)} %get-tuple-element.63.own, ...), custom_call_target="tpu_custom_call" | custom-call | tf_op jit(solution)/shard_map/pallas_call | solution.py:514
  94.8 1.4 collective-permute-start.29
  98.6 2.1 %collective-permute-start.31 = (f32[8,256]{1,0:T(8,128)S(1)}, f32[8,256]{1,0:T(8,128)S(1)}, u32[]{:S(2)}, u32[]{:S(2)}) collective-permute-start(f32[8,256]{1,0:T(8,128)S(1)} %shard_map.103.q0), channel_id=1, source_target_pairs={{0,16},{8,24},{16,0},{24,8},{1,17},{9,25},{17,1},{25,9},{2,18},{10... | collective-permute-start | bytes 24584 | tf_op jit(solution)/shard_map/ppermute | solution.py:521
  100.7 1.2 collective-permute-start.32
  104.6 1.2 collective-permute-start.33
  105.8 2.4 %collective-permute-start.34 = (f32[8,256]{1,0:T(8,128)S(1)}, f32[8,256]{1,0:T(8,128)S(1)}, u32[]{:S(2)}, u32[]{:S(2)}) collective-permute-start(f32[8,256]{1,0:T(8,128)S(1)} %get-tuple-element.72.gy0), channel_id=1, source_target_pairs={{0,64},{32,96},{64,0},{96,32},{1,65},{33,97},{65,1},{97,33},{2,66}... | collective-permute-start | bytes 24584 | tf_op jit(solution)/shard_map/ppermute | solution.py:521
  108.2 1.2 collective-permute-start.35
  109.4 1.7 %shard_map.105.offsets = f32[4,8,256]{2,1,0:T(8,128)S(1)} custom-call(s32[4]{0:T(128)S(1)} %pad_add_fusion.place, f32[4,8,256]{2,1,0:T(8,128)S(1)} %get-tuple-element.75.qs, f32[4,264,256]{2,1,0:T(8,128)S(1)} %get-tuple-element.65.xs, f32[8,256]{1,0:T(8,128)S(1)} %collective-permute-done.29.far, f32[256,256]{1,0:T(8,128)S(1)} %collective-permute-done.9.other, ...), custom_call_target="tpu_custom_call" | custom-call | tf_op jit(solution)/shard_map/pallas_call | solution.py:514
  111.1 4.8 %shard_map.106 = (f32[512,256]{1,0:T(8,128)}, bf16[512,256]{1,0:T(8,128)(2,1)S(1)}, bf16[512,256]{1,0:T(8,128)(2,1)S(1)}, f32[136,128]{1,0:T(8,128)S(1)}, f32[136,128]{1,0:T(8,128)S(1)}) custom-call(s32[4]{0:T(128)S(1)} %pad_add_fusion.place, f32[16,1024]{1,0:T(8,128)S(1)} %get-tuple-element.46.table, f32[8,256]{1,0:T(8,128)S(1)} %get-tuple-element.72.gy0, ...), custom_call_target="tpu_custom_call" | custom-call | tf_op jit(solution)/shard_map/pallas_call | solution.py:514
  115.9 1.4 shard_map.107
  117.2 3.1 %collective-permute-start.36 = (f32[16,64,128]{2,1,0:T(8,128)S(1)}, f32[16,64,128]{2,1,0:T(8,128)S(1)}, u32[]{:S(2)}, u32[]{:S(2)}) collective-permute-start(f32[16,64,128]{2,1,0:T(8,128)S(1)} %get-tuple-element.83), channel_id=1, source_target_pairs={{0,4},{4,0},{1,5},{5,1},{2,6},{6,2},{3,7},{7,3},{8,12},{12,8},{9,1... | collective-permute-start | bytes 1572872 | tf_op jit(solution)/shard_map/ppermute | solution.py:530
  120.3 1.5 collective-permute-done.36.b
  122.7 5.4 %all-to-all-start = ((f32[16,64,128]{2,1,0:T(8,128)}), f32[16,64,128]{2,1,0:T(8,128)S(1)}, u32[]{:S(2)}, u32[]{:S(2)}) async-start(f32[16,64,128]{2,1,0:T(8,128)} %shard_map.108), calls=%async_computation | async-start | bytes 1048576 | tf_op jit(solution)/shard_map/all_to_all | solution.py:617
  129.1 1.4 shard_map.111.s
  130.6 1.1 collective-permute-done.38.s_far
  131.7 1.6 %collective-permute-start.39 = (f32[144,128]{1,0:T(8,128)S(1)}, f32[144,128]{1,0:T(8,128)S(1)}, u32[]{:S(2)}, u32[]{:S(2)}) collective-permute-start(f32[144,128]{1,0:T(8,128)S(1)} %shard_map.112.a), channel_id=1, source_target_pairs={{0,8},{8,16},{16,24},{24,0},{1,9},{9,17},{17,25},{25,1},{2,10},{10... | collective-permute-start | bytes 221192 | tf_op jit(solution)/shard_map/ppermute | solution.py:521
  133.4 2.4 %collective-permute-start.40 = (f32[144,128]{1,0:T(8,128)S(1)}, f32[144,128]{1,0:T(8,128)S(1)}, u32[]{:S(2)}, u32[]{:S(2)}) collective-permute-start(f32[144,128]{1,0:T(8,128)S(1)} %shard_map.112.a), channel_id=1, source_target_pairs={{0,16},{8,24},{16,0},{24,8},{1,17},{9,25},{17,1},{25,9},{2,18},{10... | collective-permute-start | bytes 221192 | tf_op jit(solution)/shard_map/ppermute | solution.py:521
  135.8 1.2 collective-permute-start.41
  137.0 1.8 %collective-permute-done.39.b = f32[144,128]{1,0:T(8,128)S(1)} collective-permute-done((f32[144,128]{1,0:T(8,128)S(1)}, f32[144,128]{1,0:T(8,128)S(1)}, u32[]{:S(2)}, u32[]{:S(2)}) %collective-permute-start.39) | collective-permute-done | bytes 73760 | tf_op jit(solution)/shard_map/ppermute | solution.py:521
  138.7 1.2 collective-permute-done.40.c
  139.9 1.3 collective-permute-start.42
  141.2 2.4 %collective-permute-start.43 = (f32[144,128]{1,0:T(8,128)S(1)}, f32[144,128]{1,0:T(8,128)S(1)}, u32[]{:S(2)}, u32[]{:S(2)}) collective-permute-start(f32[144,128]{1,0:T(8,128)S(1)} %shard_map.113.a), channel_id=1, source_target_pairs={{0,64},{32,96},{64,0},{96,32},{1,65},{33,97},{65,1},{97,33},{2,66}... | collective-permute-start | bytes 221192 | tf_op jit(solution)/shard_map/ppermute | solution.py:521
  143.6 1.2 collective-permute-start.44
  144.8 1.4 collective-permute-done.43.c
  147.8 3.0 %collective-permute-start.47 = (f32[8,128]{1,0:T(8,128)S(1)}, f32[8,128]{1,0:T(8,128)S(1)}, u32[]{:S(2)}, u32[]{:S(2)}) collective-permute-start(f32[8,128]{1,0:T(8,128)S(1)} %get-tuple-element.87.s0), channel_id=1, source_target_pairs={{0,2},{1,3},{2,0},{3,1},{4,6},{5,7},{6,4},{7,5},{8,10},{9,11},{10,... | collective-permute-start | bytes 12296 | tf_op jit(solution)/shard_map/ppermute | solution.py:521
  150.8 3.7 %collective-permute-start.45 = (f32[136,128]{1,0:T(8,128)S(1)}, f32[136,128]{1,0:T(8,128)S(1)}, u32[]{:S(2)}, u32[]{:S(2)}) collective-permute-start(f32[136,128]{1,0:T(8,128)S(1)} %get-tuple-element.86.mine), channel_id=1, source_target_pairs={{0,4},{4,0},{1,5},{5,1},{2,6},{6,2},{3,7},{7,3},{8,12},{12,8},{9,1... | collective-permute-start | bytes 208904 | tf_op jit(solution)/shard_map/ppermute | solution.py:530
  155.4 1.3 shard_map.115
  (78 shorter events, 23.8 us)
Async XLA Ops:
  1.4 1.0 copy-start.2
  2.5 0.7 copy-start.5
  5.0 10.9 %collective-permute-start = (f32[264,128]{1,0:T(8,128)S(1)}, f32[264,128]{1,0:T(8,128)S(1)}, u32[]{:S(2)}, u32[]{:S(2)}) collective-permute-start(f32[264,128]{1,0:T(8,128)S(1)} %get-tuple-element.48), channel_id=1, source_target_pairs={{0,1},{1,2},{2,3},{3,0},{4,5},{5,6},{6,7},{7,4},{8,9},{9,10},{10,1... | collective-permute-start | bytes 405512 | tf_op jit(solution)/shard_map/ppermute | solution.py:521
  7.6 9.2 %collective-permute-start.1 = (f32[264,128]{1,0:T(8,128)S(1)}, f32[264,128]{1,0:T(8,128)S(1)}, u32[]{:S(2)}, u32[]{:S(2)}) collective-permute-start(f32[264,128]{1,0:T(8,128)S(1)} %get-tuple-element.49), channel_id=1, source_target_pairs={{0,2},{1,3},{2,0},{3,1},{4,6},{5,7},{6,4},{7,5},{8,10},{9,11},{10,... | collective-permute-start | bytes 405512 | tf_op jit(solution)/shard_map/ppermute | solution.py:521
  10.9 5.9 %collective-permute-start.2 = (f32[264,128]{1,0:T(8,128)S(1)}, f32[264,128]{1,0:T(8,128)S(1)}, u32[]{:S(2)}, u32[]{:S(2)}) collective-permute-start(f32[264,128]{1,0:T(8,128)S(1)} %get-tuple-element.50), channel_id=1, source_target_pairs={{0,3},{1,0},{2,1},{3,2},{4,7},{5,4},{6,5},{7,6},{8,11},{9,8},{10,9... | collective-permute-start | bytes 405512 | tf_op jit(solution)/shard_map/ppermute | solution.py:521
  11.6 1.2 copy-start
  12.8 1.0 copy-start.3
  15.2 10.1 %collective-permute-start.6 = (f32[128,256]{1,0:T(8,128)S(1)}, f32[128,256]{1,0:T(8,128)S(1)}, u32[]{:S(2)}, u32[]{:S(2)}) collective-permute-start(f32[128,256]{1,0:T(8,128)S(1)} %get-tuple-element.53), channel_id=1, source_target_pairs={{0,1},{1,2},{2,3},{3,0},{4,5},{5,6},{6,7},{7,4},{8,9},{9,10},{10,1... | collective-permute-start | bytes 393224 | tf_op jit(solution)/shard_map/ppermute | solution.py:521
  20.1 16.7 %collective-permute-start.3 = (f32[264,128]{1,0:T(8,128)S(1)}, f32[264,128]{1,0:T(8,128)S(1)}, u32[]{:S(2)}, u32[]{:S(2)}) collective-permute-start(f32[264,128]{1,0:T(8,128)S(1)} %shard_map.94.e0.packed), channel_id=1, source_target_pairs={{0,1},{1,2},{2,3},{3,0},{4,5},{5,6},{6,7},{7,4},{8,9},{9,10},{10,1... | collective-permute-start | bytes 405512 | tf_op jit(solution)/shard_map/ppermute | solution.py:521
  21.8 15.0 %collective-permute-start.4 = (f32[264,128]{1,0:T(8,128)S(1)}, f32[264,128]{1,0:T(8,128)S(1)}, u32[]{:S(2)}, u32[]{:S(2)}) collective-permute-start(f32[264,128]{1,0:T(8,128)S(1)} %shard_map.94.e0.packed), channel_id=1, source_target_pairs={{0,2},{1,3},{2,0},{3,1},{4,6},{5,7},{6,4},{7,5},{8,10},{9,11},{10,... | collective-permute-start | bytes 405512 | tf_op jit(solution)/shard_map/ppermute | solution.py:521
  23.7 13.1 %collective-permute-start.5 = (f32[264,128]{1,0:T(8,128)S(1)}, f32[264,128]{1,0:T(8,128)S(1)}, u32[]{:S(2)}, u32[]{:S(2)}) collective-permute-start(f32[264,128]{1,0:T(8,128)S(1)} %shard_map.94.e0.packed), channel_id=1, source_target_pairs={{0,3},{1,0},{2,1},{3,2},{4,7},{5,4},{6,5},{7,6},{8,11},{9,8},{10,9... | collective-permute-start | bytes 405512 | tf_op jit(solution)/shard_map/ppermute | solution.py:521
  24.3 7.8 %collective-permute-start.7 = (f32[128,256]{1,0:T(8,128)S(1)}, f32[128,256]{1,0:T(8,128)S(1)}, u32[]{:S(2)}, u32[]{:S(2)}) collective-permute-start(f32[128,256]{1,0:T(8,128)S(1)} %get-tuple-element.54), channel_id=1, source_target_pairs={{0,2},{1,3},{2,0},{3,1},{4,6},{5,7},{6,4},{7,5},{8,10},{9,11},{10,... | collective-permute-start | bytes 393224 | tf_op jit(solution)/shard_map/ppermute | solution.py:521
  25.2 8.7 %collective-permute-start.8 = (f32[128,256]{1,0:T(8,128)S(1)}, f32[128,256]{1,0:T(8,128)S(1)}, u32[]{:S(2)}, u32[]{:S(2)}) collective-permute-start(f32[128,256]{1,0:T(8,128)S(1)} %get-tuple-element.55), channel_id=1, source_target_pairs={{0,3},{1,0},{2,1},{3,2},{4,7},{5,4},{6,5},{7,6},{8,11},{9,8},{10,9... | collective-permute-start | bytes 393224 | tf_op jit(solution)/shard_map/ppermute | solution.py:521
  42.7 12.5 %collective-permute-start.9 = (f32[256,256]{1,0:T(8,128)S(1)}, f32[256,256]{1,0:T(8,128)S(1)}, u32[]{:S(2)}, u32[]{:S(2)}) collective-permute-start(f32[256,256]{1,0:T(8,128)S(1)} %get-tuple-element.57.mine), channel_id=1, source_target_pairs={{0,4},{4,0},{1,5},{5,1},{2,6},{6,2},{3,7},{7,3},{8,12},{12,8},{9,1... | collective-permute-start | bytes 786440 | tf_op jit(solution)/shard_map/ppermute | solution.py:530
  45.7 3.8 %collective-permute-start.10 = (f32[8,256]{1,0:T(8,128)S(1)}, f32[8,256]{1,0:T(8,128)S(1)}, u32[]{:S(2)}, u32[]{:S(2)}) collective-permute-start(f32[8,256]{1,0:T(8,128)S(1)} %get-tuple-element.59.v0), channel_id=1, source_target_pairs={{0,1},{1,2},{2,3},{3,0},{4,5},{5,6},{6,7},{7,4},{8,9},{9,10},{10,1... | collective-permute-start | bytes 24584 | tf_op jit(solution)/shard_map/ppermute | solution.py:521
  46.8 4.0 %collective-permute-start.11 = (f32[8,256]{1,0:T(8,128)S(1)}, f32[8,256]{1,0:T(8,128)S(1)}, u32[]{:S(2)}, u32[]{:S(2)}) collective-permute-start(f32[8,256]{1,0:T(8,128)S(1)} %get-tuple-element.59.v0), channel_id=1, source_target_pairs={{0,2},{1,3},{2,0},{3,1},{4,6},{5,7},{6,4},{7,5},{8,10},{9,11},{10,... | collective-permute-start | bytes 24584 | tf_op jit(solution)/shard_map/ppermute | solution.py:521
  49.1 2.8 %collective-permute-start.12 = (f32[8,256]{1,0:T(8,128)S(1)}, f32[8,256]{1,0:T(8,128)S(1)}, u32[]{:S(2)}, u32[]{:S(2)}) collective-permute-start(f32[8,256]{1,0:T(8,128)S(1)} %get-tuple-element.59.v0), channel_id=1, source_target_pairs={{0,3},{1,0},{2,1},{3,2},{4,7},{5,4},{6,5},{7,6},{8,11},{9,8},{10,9... | collective-permute-start | bytes 24584 | tf_op jit(solution)/shard_map/ppermute | solution.py:521
  52.8 2.4 %collective-permute-start.13 = (f32[8,256]{1,0:T(8,128)S(1)}, f32[8,256]{1,0:T(8,128)S(1)}, u32[]{:S(2)}, u32[]{:S(2)}) collective-permute-start(f32[8,256]{1,0:T(8,128)S(1)} %get-tuple-element.60.v_mine), channel_id=1, source_target_pairs={{0,4},{4,0},{1,5},{5,1},{2,6},{6,2},{3,7},{7,3},{8,12},{12,8},{9,1... | collective-permute-start | bytes 24584 | tf_op jit(solution)/shard_map/ppermute | solution.py:530
  56.1 6.2 %collective-permute-start.14 = (f32[136,256]{1,0:T(8,128)S(1)}, f32[136,256]{1,0:T(8,128)S(1)}, u32[]{:S(2)}, u32[]{:S(2)}) collective-permute-start(f32[136,256]{1,0:T(8,128)S(1)} %get-tuple-element.62), channel_id=1, source_target_pairs={{0,8},{8,16},{16,24},{24,0},{1,9},{9,17},{17,25},{25,1},{2,10},{10... | collective-permute-start | bytes 417800 | tf_op jit(solution)/shard_map/ppermute | solution.py:521
  57.4 8.9 %collective-permute-start.15 = (f32[136,256]{1,0:T(8,128)S(1)}, f32[136,256]{1,0:T(8,128)S(1)}, u32[]{:S(2)}, u32[]{:S(2)}) collective-permute-start(f32[136,256]{1,0:T(8,128)S(1)} %get-tuple-element.62), channel_id=1, source_target_pairs={{0,16},{8,24},{16,0},{24,8},{1,17},{9,25},{17,1},{25,9},{2,18},{10... | collective-permute-start | bytes 417800 | tf_op jit(solution)/shard_map/ppermute | solution.py:521
  59.8 7.6 %collective-permute-start.16 = (f32[136,256]{1,0:T(8,128)S(1)}, f32[136,256]{1,0:T(8,128)S(1)}, u32[]{:S(2)}, u32[]{:S(2)}) collective-permute-start(f32[136,256]{1,0:T(8,128)S(1)} %get-tuple-element.62), channel_id=1, source_target_pairs={{0,24},{8,0},{16,8},{24,16},{1,25},{9,1},{17,9},{25,17},{2,26},{10... | collective-permute-start | bytes 417800 | tf_op jit(solution)/shard_map/ppermute | solution.py:521
  62.3 5.2 %collective-permute-start.17 = (f32[136,256]{1,0:T(8,128)S(1)}, f32[136,256]{1,0:T(8,128)S(1)}, u32[]{:S(2)}, u32[]{:S(2)}) collective-permute-start(f32[136,256]{1,0:T(8,128)S(1)} %collective-permute-done.14.m1), channel_id=1, source_target_pairs={{0,4},{4,0},{1,5},{5,1},{2,6},{6,2},{3,7},{7,3},{8,12},{12,8},{9,1... | collective-permute-start | bytes 417800 | tf_op jit(solution)/shard_map/ppermute | solution.py:530
  66.2 2.2 %collective-permute-start.18 = (f32[136,256]{1,0:T(8,128)S(1)}, f32[136,256]{1,0:T(8,128)S(1)}, u32[]{:S(2)}, u32[]{:S(2)}) collective-permute-start(f32[136,256]{1,0:T(8,128)S(1)} %collective-permute-done.15.m2), channel_id=1, source_target_pairs={{0,4},{4,0},{1,5},{5,1},{2,6},{6,2},{3,7},{7,3},{8,12},{12,8},{9,1... | collective-permute-start | bytes 417800 | tf_op jit(solution)/shard_map/ppermute | solution.py:530
  67.4 1.4 collective-permute-start.19
  70.3 6.4 %collective-permute-start.20 = (f32[136,256]{1,0:T(8,128)S(1)}, f32[136,256]{1,0:T(8,128)S(1)}, u32[]{:S(2)}, u32[]{:S(2)}) collective-permute-start(f32[136,256]{1,0:T(8,128)S(1)} %get-tuple-element.64), channel_id=1, source_target_pairs={{0,32},{32,64},{64,96},{96,0},{1,33},{33,65},{65,97},{97,1},{2,34}... | collective-permute-start | bytes 417800 | tf_op jit(solution)/shard_map/ppermute | solution.py:521
  71.7 9.2 %collective-permute-start.21 = (f32[136,256]{1,0:T(8,128)S(1)}, f32[136,256]{1,0:T(8,128)S(1)}, u32[]{:S(2)}, u32[]{:S(2)}) collective-permute-start(f32[136,256]{1,0:T(8,128)S(1)} %get-tuple-element.64), channel_id=1, source_target_pairs={{0,64},{32,96},{64,0},{96,32},{1,65},{33,97},{65,1},{97,33},{2,66}... | collective-permute-start | bytes 417800 | tf_op jit(solution)/shard_map/ppermute | solution.py:521
  74.3 7.6 %collective-permute-start.22 = (f32[136,256]{1,0:T(8,128)S(1)}, f32[136,256]{1,0:T(8,128)S(1)}, u32[]{:S(2)}, u32[]{:S(2)}) collective-permute-start(f32[136,256]{1,0:T(8,128)S(1)} %get-tuple-element.64), channel_id=1, source_target_pairs={{0,96},{32,0},{64,32},{96,64},{1,97},{33,1},{65,33},{97,65},{2,98}... | collective-permute-start | bytes 417800 | tf_op jit(solution)/shard_map/ppermute | solution.py:521
  75.3 7.8 %collective-permute-start.26 = (f32[128,256]{1,0:T(8,128)S(1)}, f32[128,256]{1,0:T(8,128)S(1)}, u32[]{:S(2)}, u32[]{:S(2)}) collective-permute-start(f32[128,256]{1,0:T(8,128)S(1)} %get-tuple-element.68.p0), channel_id=1, source_target_pairs={{0,1},{1,2},{2,3},{3,0},{4,5},{5,6},{6,7},{7,4},{8,9},{9,10},{10,1... | collective-permute-start | bytes 393224 | tf_op jit(solution)/shard_map/ppermute | solution.py:521
  76.7 13.3 %collective-permute-start.23 = (f32[136,256]{1,0:T(8,128)S(1)}, f32[136,256]{1,0:T(8,128)S(1)}, u32[]{:S(2)}, u32[]{:S(2)}) collective-permute-start(f32[136,256]{1,0:T(8,128)S(1)} %collective-permute-done.20.m1), channel_id=1, source_target_pairs={{0,4},{4,0},{1,5},{5,1},{2,6},{6,2},{3,7},{7,3},{8,12},{12,8},{9,1... | collective-permute-start | bytes 417800 | tf_op jit(solution)/shard_map/ppermute | solution.py:530
  80.8 9.2 %collective-permute-start.24 = (f32[136,256]{1,0:T(8,128)S(1)}, f32[136,256]{1,0:T(8,128)S(1)}, u32[]{:S(2)}, u32[]{:S(2)}) collective-permute-start(f32[136,256]{1,0:T(8,128)S(1)} %collective-permute-done.21.m2), channel_id=1, source_target_pairs={{0,4},{4,0},{1,5},{5,1},{2,6},{6,2},{3,7},{7,3},{8,12},{12,8},{9,1... | collective-permute-start | bytes 417800 | tf_op jit(solution)/shard_map/ppermute | solution.py:530
  81.9 8.1 %collective-permute-start.25 = (f32[136,256]{1,0:T(8,128)S(1)}, f32[136,256]{1,0:T(8,128)S(1)}, u32[]{:S(2)}, u32[]{:S(2)}) collective-permute-start(f32[136,256]{1,0:T(8,128)S(1)} %collective-permute-done.22.m3), channel_id=1, source_target_pairs={{0,4},{4,0},{1,5},{5,1},{2,6},{6,2},{3,7},{7,3},{8,12},{12,8},{9,1... | collective-permute-start | bytes 417800 | tf_op jit(solution)/shard_map/ppermute | solution.py:530
  81.9 6.1 %collective-permute-start.27 = (f32[128,256]{1,0:T(8,128)S(1)}, f32[128,256]{1,0:T(8,128)S(1)}, u32[]{:S(2)}, u32[]{:S(2)}) collective-permute-start(f32[128,256]{1,0:T(8,128)S(1)} %get-tuple-element.68.p0), channel_id=1, source_target_pairs={{0,2},{1,3},{2,0},{3,1},{4,6},{5,7},{6,4},{7,5},{8,10},{9,11},{10,... | collective-permute-start | bytes 393224 | tf_op jit(solution)/shard_map/ppermute | solution.py:521
  83.1 6.9 %collective-permute-start.28 = (f32[128,256]{1,0:T(8,128)S(1)}, f32[128,256]{1,0:T(8,128)S(1)}, u32[]{:S(2)}, u32[]{:S(2)}) collective-permute-start(f32[128,256]{1,0:T(8,128)S(1)} %get-tuple-element.68.p0), channel_id=1, source_target_pairs={{0,3},{1,0},{2,1},{3,2},{4,7},{5,4},{6,5},{7,6},{8,11},{9,8},{10,9... | collective-permute-start | bytes 393224 | tf_op jit(solution)/shard_map/ppermute | solution.py:521
  94.8 2.3 %collective-permute-start.29 = (f32[8,256]{1,0:T(8,128)S(1)}, f32[8,256]{1,0:T(8,128)S(1)}, u32[]{:S(2)}, u32[]{:S(2)}) collective-permute-start(f32[8,256]{1,0:T(8,128)S(1)} %get-tuple-element.71.own), channel_id=1, source_target_pairs={{0,4},{4,0},{1,5},{5,1},{2,6},{6,2},{3,7},{7,3},{8,12},{12,8},{9,1... | collective-permute-start | bytes 24584 | tf_op jit(solution)/shard_map/ppermute | solution.py:530
  97.8 4.1 %collective-permute-start.30 = (f32[8,256]{1,0:T(8,128)S(1)}, f32[8,256]{1,0:T(8,128)S(1)}, u32[]{:S(2)}, u32[]{:S(2)}) collective-permute-start(f32[8,256]{1,0:T(8,128)S(1)} %shard_map.103.q0), channel_id=1, source_target_pairs={{0,8},{8,16},{16,24},{24,0},{1,9},{9,17},{17,25},{25,1},{2,10},{10... | collective-permute-start | bytes 24584 | tf_op jit(solution)/shard_map/ppermute | solution.py:521
  98.6 4.0 %collective-permute-start.31 = (f32[8,256]{1,0:T(8,128)S(1)}, f32[8,256]{1,0:T(8,128)S(1)}, u32[]{:S(2)}, u32[]{:S(2)}) collective-permute-start(f32[8,256]{1,0:T(8,128)S(1)} %shard_map.103.q0), channel_id=1, source_target_pairs={{0,16},{8,24},{16,0},{24,8},{1,17},{9,25},{17,1},{25,9},{2,18},{10... | collective-permute-start | bytes 24584 | tf_op jit(solution)/shard_map/ppermute | solution.py:521
  100.7 2.9 %collective-permute-start.32 = (f32[8,256]{1,0:T(8,128)S(1)}, f32[8,256]{1,0:T(8,128)S(1)}, u32[]{:S(2)}, u32[]{:S(2)}) collective-permute-start(f32[8,256]{1,0:T(8,128)S(1)} %shard_map.103.q0), channel_id=1, source_target_pairs={{0,24},{8,0},{16,8},{24,16},{1,25},{9,1},{17,9},{25,17},{2,26},{10... | collective-permute-start | bytes 24584 | tf_op jit(solution)/shard_map/ppermute | solution.py:521
  104.6 6.5 %collective-permute-start.33 = (f32[8,256]{1,0:T(8,128)S(1)}, f32[8,256]{1,0:T(8,128)S(1)}, u32[]{:S(2)}, u32[]{:S(2)}) collective-permute-start(f32[8,256]{1,0:T(8,128)S(1)} %get-tuple-element.72.gy0), channel_id=1, source_target_pairs={{0,32},{32,64},{64,96},{96,0},{1,33},{33,65},{65,97},{97,1},{2,34}... | collective-permute-start | bytes 24584 | tf_op jit(solution)/shard_map/ppermute | solution.py:521
  105.8 5.3 %collective-permute-start.34 = (f32[8,256]{1,0:T(8,128)S(1)}, f32[8,256]{1,0:T(8,128)S(1)}, u32[]{:S(2)}, u32[]{:S(2)}) collective-permute-start(f32[8,256]{1,0:T(8,128)S(1)} %get-tuple-element.72.gy0), channel_id=1, source_target_pairs={{0,64},{32,96},{64,0},{96,32},{1,65},{33,97},{65,1},{97,33},{2,66}... | collective-permute-start | bytes 24584 | tf_op jit(solution)/shard_map/ppermute | solution.py:521
  108.2 2.9 %collective-permute-start.35 = (f32[8,256]{1,0:T(8,128)S(1)}, f32[8,256]{1,0:T(8,128)S(1)}, u32[]{:S(2)}, u32[]{:S(2)}) collective-permute-start(f32[8,256]{1,0:T(8,128)S(1)} %get-tuple-element.72.gy0), channel_id=1, source_target_pairs={{0,96},{32,0},{64,32},{96,64},{1,97},{33,1},{65,33},{97,65},{2,98}... | collective-permute-start | bytes 24584 | tf_op jit(solution)/shard_map/ppermute | solution.py:521
  111.1 4.8 %copy-start.1 = (bf16[512,1024]{1,0:T(8,128)(2,1)S(1)}, bf16[512,1024]{1,0:T(8,128)(2,1)}, u32[]{:S(2)}) copy-start(bf16[512,1024]{1,0:T(8,128)(2,1)} %observed.5) | copy-start | bytes 3145732
  117.2 4.6 %collective-permute-start.36 = (f32[16,64,128]{2,1,0:T(8,128)S(1)}, f32[16,64,128]{2,1,0:T(8,128)S(1)}, u32[]{:S(2)}, u32[]{:S(2)}) collective-permute-start(f32[16,64,128]{2,1,0:T(8,128)S(1)} %get-tuple-element.83), channel_id=1, source_target_pairs={{0,4},{4,0},{1,5},{5,1},{2,6},{6,2},{3,7},{7,3},{8,12},{12,8},{9,1... | collective-permute-start | bytes 1572872 | tf_op jit(solution)/shard_map/ppermute | solution.py:530
  121.9 7.0 %copy-start.4 = (bf16[1024,256]{1,0:T(8,128)(2,1)S(1)}, bf16[1024,256]{1,0:T(8,128)(2,1)}, u32[]{:S(2)}) copy-start(bf16[1024,256]{1,0:T(8,128)(2,1)} %loads.5) | copy-start | bytes 1572868
  122.7 6.4 %copy-start.6 = (s32[8]{0:T(128)S(1)}, s32[8]{0:T(128)}, u32[]{:S(2)}) copy-start(s32[8]{0:T(128)} %panel_of.1) | copy-start | bytes 100
  122.7 34.0 %all-to-all-start = ((f32[16,64,128]{2,1,0:T(8,128)}), f32[16,64,128]{2,1,0:T(8,128)S(1)}, u32[]{:S(2)}, u32[]{:S(2)}) async-start(f32[16,64,128]{2,1,0:T(8,128)} %shard_map.108), calls=%async_computation | async-start | bytes 1048576 | tf_op jit(solution)/shard_map/all_to_all | solution.py:617
  128.2 3.6 %collective-permute-start.37 = (f32[136,128]{1,0:T(8,128)S(1)}, f32[136,128]{1,0:T(8,128)S(1)}, u32[]{:S(2)}, u32[]{:S(2)}) collective-permute-start(f32[136,128]{1,0:T(8,128)S(1)} %get-tuple-element.85), channel_id=1, source_target_pairs={{0,4},{4,0},{1,5},{5,1},{2,6},{6,2},{3,7},{7,3},{8,12},{12,8},{9,1... | collective-permute-start | bytes 208904 | tf_op jit(solution)/shard_map/ppermute | solution.py:530
  130.5 1.2 collective-permute-start.38
  131.7 7.0 %collective-permute-start.39 = (f32[144,128]{1,0:T(8,128)S(1)}, f32[144,128]{1,0:T(8,128)S(1)}, u32[]{:S(2)}, u32[]{:S(2)}) collective-permute-start(f32[144,128]{1,0:T(8,128)S(1)} %shard_map.112.a), channel_id=1, source_target_pairs={{0,8},{8,16},{16,24},{24,0},{1,9},{9,17},{17,25},{25,1},{2,10},{10... | collective-permute-start | bytes 221192 | tf_op jit(solution)/shard_map/ppermute | solution.py:521
  133.4 6.5 %collective-permute-start.40 = (f32[144,128]{1,0:T(8,128)S(1)}, f32[144,128]{1,0:T(8,128)S(1)}, u32[]{:S(2)}, u32[]{:S(2)}) collective-permute-start(f32[144,128]{1,0:T(8,128)S(1)} %shard_map.112.a), channel_id=1, source_target_pairs={{0,16},{8,24},{16,0},{24,8},{1,17},{9,25},{17,1},{25,9},{2,18},{10... | collective-permute-start | bytes 221192 | tf_op jit(solution)/shard_map/ppermute | solution.py:521
  135.8 4.2 %collective-permute-start.41 = (f32[144,128]{1,0:T(8,128)S(1)}, f32[144,128]{1,0:T(8,128)S(1)}, u32[]{:S(2)}, u32[]{:S(2)}) collective-permute-start(f32[144,128]{1,0:T(8,128)S(1)} %shard_map.112.a), channel_id=1, source_target_pairs={{0,24},{8,0},{16,8},{24,16},{1,25},{9,1},{17,9},{25,17},{2,26},{10... | collective-permute-start | bytes 221192 | tf_op jit(solution)/shard_map/ppermute | solution.py:521
  139.9 4.8 %collective-permute-start.42 = (f32[144,128]{1,0:T(8,128)S(1)}, f32[144,128]{1,0:T(8,128)S(1)}, u32[]{:S(2)}, u32[]{:S(2)}) collective-permute-start(f32[144,128]{1,0:T(8,128)S(1)} %shard_map.113.a), channel_id=1, source_target_pairs={{0,32},{32,64},{64,96},{96,0},{1,33},{33,65},{65,97},{97,1},{2,34}... | collective-permute-start | bytes 221192 | tf_op jit(solution)/shard_map/ppermute | solution.py:521
  141.2 5.0 %collective-permute-start.43 = (f32[144,128]{1,0:T(8,128)S(1)}, f32[144,128]{1,0:T(8,128)S(1)}, u32[]{:S(2)}, u32[]{:S(2)}) collective-permute-start(f32[144,128]{1,0:T(8,128)S(1)} %shard_map.113.a), channel_id=1, source_target_pairs={{0,64},{32,96},{64,0},{96,32},{1,65},{33,97},{65,1},{97,33},{2,66}... | collective-permute-start | bytes 221192 | tf_op jit(solution)/shard_map/ppermute | solution.py:521
  143.6 3.6 %collective-permute-start.44 = (f32[144,128]{1,0:T(8,128)S(1)}, f32[144,128]{1,0:T(8,128)S(1)}, u32[]{:S(2)}, u32[]{:S(2)}) collective-permute-start(f32[144,128]{1,0:T(8,128)S(1)} %shard_map.113.a), channel_id=1, source_target_pairs={{0,96},{32,0},{64,32},{96,64},{1,97},{33,1},{65,33},{97,65},{2,98}... | collective-permute-start | bytes 221192 | tf_op jit(solution)/shard_map/ppermute | solution.py:521
  147.2 7.3 %collective-permute-start.46 = (f32[8,128]{1,0:T(8,128)S(1)}, f32[8,128]{1,0:T(8,128)S(1)}, u32[]{:S(2)}, u32[]{:S(2)}) collective-permute-start(f32[8,128]{1,0:T(8,128)S(1)} %get-tuple-element.87.s0), channel_id=1, source_target_pairs={{0,1},{1,2},{2,3},{3,0},{4,5},{5,6},{6,7},{7,4},{8,9},{9,10},{10,1... | collective-permute-start | bytes 12296 | tf_op jit(solution)/shard_map/ppermute | solution.py:521
  147.8 6.6 %collective-permute-start.47 = (f32[8,128]{1,0:T(8,128)S(1)}, f32[8,128]{1,0:T(8,128)S(1)}, u32[]{:S(2)}, u32[]{:S(2)}) collective-permute-start(f32[8,128]{1,0:T(8,128)S(1)} %get-tuple-element.87.s0), channel_id=1, source_target_pairs={{0,2},{1,3},{2,0},{3,1},{4,6},{5,7},{6,4},{7,5},{8,10},{9,11},{10,... | collective-permute-start | bytes 12296 | tf_op jit(solution)/shard_map/ppermute | solution.py:521
  150.8 3.7 %collective-permute-start.48 = (f32[8,128]{1,0:T(8,128)S(1)}, f32[8,128]{1,0:T(8,128)S(1)}, u32[]{:S(2)}, u32[]{:S(2)}) collective-permute-start(f32[8,128]{1,0:T(8,128)S(1)} %get-tuple-element.87.s0), channel_id=1, source_target_pairs={{0,3},{1,0},{2,1},{3,2},{4,7},{5,4},{6,5},{7,6},{8,11},{9,8},{10,9... | collective-permute-start | bytes 12296 | tf_op jit(solution)/shard_map/ppermute | solution.py:521
  150.8 4.6 %collective-permute-start.45 = (f32[136,128]{1,0:T(8,128)S(1)}, f32[136,128]{1,0:T(8,128)S(1)}, u32[]{:S(2)}, u32[]{:S(2)}) collective-permute-start(f32[136,128]{1,0:T(8,128)S(1)} %get-tuple-element.86.mine), channel_id=1, source_target_pairs={{0,4},{4,0},{1,5},{5,1},{2,6},{6,2},{3,7},{7,3},{8,12},{12,8},{9,1... | collective-permute-start | bytes 208904 | tf_op jit(solution)/shard_map/ppermute | solution.py:530

commit v3 on v2

--- a/solution.py
+++ b/solution.py
@@ -75,8 +75,9 @@
     )
 
 
-def gram_kernel(place, present, both, loads, table, *outs):
+def gram_kernel(place, present, both, loads, table, kept_loads, *outs):
     coef = loads[...]
+    kept_loads[...] = coef
     series, n = coef.shape
     mask = present[...].astype(F32)
     inv_noise = 1.0 / both[:, 0:series]
@@ -132,8 +133,8 @@
         guess[...] = 2.0 * x - dot3(pair, split(dot3(split(whole), pair)))
         return err * err
 
-    err = lax.while_loop(lambda e: (e > 1e-4) & (top < 8.0), quick, start * start)
-    lax.while_loop(lambda e: e > 0.99e-8, body, err)
+    err = lax.while_loop(lambda e: (e > 2e-4) & (top < 8.0), quick, start * start)
+    lax.while_loop(lambda e: e > 3.9e-8, body, err)
     inverse = guess[...]
     gain = jnp.dot(gram, inverse, precision=HIGH, preferred_element_type=F32)
     gain = 0.5 * (gain + gain.T)
@@ -170,16 +171,21 @@
     for k, e in enumerate((e0, e1, e2, e3)):
         errs[lax.rem(place[3] + nb - k, nb)] = unpack(e[...])
 
-    def square(level, carry):
+    def square(level):
         for b in range(nb):
             err = errs[b]
             pair = split(err)
             his[level * nb + b] = pair[0]
             los[level * nb + b] = pair[1]
             errs[b] = 2.0 * err - dot3(pair, pair)
+
+    def squares(k, carry):
+        square(2 * k)
+        square(2 * k + 1)
         return carry
 
-    lax.fori_loop(0, LEVELS, square, 0)
+    lax.fori_loop(0, LEVELS // 2, squares, 0)
+    square(LEVELS - 1)
     total = errs[0]
     tops[0] = total
     for b in range(1, nb):
@@ -516,10 +522,10 @@
 
 def from_peers(arrays, axis):
     n = lax.axis_size(axis)
-    out = [arrays[0]]
-    for k in range(1, n):
-        out.append(lax.ppermute(arrays[k], axis, [(i, (i + k) % n) for i in range(n)]))
-    return out
+    out = {0: arrays[0]}
+    for k in reversed(range(1, n)):
+        out[k] = lax.ppermute(arrays[k], axis, [(i, (i + k) % n) for i in range(n)])
+    return [out[k] for k in range(n)]
 
 
 def gather(array, axis):
@@ -552,10 +558,10 @@
     powers = ((LEVELS * nb, width, width), BF16)
 
     both = jnp.concatenate([noise_var, decay_rate]).reshape(1, series + width)
-    table, *grams = call(
-        gram_kernel, [((16, series), F32)] + [packed] * nb, [], place, present, both, loadings
-    )
-    projs = call(project_kernel, [rows2] * nb, [], place, table, loadings, observed)
+    table, loads, *grams = call(
+        gram_kernel, [((16, series), F32), (loadings.shape, BF16)] + [packed] * nb, [], place, present, both, loadings
+    )
+    projs = call(project_kernel, [rows2] * nb, [], place, table, loads, observed)
     grams = from_peers(grams, "panel")
     projs = from_peers(projs, "panel")
     (err,) = call(inverse_kernel, [packed], [square], table, *grams, smem=0)
@@ -571,7 +577,7 @@
     end_far = swap(seg_end, ac)
     projs = gather(proj, "panel")
     pair, pair_half = call(pair_kernel, [map_shape, half_shape], [], place, seg, seg_far, seg_end, end_far)
-    (turned,) = call(turn_kernel, [((width, series), BF16)], [], loadings, smem=0)
+    (turned,) = call(turn_kernel, [((width, series), BF16)], [], loads, smem=0)
     near = gather(pair_half, ax)[1:]
     group, group_half, xs = call(
         group_kernel, [map_shape, half_shape, maps4], [],
@@ -590,9 +596,7 @@
     )
     first_far = swap(first, ac)
     (pair_first,) = call(pair_back_kernel, [vec], [], place, first, first_far, seg, seg_far)
-    group_first, gxs = call(
-        group_back_kernel, [vec, vecs4], [], place, *gather(pair_first, ax), xs
-    )
+    group_first, gxs = call(group_back_kernel, [vec, vecs4], [], place, *gather(pair_first, ax), xs)
     flat = ((time_rows, width), BF16)
     piece = ((BLOCK + 8, half), F32)
     firsts_y = gather(group_first, ay)

time: 160 us -> 161 us (level)
  waiting for transfers between devices: 34 us -> 49.8 us
  starting transfers between devices: 76.9 us -> 63.1 us
    ppermute x36, waiting for transfers between devices: 28 us -> 44.5 us  [from_peers(): out[k] = lax.ppermute(arrays[k], axis, [(i, (i + k) % n) for i in range(n)])]
    ppermute x36, starting transfers between devices: 53.4 us -> 40.2 us  [from_peers(): out[k] = lax.ppermute(arrays[k], axis, [(i, (i + k) % n) for i in range(n)])]
    unnamed x14 -> x10, local copies, waits for them, and re-layouts: 4.04 us -> 2.99 us
  transfers between devices with their start and end apart: 50 -> 50, of which waited for: 24 -> 28; matrix products, arithmetic and copies ran while one was open for 0% -> 0% of each run, Pallas kernels for 10% -> 10%
where the time goes in v3:
time: 161 us; the launch traced here: 158 us
  starting transfers between devices  63.1 us (39%)
  waiting for transfers between devices  49.8 us (31%)
  Pallas kernels  40 us (25%)
  local copies, waits for them, and re-layouts  3.52 us (2%)
    ppermute x36, waiting for transfers between devices, from_peers(): out[k] = lax.ppermute(arrays[k], axis, [(i, (i + k) % n) for i in range(n)])  44.5 us
    ppermute x36, starting transfers between devices, from_peers(): out[k] = lax.ppermute(arrays[k], axis, [(i, (i + k) % n) for i in range(n)])  40.2 us
    pallas_call x24, Pallas kernels, call(): return made(*args)  40 us
    ppermute x13, starting transfers between devices, swap(): return lax.ppermute(array, axis, [(0, 1), (1, 0)])  18.6 us
    ppermute x13, waiting for transfers between devices, swap(): return lax.ppermute(array, axis, [(0, 1), (1, 0)])  5.36 us
    all_to_all x1, starting transfers between devices, step(): arrived = lax.all_to_all(spread, (ay, ax), 0, 0, tiled=True)  4.24 us
  transfers between devices with their start and end apart: 50, of which 28 were waited for; matrix products, arithmetic and copies ran while one was open for 0% of the time, Pallas kernels for 10%

profile of v3, /device:TPU:1, one launch (start us, length us, event | category | flops | bytes accessed | tf_op | source)
XLA Modules:
  0.0 158.1 jit_solution(6406795700418231085)
XLA Ops:
  1.4 1.0 copy-done.2
  3.2 1.8 %shard_map.93 = (f32[16,1024]{1,0:T(8,128)S(1)}, bf16[1024,256]{1,0:T(8,128)(2,1)S(1)}, f32[264,128]{1,0:T(8,128)S(1)}, f32[264,128]{1,0:T(8,128)S(1)}, f32[264,128]{1,0:T(8,128)S(1)}, /*index=5*/f32[264,128]{1,0:T(8,128)S(1)}) custom-call(s32[4]{0:T(128)S(1)} %pad_add_fusion.place, s32[4,1024]{1,0:T(4,128)S(1)} %copy-done.3, f32[1,1280]{1,0:T(1,128)S(1)} %reshape.11.both, ...), custom_call_target="tpu_custom_call" | custom-call | tf_op jit(solution)/shard_map/pallas_call | solution.py:520
  5.0 2.5 %collective-permute-start = (f32[264,128]{1,0:T(8,128)S(1)}, f32[264,128]{1,0:T(8,128)S(1)}, u32[]{:S(2)}, u32[]{:S(2)}) collective-permute-start(f32[264,128]{1,0:T(8,128)S(1)} %get-tuple-element.49), channel_id=1, source_target_pairs={{0,1},{1,2},{2,3},{3,0},{4,5},{5,6},{6,7},{7,4},{8,9},{9,10},{10,1... | collective-permute-start | bytes 405512 | tf_op jit(solution)/shard_map/ppermute | solution.py:527
  7.6 3.3 %collective-permute-start.1 = (f32[264,128]{1,0:T(8,128)S(1)}, f32[264,128]{1,0:T(8,128)S(1)}, u32[]{:S(2)}, u32[]{:S(2)}) collective-permute-start(f32[264,128]{1,0:T(8,128)S(1)} %get-tuple-element.50), channel_id=1, source_target_pairs={{0,2},{1,3},{2,0},{3,1},{4,6},{5,7},{6,4},{7,5},{8,10},{9,11},{10,... | collective-permute-start | bytes 405512 | tf_op jit(solution)/shard_map/ppermute | solution.py:527
  11.6 1.2 copy-done
  12.8 1.3 shard_map.96
  14.9 1.8 %collective-permute-done.1.g2 = f32[264,128]{1,0:T(8,128)S(1)} collective-permute-done((f32[264,128]{1,0:T(8,128)S(1)}, f32[264,128]{1,0:T(8,128)S(1)}, u32[]{:S(2)}, u32[]{:S(2)}) %collective-permute-start.1) | collective-permute-done | bytes 135200 | tf_op jit(solution)/shard_map/ppermute | solution.py:527
  16.8 3.3 %shard_map.94.e0.packed = f32[264,128]{1,0:T(8,128)S(1)} custom-call(f32[16,1024]{1,0:T(8,128)S(1)} %get-tuple-element.47.table, f32[264,128]{1,0:T(8,128)S(1)} %get-tuple-element.48.g0, f32[264,128]{1,0:T(8,128)S(1)} %collective-permute-done.g1, f32[264,128]{1,0:T(8,128)S(1)} %collective-permute-done.1.g2, f32[264,128]{1,0:T(8,128)S(1)} %collective-permute-done.2.g3), custom_call_target="tpu_custom_call" | custom-call | tf_op jit(solution)/shard_map/pallas_call | solution.py:520
  20.1 2.5 %collective-permute-start.5 = (f32[264,128]{1,0:T(8,128)S(1)}, f32[264,128]{1,0:T(8,128)S(1)}, u32[]{:S(2)}, u32[]{:S(2)}) collective-permute-start(f32[264,128]{1,0:T(8,128)S(1)} %shard_map.94.e0.packed), channel_id=1, source_target_pairs={{0,3},{1,0},{2,1},{3,2},{4,7},{5,4},{6,5},{7,6},{8,11},{9,8},{10,9... | collective-permute-start | bytes 405512 | tf_op jit(solution)/shard_map/ppermute | solution.py:527
  22.6 1.0 collective-permute-start.4
  23.6 1.9 %collective-permute-start.7 = (f32[128,256]{1,0:T(8,128)S(1)}, f32[128,256]{1,0:T(8,128)S(1)}, u32[]{:S(2)}, u32[]{:S(2)}) collective-permute-start(f32[128,256]{1,0:T(8,128)S(1)} %get-tuple-element.56), channel_id=1, source_target_pairs={{0,2},{1,3},{2,0},{3,1},{4,6},{5,7},{6,4},{7,5},{8,10},{9,11},{10,... | collective-permute-start | bytes 393224 | tf_op jit(solution)/shard_map/ppermute | solution.py:527
  25.5 2.1 %collective-permute-start.8 = (f32[128,256]{1,0:T(8,128)S(1)}, f32[128,256]{1,0:T(8,128)S(1)}, u32[]{:S(2)}, u32[]{:S(2)}) collective-permute-start(f32[128,256]{1,0:T(8,128)S(1)} %get-tuple-element.57), channel_id=1, source_target_pairs={{0,3},{1,0},{2,1},{3,2},{4,7},{5,4},{6,5},{7,6},{8,11},{9,8},{10,9... | collective-permute-start | bytes 393224 | tf_op jit(solution)/shard_map/ppermute | solution.py:527
  27.6 5.7 %collective-permute-done.7.p2 = f32[128,256]{1,0:T(8,128)S(1)} collective-permute-done((f32[128,256]{1,0:T(8,128)S(1)}, f32[128,256]{1,0:T(8,128)S(1)}, u32[]{:S(2)}, u32[]{:S(2)}) %collective-permute-start.7) | collective-permute-done | bytes 131104 | tf_op jit(solution)/shard_map/ppermute | solution.py:527
  34.0 2.9 %shard_map.97 = (f32[128,256]{1,0:T(8,128)S(1)}, f32[8,256]{1,0:T(8,128)S(1)}) custom-call(f32[16,1024]{1,0:T(8,128)S(1)} %get-tuple-element.47.table, f32[264,128]{1,0:T(8,128)S(1)} %shard_map.94.e0.packed, f32[128,256]{1,0:T(8,128)S(1)} %get-tuple-element.54.p0, f32[128,256]{1,0:T(8,128)S(1)} %collective-permute-done.6.p1, ...), custom_call_target="tpu_custom_call" | custom-call | tf_op jit(solution)/shard_map/pallas_call | solution.py:520
  36.9 5.6 %shard_map.95 = (bf16[28,256,256]{2,1,0:T(8,128)(2,1)S(1)}, bf16[28,256,256]{2,1,0:T(8,128)(2,1)S(1)}, f32[4,256,256]{2,1,0:T(8,128)S(1)}, f32[256,256]{1,0:T(8,128)S(1)}) custom-call(s32[4]{0:T(128)S(1)} %pad_add_fusion.place, f32[264,128]{1,0:T(8,128)S(1)} %shard_map.94.e0.packed, f32[264,128]{1,0:T(8,128)S(1)} %collective-permute-done.3.e1, ...), custom_call_target="tpu_custom_call" | custom-call | tf_op jit(solution)/shard_map/pallas_call | solution.py:520
  42.5 1.9 %collective-permute-start.9 = (f32[256,256]{1,0:T(8,128)S(1)}, f32[256,256]{1,0:T(8,128)S(1)}, u32[]{:S(2)}, u32[]{:S(2)}) collective-permute-start(f32[256,256]{1,0:T(8,128)S(1)} %get-tuple-element.59.mine), channel_id=1, source_target_pairs={{0,4},{4,0},{1,5},{5,1},{2,6},{6,2},{3,7},{7,3},{8,12},{12,8},{9,1... | collective-permute-start | bytes 786440 | tf_op jit(solution)/shard_map/ppermute | solution.py:536
  44.4 2.5 %collective-permute-start.12 = (f32[8,256]{1,0:T(8,128)S(1)}, f32[8,256]{1,0:T(8,128)S(1)}, u32[]{:S(2)}, u32[]{:S(2)}) collective-permute-start(f32[8,256]{1,0:T(8,128)S(1)} %get-tuple-element.61.v0), channel_id=1, source_target_pairs={{0,3},{1,0},{2,1},{3,2},{4,7},{5,4},{6,5},{7,6},{8,11},{9,8},{10,9... | collective-permute-start | bytes 24584 | tf_op jit(solution)/shard_map/ppermute | solution.py:527
  47.7 3.2 %collective-permute-done.11.v2 = f32[8,256]{1,0:T(8,128)S(1)} collective-permute-done((f32[8,256]{1,0:T(8,128)S(1)}, f32[8,256]{1,0:T(8,128)S(1)}, u32[]{:S(2)}, u32[]{:S(2)}) %collective-permute-start.11) | collective-permute-done | bytes 8224 | tf_op jit(solution)/shard_map/ppermute | solution.py:527
  50.9 0.9 shard_map.98
  51.9 2.0 %collective-permute-start.13 = (f32[8,256]{1,0:T(8,128)S(1)}, f32[8,256]{1,0:T(8,128)S(1)}, u32[]{:S(2)}, u32[]{:S(2)}) collective-permute-start(f32[8,256]{1,0:T(8,128)S(1)} %get-tuple-element.62.v_mine), channel_id=1, source_target_pairs={{0,4},{4,0},{1,5},{5,1},{2,6},{6,2},{3,7},{7,3},{8,12},{12,8},{9,1... | collective-permute-start | bytes 24584 | tf_op jit(solution)/shard_map/ppermute | solution.py:536
  53.9 0.8 collective-permute-done.13.v_other
  54.7 0.9 shard_map.99
  55.6 2.5 %collective-permute-start.16 = (f32[136,256]{1,0:T(8,128)S(1)}, f32[136,256]{1,0:T(8,128)S(1)}, u32[]{:S(2)}, u32[]{:S(2)}) collective-permute-start(f32[136,256]{1,0:T(8,128)S(1)} %get-tuple-element.64), channel_id=1, source_target_pairs={{0,24},{8,0},{16,8},{24,16},{1,25},{9,1},{17,9},{25,17},{2,26},{10... | collective-permute-start | bytes 417800 | tf_op jit(solution)/shard_map/ppermute | solution.py:527
  59.2 4.4 %collective-permute-done.16.m3 = f32[136,256]{1,0:T(8,128)S(1)} collective-permute-done((f32[136,256]{1,0:T(8,128)S(1)}, f32[136,256]{1,0:T(8,128)S(1)}, u32[]{:S(2)}, u32[]{:S(2)}) %collective-permute-start.16) | collective-permute-done | bytes 139296 | tf_op jit(solution)/shard_map/ppermute | solution.py:527
  63.6 1.4 collective-permute-start.19
  65.0 1.8 %collective-permute-start.18 = (f32[136,256]{1,0:T(8,128)S(1)}, f32[136,256]{1,0:T(8,128)S(1)}, u32[]{:S(2)}, u32[]{:S(2)}) collective-permute-start(f32[136,256]{1,0:T(8,128)S(1)} %collective-permute-done.15.m2), channel_id=1, source_target_pairs={{0,4},{4,0},{1,5},{5,1},{2,6},{6,2},{3,7},{7,3},{8,12},{12,8},{9,1... | collective-permute-start | bytes 417800 | tf_op jit(solution)/shard_map/ppermute | solution.py:536
  66.8 1.4 collective-permute-done.14.m1
  68.7 1.0 collective-permute-done.17.o1
  69.7 1.5 shard_map.100
  71.2 2.8 %collective-permute-start.22 = (f32[136,256]{1,0:T(8,128)S(1)}, f32[136,256]{1,0:T(8,128)S(1)}, u32[]{:S(2)}, u32[]{:S(2)}) collective-permute-start(f32[136,256]{1,0:T(8,128)S(1)} %get-tuple-element.66), channel_id=1, source_target_pairs={{0,96},{32,0},{64,32},{96,64},{1,97},{33,1},{65,33},{97,65},{2,98}... | collective-permute-start | bytes 417800 | tf_op jit(solution)/shard_map/ppermute | solution.py:527
  75.2 4.4 %collective-permute-done.22.m3 = f32[136,256]{1,0:T(8,128)S(1)} collective-permute-done((f32[136,256]{1,0:T(8,128)S(1)}, f32[136,256]{1,0:T(8,128)S(1)}, u32[]{:S(2)}, u32[]{:S(2)}) %collective-permute-start.22) | collective-permute-done | bytes 139296 | tf_op jit(solution)/shard_map/ppermute | solution.py:527
  79.5 1.3 collective-permute-start.25
  80.9 1.9 %collective-permute-start.24 = (f32[136,256]{1,0:T(8,128)S(1)}, f32[136,256]{1,0:T(8,128)S(1)}, u32[]{:S(2)}, u32[]{:S(2)}) collective-permute-start(f32[136,256]{1,0:T(8,128)S(1)} %collective-permute-done.21.m2), channel_id=1, source_target_pairs={{0,4},{4,0},{1,5},{5,1},{2,6},{6,2},{3,7},{7,3},{8,12},{12,8},{9,1... | collective-permute-start | bytes 417800 | tf_op jit(solution)/shard_map/ppermute | solution.py:536
  82.7 1.4 collective-permute-done.20.m1
  84.6 1.5 collective-permute-start.27
  86.1 3.0 %shard_map.101 = (f32[4,264,256]{2,1,0:T(8,128)S(1)}, f32[4,256,256]{2,1,0:T(8,128)S(1)}) custom-call(s32[4]{0:T(128)S(1)} %pad_add_fusion.place, f32[4,264,256]{2,1,0:T(8,128)S(1)} %get-tuple-element.67.xs, f32[256,256]{1,0:T(8,128)S(1)} %collective-permute-done.9.other, f32[8,256]{1,0:T(8,128)S(1)} %collective-permute-done.13.v_other, ...), custom_call_target="tpu_custom_call" | custom-call | tf_op jit(solution)/shard_map/pallas_call | solution.py:520
  89.1 2.0 %collective-permute-done.27.p2 = f32[128,256]{1,0:T(8,128)S(1)} collective-permute-done((f32[128,256]{1,0:T(8,128)S(1)}, f32[128,256]{1,0:T(8,128)S(1)}, u32[]{:S(2)}, u32[]{:S(2)}) %collective-permute-start.27) | collective-permute-done | bytes 131104 | tf_op jit(solution)/shard_map/ppermute | solution.py:527
  91.1 3.2 %collective-permute-done.26.p1 = f32[128,256]{1,0:T(8,128)S(1)} collective-permute-done((f32[128,256]{1,0:T(8,128)S(1)}, f32[128,256]{1,0:T(8,128)S(1)}, u32[]{:S(2)}, u32[]{:S(2)}) %collective-permute-start.26) | collective-permute-done | bytes 131104 | tf_op jit(solution)/shard_map/ppermute | solution.py:527
  94.3 4.8 %shard_map.102 = (f32[4,128,256]{2,1,0:T(8,128)S(1)}, f32[4,128,256]{2,1,0:T(8,128)S(1)}, f32[4,8,256]{2,1,0:T(8,128)S(1)}, f32[8,256]{1,0:T(8,128)S(1)}, f32[4,264,256]{2,1,0:T(8,128)S(1)}) custom-call(s32[4]{0:T(128)S(1)} %pad_add_fusion.place, f32[16,1024]{1,0:T(8,128)S(1)} %get-tuple-element.47.table, f32[264,256]{1,0:T(8,128)S(1)} %get-tuple-element.65.own, ...), custom_call_target="tpu_custom_call" | custom-call | tf_op jit(solution)/shard_map/pallas_call | solution.py:520
  99.7 0.8 collective-permute-done.29.far
  102.7 1.0 collective-permute-done.32.q3
  103.8 1.8 %collective-permute-done.31.q2 = f32[8,256]{1,0:T(8,128)S(1)} collective-permute-done((f32[8,256]{1,0:T(8,128)S(1)}, f32[8,256]{1,0:T(8,128)S(1)}, u32[]{:S(2)}, u32[]{:S(2)}) %collective-permute-start.31) | collective-permute-done | bytes 8224 | tf_op jit(solution)/shard_map/ppermute | solution.py:527
  106.2 1.0 shard_map.104
  107.1 0.9 collective-permute-start.35
  108.7 1.7 %shard_map.105.offsets = f32[4,8,256]{2,1,0:T(8,128)S(1)} custom-call(s32[4]{0:T(128)S(1)} %pad_add_fusion.place, f32[4,8,256]{2,1,0:T(8,128)S(1)} %get-tuple-element.77.qs, f32[4,264,256]{2,1,0:T(8,128)S(1)} %get-tuple-element.67.xs, f32[8,256]{1,0:T(8,128)S(1)} %collective-permute-done.29.far, f32[256,256]{1,0:T(8,128)S(1)} %collective-permute-done.9.other, ...), custom_call_target="tpu_custom_call" | custom-call | tf_op jit(solution)/shard_map/pallas_call | solution.py:520
  110.4 1.6 %collective-permute-done.34.gy2 = f32[8,256]{1,0:T(8,128)S(1)} collective-permute-done((f32[8,256]{1,0:T(8,128)S(1)}, f32[8,256]{1,0:T(8,128)S(1)}, u32[]{:S(2)}, u32[]{:S(2)}) %collective-permute-start.34) | collective-permute-done | bytes 8224 | tf_op jit(solution)/shard_map/ppermute | solution.py:527
  112.1 4.8 %shard_map.106 = (f32[512,256]{1,0:T(8,128)}, bf16[512,256]{1,0:T(8,128)(2,1)S(1)}, bf16[512,256]{1,0:T(8,128)(2,1)S(1)}, f32[136,128]{1,0:T(8,128)S(1)}, f32[136,128]{1,0:T(8,128)S(1)}) custom-call(s32[4]{0:T(128)S(1)} %pad_add_fusion.place, f32[16,1024]{1,0:T(8,128)S(1)} %get-tuple-element.47.table, f32[8,256]{1,0:T(8,128)S(1)} %get-tuple-element.74.gy0, ...), custom_call_target="tpu_custom_call" | custom-call | tf_op jit(solution)/shard_map/pallas_call | solution.py:520
  116.9 1.3 shard_map.107
  118.2 3.3 %collective-permute-start.36 = (f32[16,64,128]{2,1,0:T(8,128)S(1)}, f32[16,64,128]{2,1,0:T(8,128)S(1)}, u32[]{:S(2)}, u32[]{:S(2)}) collective-permute-start(f32[16,64,128]{2,1,0:T(8,128)S(1)} %get-tuple-element.85), channel_id=1, source_target_pairs={{0,4},{4,0},{1,5},{5,1},{2,6},{6,2},{3,7},{7,3},{8,12},{12,8},{9,1... | collective-permute-start | bytes 1572872 | tf_op jit(solution)/shard_map/ppermute | solution.py:536
  121.5 1.5 collective-permute-done.36.b
  123.1 0.9 shard_map.108
  123.9 4.2 %all-to-all-start = ((f32[16,64,128]{2,1,0:T(8,128)}), f32[16,64,128]{2,1,0:T(8,128)S(1)}, u32[]{:S(2)}, u32[]{:S(2)}) async-start(f32[16,64,128]{2,1,0:T(8,128)} %shard_map.108), calls=%async_computation | async-start | bytes 1048576 | tf_op jit(solution)/shard_map/all_to_all | solution.py:621
  129.1 1.4 shard_map.111.s
  130.6 1.2 collective-permute-done.38.s_far
  131.8 2.9 %collective-permute-start.41 = (f32[144,128]{1,0:T(8,128)S(1)}, f32[144,128]{1,0:T(8,128)S(1)}, u32[]{:S(2)}, u32[]{:S(2)}) collective-permute-start(f32[144,128]{1,0:T(8,128)S(1)} %shard_map.112.a), channel_id=1, source_target_pairs={{0,24},{8,0},{16,8},{24,16},{1,25},{9,1},{17,9},{25,17},{2,26},{10... | collective-permute-start | bytes 221192 | tf_op jit(solution)/shard_map/ppermute | solution.py:527
  135.8 1.4 collective-permute-done.41.d
  137.2 2.5 %collective-permute-done.40.c = f32[144,128]{1,0:T(8,128)S(1)} collective-permute-done((f32[144,128]{1,0:T(8,128)S(1)}, f32[144,128]{1,0:T(8,128)S(1)}, u32[]{:S(2)}, u32[]{:S(2)}) %collective-permute-start.40) | collective-permute-done | bytes 73760 | tf_op jit(solution)/shard_map/ppermute | solution.py:527
  139.6 2.0 %collective-permute-done.39.b = f32[144,128]{1,0:T(8,128)S(1)} collective-permute-done((f32[144,128]{1,0:T(8,128)S(1)}, f32[144,128]{1,0:T(8,128)S(1)}, u32[]{:S(2)}, u32[]{:S(2)}) %collective-permute-start.39) | collective-permute-done | bytes 73760 | tf_op jit(solution)/shard_map/ppermute | solution.py:527
  141.6 2.5 %collective-permute-start.44 = (f32[144,128]{1,0:T(8,128)S(1)}, f32[144,128]{1,0:T(8,128)S(1)}, u32[]{:S(2)}, u32[]{:S(2)}) collective-permute-start(f32[144,128]{1,0:T(8,128)S(1)} %shard_map.113.a), channel_id=1, source_target_pairs={{0,96},{32,0},{64,32},{96,64},{1,97},{33,1},{65,33},{97,65},{2,98}... | collective-permute-start | bytes 221192 | tf_op jit(solution)/shard_map/ppermute | solution.py:527
  145.5 3.4 %collective-permute-done.43.c = f32[144,128]{1,0:T(8,128)S(1)} collective-permute-done((f32[144,128]{1,0:T(8,128)S(1)}, f32[144,128]{1,0:T(8,128)S(1)}, u32[]{:S(2)}, u32[]{:S(2)}) %collective-permute-start.43) | collective-permute-done | bytes 73760 | tf_op jit(solution)/shard_map/ppermute | solution.py:527
  148.9 1.1 collective-permute-done.42.b
  150.3 1.6 collective-permute-start.47
  152.3 2.8 %collective-permute-start.45 = (f32[136,128]{1,0:T(8,128)S(1)}, f32[136,128]{1,0:T(8,128)S(1)}, u32[]{:S(2)}, u32[]{:S(2)}) collective-permute-start(f32[136,128]{1,0:T(8,128)S(1)} %get-tuple-element.88.mine), channel_id=1, source_target_pairs={{0,4},{4,0},{1,5},{5,1},{2,6},{6,2},{3,7},{7,3},{8,12},{12,8},{9,1... | collective-permute-start | bytes 208904 | tf_op jit(solution)/shard_map/ppermute | solution.py:536
  156.1 1.4 shard_map.115
  (74 shorter events, 18.1 us)
Async XLA Ops:
  1.4 1.0 copy-start.2
  2.5 0.7 copy-start.3
  5.0 9.9 %collective-permute-start = (f32[264,128]{1,0:T(8,128)S(1)}, f32[264,128]{1,0:T(8,128)S(1)}, u32[]{:S(2)}, u32[]{:S(2)}) collective-permute-start(f32[264,128]{1,0:T(8,128)S(1)} %get-tuple-element.49), channel_id=1, source_target_pairs={{0,1},{1,2},{2,3},{3,0},{4,5},{5,6},{6,7},{7,4},{8,9},{9,10},{10,1... | collective-permute-start | bytes 405512 | tf_op jit(solution)/shard_map/ppermute | solution.py:527
  7.6 9.2 %collective-permute-start.1 = (f32[264,128]{1,0:T(8,128)S(1)}, f32[264,128]{1,0:T(8,128)S(1)}, u32[]{:S(2)}, u32[]{:S(2)}) collective-permute-start(f32[264,128]{1,0:T(8,128)S(1)} %get-tuple-element.50), channel_id=1, source_target_pairs={{0,2},{1,3},{2,0},{3,1},{4,6},{5,7},{6,4},{7,5},{8,10},{9,11},{10,... | collective-permute-start | bytes 405512 | tf_op jit(solution)/shard_map/ppermute | solution.py:527
  10.9 5.9 %collective-permute-start.2 = (f32[264,128]{1,0:T(8,128)S(1)}, f32[264,128]{1,0:T(8,128)S(1)}, u32[]{:S(2)}, u32[]{:S(2)}) collective-permute-start(f32[264,128]{1,0:T(8,128)S(1)} %get-tuple-element.51), channel_id=1, source_target_pairs={{0,3},{1,0},{2,1},{3,2},{4,7},{5,4},{6,5},{7,6},{8,11},{9,8},{10,9... | collective-permute-start | bytes 405512 | tf_op jit(solution)/shard_map/ppermute | solution.py:527
  11.6 1.2 copy-start
  14.1 11.4 %collective-permute-start.6 = (f32[128,256]{1,0:T(8,128)S(1)}, f32[128,256]{1,0:T(8,128)S(1)}, u32[]{:S(2)}, u32[]{:S(2)}) collective-permute-start(f32[128,256]{1,0:T(8,128)S(1)} %get-tuple-element.55), channel_id=1, source_target_pairs={{0,1},{1,2},{2,3},{3,0},{4,5},{5,6},{6,7},{7,4},{8,9},{9,10},{10,1... | collective-permute-start | bytes 393224 | tf_op jit(solution)/shard_map/ppermute | solution.py:527
  20.1 16.8 %collective-permute-start.5 = (f32[264,128]{1,0:T(8,128)S(1)}, f32[264,128]{1,0:T(8,128)S(1)}, u32[]{:S(2)}, u32[]{:S(2)}) collective-permute-start(f32[264,128]{1,0:T(8,128)S(1)} %shard_map.94.e0.packed), channel_id=1, source_target_pairs={{0,3},{1,0},{2,1},{3,2},{4,7},{5,4},{6,5},{7,6},{8,11},{9,8},{10,9... | collective-permute-start | bytes 405512 | tf_op jit(solution)/shard_map/ppermute | solution.py:527
  22.6 14.3 %collective-permute-start.4 = (f32[264,128]{1,0:T(8,128)S(1)}, f32[264,128]{1,0:T(8,128)S(1)}, u32[]{:S(2)}, u32[]{:S(2)}) collective-permute-start(f32[264,128]{1,0:T(8,128)S(1)} %shard_map.94.e0.packed), channel_id=1, source_target_pairs={{0,2},{1,3},{2,0},{3,1},{4,6},{5,7},{6,4},{7,5},{8,10},{9,11},{10,... | collective-permute-start | bytes 405512 | tf_op jit(solution)/shard_map/ppermute | solution.py:527
  23.6 13.3 %collective-permute-start.3 = (f32[264,128]{1,0:T(8,128)S(1)}, f32[264,128]{1,0:T(8,128)S(1)}, u32[]{:S(2)}, u32[]{:S(2)}) collective-permute-start(f32[264,128]{1,0:T(8,128)S(1)} %shard_map.94.e0.packed), channel_id=1, source_target_pairs={{0,1},{1,2},{2,3},{3,0},{4,5},{5,6},{6,7},{7,4},{8,9},{9,10},{10,1... | collective-permute-start | bytes 405512 | tf_op jit(solution)/shard_map/ppermute | solution.py:527
  23.6 9.7 %collective-permute-start.7 = (f32[128,256]{1,0:T(8,128)S(1)}, f32[128,256]{1,0:T(8,128)S(1)}, u32[]{:S(2)}, u32[]{:S(2)}) collective-permute-start(f32[128,256]{1,0:T(8,128)S(1)} %get-tuple-element.56), channel_id=1, source_target_pairs={{0,2},{1,3},{2,0},{3,1},{4,6},{5,7},{6,4},{7,5},{8,10},{9,11},{10,... | collective-permute-start | bytes 393224 | tf_op jit(solution)/shard_map/ppermute | solution.py:527
  25.5 8.4 %collective-permute-start.8 = (f32[128,256]{1,0:T(8,128)S(1)}, f32[128,256]{1,0:T(8,128)S(1)}, u32[]{:S(2)}, u32[]{:S(2)}) collective-permute-start(f32[128,256]{1,0:T(8,128)S(1)} %get-tuple-element.57), channel_id=1, source_target_pairs={{0,3},{1,0},{2,1},{3,2},{4,7},{5,4},{6,5},{7,6},{8,11},{9,8},{10,9... | collective-permute-start | bytes 393224 | tf_op jit(solution)/shard_map/ppermute | solution.py:527
  42.5 12.2 %collective-permute-start.9 = (f32[256,256]{1,0:T(8,128)S(1)}, f32[256,256]{1,0:T(8,128)S(1)}, u32[]{:S(2)}, u32[]{:S(2)}) collective-permute-start(f32[256,256]{1,0:T(8,128)S(1)} %get-tuple-element.59.mine), channel_id=1, source_target_pairs={{0,4},{4,0},{1,5},{5,1},{2,6},{6,2},{3,7},{7,3},{8,12},{12,8},{9,1... | collective-permute-start | bytes 786440 | tf_op jit(solution)/shard_map/ppermute | solution.py:536
  44.4 3.3 %collective-permute-start.12 = (f32[8,256]{1,0:T(8,128)S(1)}, f32[8,256]{1,0:T(8,128)S(1)}, u32[]{:S(2)}, u32[]{:S(2)}) collective-permute-start(f32[8,256]{1,0:T(8,128)S(1)} %get-tuple-element.61.v0), channel_id=1, source_target_pairs={{0,3},{1,0},{2,1},{3,2},{4,7},{5,4},{6,5},{7,6},{8,11},{9,8},{10,9... | collective-permute-start | bytes 24584 | tf_op jit(solution)/shard_map/ppermute | solution.py:527
  46.9 4.0 %collective-permute-start.11 = (f32[8,256]{1,0:T(8,128)S(1)}, f32[8,256]{1,0:T(8,128)S(1)}, u32[]{:S(2)}, u32[]{:S(2)}) collective-permute-start(f32[8,256]{1,0:T(8,128)S(1)} %get-tuple-element.61.v0), channel_id=1, source_target_pairs={{0,2},{1,3},{2,0},{3,1},{4,6},{5,7},{6,4},{7,5},{8,10},{9,11},{10,... | collective-permute-start | bytes 24584 | tf_op jit(solution)/shard_map/ppermute | solution.py:527
  47.1 3.8 %collective-permute-start.10 = (f32[8,256]{1,0:T(8,128)S(1)}, f32[8,256]{1,0:T(8,128)S(1)}, u32[]{:S(2)}, u32[]{:S(2)}) collective-permute-start(f32[8,256]{1,0:T(8,128)S(1)} %get-tuple-element.61.v0), channel_id=1, source_target_pairs={{0,1},{1,2},{2,3},{3,0},{4,5},{5,6},{6,7},{7,4},{8,9},{9,10},{10,1... | collective-permute-start | bytes 24584 | tf_op jit(solution)/shard_map/ppermute | solution.py:527
  51.9 2.8 %collective-permute-start.13 = (f32[8,256]{1,0:T(8,128)S(1)}, f32[8,256]{1,0:T(8,128)S(1)}, u32[]{:S(2)}, u32[]{:S(2)}) collective-permute-start(f32[8,256]{1,0:T(8,128)S(1)} %get-tuple-element.62.v_mine), channel_id=1, source_target_pairs={{0,4},{4,0},{1,5},{5,1},{2,6},{6,2},{3,7},{7,3},{8,12},{12,8},{9,1... | collective-permute-start | bytes 24584 | tf_op jit(solution)/shard_map/ppermute | solution.py:536
  55.6 8.1 %collective-permute-start.16 = (f32[136,256]{1,0:T(8,128)S(1)}, f32[136,256]{1,0:T(8,128)S(1)}, u32[]{:S(2)}, u32[]{:S(2)}) collective-permute-start(f32[136,256]{1,0:T(8,128)S(1)} %get-tuple-element.64), channel_id=1, source_target_pairs={{0,24},{8,0},{16,8},{24,16},{1,25},{9,1},{17,9},{25,17},{2,26},{10... | collective-permute-start | bytes 417800 | tf_op jit(solution)/shard_map/ppermute | solution.py:527
  58.1 6.9 %collective-permute-start.15 = (f32[136,256]{1,0:T(8,128)S(1)}, f32[136,256]{1,0:T(8,128)S(1)}, u32[]{:S(2)}, u32[]{:S(2)}) collective-permute-start(f32[136,256]{1,0:T(8,128)S(1)} %get-tuple-element.64), channel_id=1, source_target_pairs={{0,16},{8,24},{16,0},{24,8},{1,17},{9,25},{17,1},{25,9},{2,18},{10... | collective-permute-start | bytes 417800 | tf_op jit(solution)/shard_map/ppermute | solution.py:527
  58.6 9.6 %collective-permute-start.14 = (f32[136,256]{1,0:T(8,128)S(1)}, f32[136,256]{1,0:T(8,128)S(1)}, u32[]{:S(2)}, u32[]{:S(2)}) collective-permute-start(f32[136,256]{1,0:T(8,128)S(1)} %get-tuple-element.64), channel_id=1, source_target_pairs={{0,8},{8,16},{16,24},{24,0},{1,9},{9,17},{17,25},{25,1},{2,10},{10... | collective-permute-start | bytes 417800 | tf_op jit(solution)/shard_map/ppermute | solution.py:527
  63.6 5.1 %collective-permute-start.19 = (f32[136,256]{1,0:T(8,128)S(1)}, f32[136,256]{1,0:T(8,128)S(1)}, u32[]{:S(2)}, u32[]{:S(2)}) collective-permute-start(f32[136,256]{1,0:T(8,128)S(1)} %collective-permute-done.16.m3), channel_id=1, source_target_pairs={{0,4},{4,0},{1,5},{5,1},{2,6},{6,2},{3,7},{7,3},{8,12},{12,8},{9,1... | collective-permute-start | bytes 417800 | tf_op jit(solution)/shard_map/ppermute | solution.py:536
  65.0 3.7 %collective-permute-start.18 = (f32[136,256]{1,0:T(8,128)S(1)}, f32[136,256]{1,0:T(8,128)S(1)}, u32[]{:S(2)}, u32[]{:S(2)}) collective-permute-start(f32[136,256]{1,0:T(8,128)S(1)} %collective-permute-done.15.m2), channel_id=1, source_target_pairs={{0,4},{4,0},{1,5},{5,1},{2,6},{6,2},{3,7},{7,3},{8,12},{12,8},{9,1... | collective-permute-start | bytes 417800 | tf_op jit(solution)/shard_map/ppermute | solution.py:536
  68.2 1.5 collective-permute-start.17
  71.2 8.3 %collective-permute-start.22 = (f32[136,256]{1,0:T(8,128)S(1)}, f32[136,256]{1,0:T(8,128)S(1)}, u32[]{:S(2)}, u32[]{:S(2)}) collective-permute-start(f32[136,256]{1,0:T(8,128)S(1)} %get-tuple-element.66), channel_id=1, source_target_pairs={{0,96},{32,0},{64,32},{96,64},{1,97},{33,1},{65,33},{97,65},{2,98}... | collective-permute-start | bytes 417800 | tf_op jit(solution)/shard_map/ppermute | solution.py:527
  74.0 6.9 %collective-permute-start.21 = (f32[136,256]{1,0:T(8,128)S(1)}, f32[136,256]{1,0:T(8,128)S(1)}, u32[]{:S(2)}, u32[]{:S(2)}) collective-permute-start(f32[136,256]{1,0:T(8,128)S(1)} %get-tuple-element.66), channel_id=1, source_target_pairs={{0,64},{32,96},{64,0},{96,32},{1,65},{33,97},{65,1},{97,33},{2,66}... | collective-permute-start | bytes 417800 | tf_op jit(solution)/shard_map/ppermute | solution.py:527
  74.3 9.7 %collective-permute-start.20 = (f32[136,256]{1,0:T(8,128)S(1)}, f32[136,256]{1,0:T(8,128)S(1)}, u32[]{:S(2)}, u32[]{:S(2)}) collective-permute-start(f32[136,256]{1,0:T(8,128)S(1)} %get-tuple-element.66), channel_id=1, source_target_pairs={{0,32},{32,64},{64,96},{96,0},{1,33},{33,65},{65,97},{97,1},{2,34}... | collective-permute-start | bytes 417800 | tf_op jit(solution)/shard_map/ppermute | solution.py:527
  75.0 11.1 %collective-permute-start.28 = (f32[128,256]{1,0:T(8,128)S(1)}, f32[128,256]{1,0:T(8,128)S(1)}, u32[]{:S(2)}, u32[]{:S(2)}) collective-permute-start(f32[128,256]{1,0:T(8,128)S(1)} %get-tuple-element.70.p0), channel_id=1, source_target_pairs={{0,3},{1,0},{2,1},{3,2},{4,7},{5,4},{6,5},{7,6},{8,11},{9,8},{10,9... | collective-permute-start | bytes 393224 | tf_op jit(solution)/shard_map/ppermute | solution.py:527
  79.5 14.8 %collective-permute-start.25 = (f32[136,256]{1,0:T(8,128)S(1)}, f32[136,256]{1,0:T(8,128)S(1)}, u32[]{:S(2)}, u32[]{:S(2)}) collective-permute-start(f32[136,256]{1,0:T(8,128)S(1)} %collective-permute-done.22.m3), channel_id=1, source_target_pairs={{0,4},{4,0},{1,5},{5,1},{2,6},{6,2},{3,7},{7,3},{8,12},{12,8},{9,1... | collective-permute-start | bytes 417800 | tf_op jit(solution)/shard_map/ppermute | solution.py:536
  80.9 13.5 %collective-permute-start.24 = (f32[136,256]{1,0:T(8,128)S(1)}, f32[136,256]{1,0:T(8,128)S(1)}, u32[]{:S(2)}, u32[]{:S(2)}) collective-permute-start(f32[136,256]{1,0:T(8,128)S(1)} %collective-permute-done.21.m2), channel_id=1, source_target_pairs={{0,4},{4,0},{1,5},{5,1},{2,6},{6,2},{3,7},{7,3},{8,12},{12,8},{9,1... | collective-permute-start | bytes 417800 | tf_op jit(solution)/shard_map/ppermute | solution.py:536
  84.1 10.3 %collective-permute-start.23 = (f32[136,256]{1,0:T(8,128)S(1)}, f32[136,256]{1,0:T(8,128)S(1)}, u32[]{:S(2)}, u32[]{:S(2)}) collective-permute-start(f32[136,256]{1,0:T(8,128)S(1)} %collective-permute-done.20.m1), channel_id=1, source_target_pairs={{0,4},{4,0},{1,5},{5,1},{2,6},{6,2},{3,7},{7,3},{8,12},{12,8},{9,1... | collective-permute-start | bytes 417800 | tf_op jit(solution)/shard_map/ppermute | solution.py:536
  84.6 6.5 %collective-permute-start.27 = (f32[128,256]{1,0:T(8,128)S(1)}, f32[128,256]{1,0:T(8,128)S(1)}, u32[]{:S(2)}, u32[]{:S(2)}) collective-permute-start(f32[128,256]{1,0:T(8,128)S(1)} %get-tuple-element.70.p0), channel_id=1, source_target_pairs={{0,2},{1,3},{2,0},{3,1},{4,6},{5,7},{6,4},{7,5},{8,10},{9,11},{10,... | collective-permute-start | bytes 393224 | tf_op jit(solution)/shard_map/ppermute | solution.py:527
  86.1 8.2 %collective-permute-start.26 = (f32[128,256]{1,0:T(8,128)S(1)}, f32[128,256]{1,0:T(8,128)S(1)}, u32[]{:S(2)}, u32[]{:S(2)}) collective-permute-start(f32[128,256]{1,0:T(8,128)S(1)} %get-tuple-element.70.p0), channel_id=1, source_target_pairs={{0,1},{1,2},{2,3},{3,0},{4,5},{5,6},{6,7},{7,4},{8,9},{9,10},{10,1... | collective-permute-start | bytes 393224 | tf_op jit(solution)/shard_map/ppermute | solution.py:527
  99.2 1.4 collective-permute-start.29
  101.3 2.5 %collective-permute-start.32 = (f32[8,256]{1,0:T(8,128)S(1)}, f32[8,256]{1,0:T(8,128)S(1)}, u32[]{:S(2)}, u32[]{:S(2)}) collective-permute-start(f32[8,256]{1,0:T(8,128)S(1)} %shard_map.103.q0), channel_id=1, source_target_pairs={{0,24},{8,0},{16,8},{24,16},{1,25},{9,1},{17,9},{25,17},{2,26},{10... | collective-permute-start | bytes 24584 | tf_op jit(solution)/shard_map/ppermute | solution.py:527
  101.6 4.0 %collective-permute-start.31 = (f32[8,256]{1,0:T(8,128)S(1)}, f32[8,256]{1,0:T(8,128)S(1)}, u32[]{:S(2)}, u32[]{:S(2)}) collective-permute-start(f32[8,256]{1,0:T(8,128)S(1)} %shard_map.103.q0), channel_id=1, source_target_pairs={{0,16},{8,24},{16,0},{24,8},{1,17},{9,25},{17,1},{25,9},{2,18},{10... | collective-permute-start | bytes 24584 | tf_op jit(solution)/shard_map/ppermute | solution.py:527
  102.1 4.1 %collective-permute-start.30 = (f32[8,256]{1,0:T(8,128)S(1)}, f32[8,256]{1,0:T(8,128)S(1)}, u32[]{:S(2)}, u32[]{:S(2)}) collective-permute-start(f32[8,256]{1,0:T(8,128)S(1)} %shard_map.103.q0), channel_id=1, source_target_pairs={{0,8},{8,16},{16,24},{24,0},{1,9},{9,17},{17,25},{25,1},{2,10},{10... | collective-permute-start | bytes 24584 | tf_op jit(solution)/shard_map/ppermute | solution.py:527
  107.1 3.3 %collective-permute-start.35 = (f32[8,256]{1,0:T(8,128)S(1)}, f32[8,256]{1,0:T(8,128)S(1)}, u32[]{:S(2)}, u32[]{:S(2)}) collective-permute-start(f32[8,256]{1,0:T(8,128)S(1)} %get-tuple-element.74.gy0), channel_id=1, source_target_pairs={{0,96},{32,0},{64,32},{96,64},{1,97},{33,1},{65,33},{97,65},{2,98}... | collective-permute-start | bytes 24584 | tf_op jit(solution)/shard_map/ppermute | solution.py:527
  108.0 4.0 %collective-permute-start.34 = (f32[8,256]{1,0:T(8,128)S(1)}, f32[8,256]{1,0:T(8,128)S(1)}, u32[]{:S(2)}, u32[]{:S(2)}) collective-permute-start(f32[8,256]{1,0:T(8,128)S(1)} %get-tuple-element.74.gy0), channel_id=1, source_target_pairs={{0,64},{32,96},{64,0},{96,32},{1,65},{33,97},{65,1},{97,33},{2,66}... | collective-permute-start | bytes 24584 | tf_op jit(solution)/shard_map/ppermute | solution.py:527
  108.0 4.1 %collective-permute-start.33 = (f32[8,256]{1,0:T(8,128)S(1)}, f32[8,256]{1,0:T(8,128)S(1)}, u32[]{:S(2)}, u32[]{:S(2)}) collective-permute-start(f32[8,256]{1,0:T(8,128)S(1)} %get-tuple-element.74.gy0), channel_id=1, source_target_pairs={{0,32},{32,64},{64,96},{96,0},{1,33},{33,65},{65,97},{97,1},{2,34}... | collective-permute-start | bytes 24584 | tf_op jit(solution)/shard_map/ppermute | solution.py:527
  112.1 4.8 %copy-start.1 = (bf16[512,1024]{1,0:T(8,128)(2,1)S(1)}, bf16[512,1024]{1,0:T(8,128)(2,1)}, u32[]{:S(2)}) copy-start(bf16[512,1024]{1,0:T(8,128)(2,1)} %observed.5) | copy-start | bytes 3145732
  118.2 4.8 %collective-permute-start.36 = (f32[16,64,128]{2,1,0:T(8,128)S(1)}, f32[16,64,128]{2,1,0:T(8,128)S(1)}, u32[]{:S(2)}, u32[]{:S(2)}) collective-permute-start(f32[16,64,128]{2,1,0:T(8,128)S(1)} %get-tuple-element.85), channel_id=1, source_target_pairs={{0,4},{4,0},{1,5},{5,1},{2,6},{6,2},{3,7},{7,3},{8,12},{12,8},{9,1... | collective-permute-start | bytes 1572872 | tf_op jit(solution)/shard_map/ppermute | solution.py:536
  123.9 5.2 %copy-start.4 = (s32[8]{0:T(128)S(1)}, s32[8]{0:T(128)}, u32[]{:S(2)}) copy-start(s32[8]{0:T(128)} %panel_of.1) | copy-start | bytes 100
  123.9 33.5 %all-to-all-start = ((f32[16,64,128]{2,1,0:T(8,128)}), f32[16,64,128]{2,1,0:T(8,128)S(1)}, u32[]{:S(2)}, u32[]{:S(2)}) async-start(f32[16,64,128]{2,1,0:T(8,128)} %shard_map.108), calls=%async_computation | async-start | bytes 1048576 | tf_op jit(solution)/shard_map/all_to_all | solution.py:621
  128.2 3.6 %collective-permute-start.37 = (f32[136,128]{1,0:T(8,128)S(1)}, f32[136,128]{1,0:T(8,128)S(1)}, u32[]{:S(2)}, u32[]{:S(2)}) collective-permute-start(f32[136,128]{1,0:T(8,128)S(1)} %get-tuple-element.87), channel_id=1, source_target_pairs={{0,4},{4,0},{1,5},{5,1},{2,6},{6,2},{3,7},{7,3},{8,12},{12,8},{9,1... | collective-permute-start | bytes 208904 | tf_op jit(solution)/shard_map/ppermute | solution.py:536
  130.5 1.2 collective-permute-start.38
  131.8 5.4 %collective-permute-start.41 = (f32[144,128]{1,0:T(8,128)S(1)}, f32[144,128]{1,0:T(8,128)S(1)}, u32[]{:S(2)}, u32[]{:S(2)}) collective-permute-start(f32[144,128]{1,0:T(8,128)S(1)} %shard_map.112.a), channel_id=1, source_target_pairs={{0,24},{8,0},{16,8},{24,16},{1,25},{9,1},{17,9},{25,17},{2,26},{10... | collective-permute-start | bytes 221192 | tf_op jit(solution)/shard_map/ppermute | solution.py:527
  134.6 5.0 %collective-permute-start.40 = (f32[144,128]{1,0:T(8,128)S(1)}, f32[144,128]{1,0:T(8,128)S(1)}, u32[]{:S(2)}, u32[]{:S(2)}) collective-permute-start(f32[144,128]{1,0:T(8,128)S(1)} %shard_map.112.a), channel_id=1, source_target_pairs={{0,16},{8,24},{16,0},{24,8},{1,17},{9,25},{17,1},{25,9},{2,18},{10... | collective-permute-start | bytes 221192 | tf_op jit(solution)/shard_map/ppermute | solution.py:527
  135.2 6.4 %collective-permute-start.39 = (f32[144,128]{1,0:T(8,128)S(1)}, f32[144,128]{1,0:T(8,128)S(1)}, u32[]{:S(2)}, u32[]{:S(2)}) collective-permute-start(f32[144,128]{1,0:T(8,128)S(1)} %shard_map.112.a), channel_id=1, source_target_pairs={{0,8},{8,16},{16,24},{24,0},{1,9},{9,17},{17,25},{25,1},{2,10},{10... | collective-permute-start | bytes 221192 | tf_op jit(solution)/shard_map/ppermute | solution.py:527
  141.6 3.9 %collective-permute-start.44 = (f32[144,128]{1,0:T(8,128)S(1)}, f32[144,128]{1,0:T(8,128)S(1)}, u32[]{:S(2)}, u32[]{:S(2)}) collective-permute-start(f32[144,128]{1,0:T(8,128)S(1)} %shard_map.113.a), channel_id=1, source_target_pairs={{0,96},{32,0},{64,32},{96,64},{1,97},{33,1},{65,33},{97,65},{2,98}... | collective-permute-start | bytes 221192 | tf_op jit(solution)/shard_map/ppermute | solution.py:527
  144.1 4.8 %collective-permute-start.43 = (f32[144,128]{1,0:T(8,128)S(1)}, f32[144,128]{1,0:T(8,128)S(1)}, u32[]{:S(2)}, u32[]{:S(2)}) collective-permute-start(f32[144,128]{1,0:T(8,128)S(1)} %shard_map.113.a), channel_id=1, source_target_pairs={{0,64},{32,96},{64,0},{96,32},{1,65},{33,97},{65,1},{97,33},{2,66}... | collective-permute-start | bytes 221192 | tf_op jit(solution)/shard_map/ppermute | solution.py:527
  144.7 5.3 %collective-permute-start.42 = (f32[144,128]{1,0:T(8,128)S(1)}, f32[144,128]{1,0:T(8,128)S(1)}, u32[]{:S(2)}, u32[]{:S(2)}) collective-permute-start(f32[144,128]{1,0:T(8,128)S(1)} %shard_map.113.a), channel_id=1, source_target_pairs={{0,32},{32,64},{64,96},{96,0},{1,33},{33,65},{65,97},{97,1},{2,34}... | collective-permute-start | bytes 221192 | tf_op jit(solution)/shard_map/ppermute | solution.py:527
  149.9 5.1 %collective-permute-start.48 = (f32[8,128]{1,0:T(8,128)S(1)}, f32[8,128]{1,0:T(8,128)S(1)}, u32[]{:S(2)}, u32[]{:S(2)}) collective-permute-start(f32[8,128]{1,0:T(8,128)S(1)} %get-tuple-element.89.s0), channel_id=1, source_target_pairs={{0,3},{1,0},{2,1},{3,2},{4,7},{5,4},{6,5},{7,6},{8,11},{9,8},{10,9... | collective-permute-start | bytes 12296 | tf_op jit(solution)/shard_map/ppermute | solution.py:527
  150.3 4.8 %collective-permute-start.47 = (f32[8,128]{1,0:T(8,128)S(1)}, f32[8,128]{1,0:T(8,128)S(1)}, u32[]{:S(2)}, u32[]{:S(2)}) collective-permute-start(f32[8,128]{1,0:T(8,128)S(1)} %get-tuple-element.89.s0), channel_id=1, source_target_pairs={{0,2},{1,3},{2,0},{3,1},{4,6},{5,7},{6,4},{7,5},{8,10},{9,11},{10,... | collective-permute-start | bytes 12296 | tf_op jit(solution)/shard_map/ppermute | solution.py:527
  151.9 3.7 %collective-permute-start.46 = (f32[8,128]{1,0:T(8,128)S(1)}, f32[8,128]{1,0:T(8,128)S(1)}, u32[]{:S(2)}, u32[]{:S(2)}) collective-permute-start(f32[8,128]{1,0:T(8,128)S(1)} %get-tuple-element.89.s0), channel_id=1, source_target_pairs={{0,1},{1,2},{2,3},{3,0},{4,5},{5,6},{6,7},{7,4},{8,9},{9,10},{10,1... | collective-permute-start | bytes 12296 | tf_op jit(solution)/shard_map/ppermute | solution.py:527
  152.3 3.7 %collective-permute-start.45 = (f32[136,128]{1,0:T(8,128)S(1)}, f32[136,128]{1,0:T(8,128)S(1)}, u32[]{:S(2)}, u32[]{:S(2)}) collective-permute-start(f32[136,128]{1,0:T(8,128)S(1)} %get-tuple-element.88.mine), channel_id=1, source_target_pairs={{0,4},{4,0},{1,5},{5,1},{2,6},{6,2},{3,7},{7,3},{8,12},{12,8},{9,1... | collective-permute-start | bytes 208904 | tf_op jit(solution)/shard_map/ppermute | solution.py:536

commit v4 on v3

--- a/solution.py
+++ b/solution.py
@@ -28,6 +28,12 @@
 
 def dot(a, b, dims=((1,), (0,))):
     return lax.dot_general(a, b, (dims, ((), ())), preferred_element_type=F32)
+
+
+def stacked(parts, b):
+    rows = parts[0].shape[0]
+    both = dot(jnp.concatenate(parts, axis=0), b)
+    return both[:rows] + both[rows:]
 
 
 def dot3(a, b, dims=((1,), (0,))):
@@ -87,7 +93,7 @@
     high, low = split(coef.T.astype(F32) * inv_noise)
     for k, out in enumerate(outs):
         kept = table[pl.ds(lax.rem(place[3] + k, len(outs)), 1), :].astype(BF16)
-        store_packed(out, dot(high * kept, coef) + dot(low * kept, coef))
+        store_packed(out, stacked((high * kept, low * kept), coef))
 
 
 def project_kernel(place, table, loads, observed, *outs):
@@ -95,8 +101,7 @@
     for k in range(len(outs)):
         b = lax.rem(place[3] + k, len(outs))
         rows = observed[pl.ds(pl.multiple_of(b * BLOCK, BLOCK), BLOCK), :].astype(F32)
-        hi, lo = split(rows * table[pl.ds(8 + b, 1), :])
-        outs[k][...] = dot(hi, coef) + dot(lo, coef)
+        outs[k][...] = stacked(split(rows * table[pl.ds(8 + b, 1), :]), coef)
 
 
 def turn_kernel(loads, out):
@@ -432,7 +437,7 @@
     squares = jnp.zeros((1, series), F32)
     for b in range(nb):
         part = slice(b * BLOCK, (b + 1) * BLOCK)
-        miss = observed[part, :].astype(F32) - (dot(high[part, :], coef) + dot(low[part, :], coef))
+        miss = observed[part, :].astype(F32) - stacked((high[part, :], low[part, :]), coef)
         squares = squares + jnp.sum(miss * miss, axis=0, keepdims=True) * weight[b : b + 1]
     counts = float(BLOCK) * jnp.sum(weight, axis=0, keepdims=True)
     lane = lax.broadcasted_iota(jnp.int32, (8, n), 1)

time: 161 us -> 161 us (level)
  no operation moved by 1% of the time
where the time goes in v4:
time: 161 us; the launch traced here: 158 us
  starting transfers between devices  63.1 us (39%)
  waiting for transfers between devices  49.9 us (31%)
  Pallas kernels  39.9 us (25%)
  local copies, waits for them, and re-layouts  3.52 us (2%)
    ppermute x36, waiting for transfers between devices, from_peers(): out[k] = lax.ppermute(arrays[k], axis, [(i, (i + k) % n) for i in range(n)])  44.5 us
    ppermute x36, starting transfers between devices, from_peers(): out[k] = lax.ppermute(arrays[k], axis, [(i, (i + k) % n) for i in range(n)])  40.2 us
    pallas_call x24, Pallas kernels, call(): return made(*args)  39.9 us
    ppermute x13, starting transfers between devices, swap(): return lax.ppermute(array, axis, [(0, 1), (1, 0)])  18.6 us
    ppermute x13, waiting for transfers between devices, swap(): return lax.ppermute(array, axis, [(0, 1), (1, 0)])  5.36 us
    all_to_all x1, starting transfers between devices, step(): arrived = lax.all_to_all(spread, (ay, ax), 0, 0, tiled=True)  4.24 us
  transfers between devices with their start and end apart: 50, of which 28 were waited for; matrix products, arithmetic and copies ran while one was open for 0% of the time, Pallas kernels for 10%

profile of v4, /device:TPU:1, one launch (start us, length us, event | category | flops | bytes accessed | tf_op | source)
XLA Modules:
  0.0 158.0 jit_solution(6572150494344571471)
XLA Ops:
  1.4 1.0 copy-done.2
  3.2 1.8 %shard_map.93 = (f32[16,1024]{1,0:T(8,128)S(1)}, bf16[1024,256]{1,0:T(8,128)(2,1)S(1)}, f32[264,128]{1,0:T(8,128)S(1)}, f32[264,128]{1,0:T(8,128)S(1)}, f32[264,128]{1,0:T(8,128)S(1)}, /*index=5*/f32[264,128]{1,0:T(8,128)S(1)}) custom-call(s32[4]{0:T(128)S(1)} %pad_add_fusion.place, s32[4,1024]{1,0:T(4,128)S(1)} %copy-done.3, f32[1,1280]{1,0:T(1,128)S(1)} %reshape.11.both, ...), custom_call_target="tpu_custom_call" | custom-call | tf_op jit(solution)/shard_map/pallas_call | solution.py:525
  5.0 2.5 %collective-permute-start = (f32[264,128]{1,0:T(8,128)S(1)}, f32[264,128]{1,0:T(8,128)S(1)}, u32[]{:S(2)}, u32[]{:S(2)}) collective-permute-start(f32[264,128]{1,0:T(8,128)S(1)} %get-tuple-element.49), channel_id=1, source_target_pairs={{0,1},{1,2},{2,3},{3,0},{4,5},{5,6},{6,7},{7,4},{8,9},{9,10},{10,1... | collective-permute-start | bytes 405512 | tf_op jit(solution)/shard_map/ppermute | solution.py:532
  7.6 3.3 %collective-permute-start.1 = (f32[264,128]{1,0:T(8,128)S(1)}, f32[264,128]{1,0:T(8,128)S(1)}, u32[]{:S(2)}, u32[]{:S(2)}) collective-permute-start(f32[264,128]{1,0:T(8,128)S(1)} %get-tuple-element.50), channel_id=1, source_target_pairs={{0,2},{1,3},{2,0},{3,1},{4,6},{5,7},{6,4},{7,5},{8,10},{9,11},{10,... | collective-permute-start | bytes 405512 | tf_op jit(solution)/shard_map/ppermute | solution.py:532
  11.6 1.2 copy-done
  12.8 1.3 shard_map.96
  14.9 1.9 %collective-permute-done.1.g2 = f32[264,128]{1,0:T(8,128)S(1)} collective-permute-done((f32[264,128]{1,0:T(8,128)S(1)}, f32[264,128]{1,0:T(8,128)S(1)}, u32[]{:S(2)}, u32[]{:S(2)}) %collective-permute-start.1) | collective-permute-done | bytes 135200 | tf_op jit(solution)/shard_map/ppermute | solution.py:532
  16.8 3.3 %shard_map.94.e0.packed = f32[264,128]{1,0:T(8,128)S(1)} custom-call(f32[16,1024]{1,0:T(8,128)S(1)} %get-tuple-element.47.table, f32[264,128]{1,0:T(8,128)S(1)} %get-tuple-element.48.g0, f32[264,128]{1,0:T(8,128)S(1)} %collective-permute-done.g1, f32[264,128]{1,0:T(8,128)S(1)} %collective-permute-done.1.g2, f32[264,128]{1,0:T(8,128)S(1)} %collective-permute-done.2.g3), custom_call_target="tpu_custom_call" | custom-call | tf_op jit(solution)/shard_map/pallas_call | solution.py:525
  20.1 2.5 %collective-permute-start.5 = (f32[264,128]{1,0:T(8,128)S(1)}, f32[264,128]{1,0:T(8,128)S(1)}, u32[]{:S(2)}, u32[]{:S(2)}) collective-permute-start(f32[264,128]{1,0:T(8,128)S(1)} %shard_map.94.e0.packed), channel_id=1, source_target_pairs={{0,3},{1,0},{2,1},{3,2},{4,7},{5,4},{6,5},{7,6},{8,11},{9,8},{10,9... | collective-permute-start | bytes 405512 | tf_op jit(solution)/shard_map/ppermute | solution.py:532
  22.6 1.0 collective-permute-start.4
  23.6 1.9 %collective-permute-start.7 = (f32[128,256]{1,0:T(8,128)S(1)}, f32[128,256]{1,0:T(8,128)S(1)}, u32[]{:S(2)}, u32[]{:S(2)}) collective-permute-start(f32[128,256]{1,0:T(8,128)S(1)} %get-tuple-element.56), channel_id=1, source_target_pairs={{0,2},{1,3},{2,0},{3,1},{4,6},{5,7},{6,4},{7,5},{8,10},{9,11},{10,... | collective-permute-start | bytes 393224 | tf_op jit(solution)/shard_map/ppermute | solution.py:532
  25.5 2.1 %collective-permute-start.8 = (f32[128,256]{1,0:T(8,128)S(1)}, f32[128,256]{1,0:T(8,128)S(1)}, u32[]{:S(2)}, u32[]{:S(2)}) collective-permute-start(f32[128,256]{1,0:T(8,128)S(1)} %get-tuple-element.57), channel_id=1, source_target_pairs={{0,3},{1,0},{2,1},{3,2},{4,7},{5,4},{6,5},{7,6},{8,11},{9,8},{10,9... | collective-permute-start | bytes 393224 | tf_op jit(solution)/shard_map/ppermute | solution.py:532
  27.6 5.7 %collective-permute-done.7.p2 = f32[128,256]{1,0:T(8,128)S(1)} collective-permute-done((f32[128,256]{1,0:T(8,128)S(1)}, f32[128,256]{1,0:T(8,128)S(1)}, u32[]{:S(2)}, u32[]{:S(2)}) %collective-permute-start.7) | collective-permute-done | bytes 131104 | tf_op jit(solution)/shard_map/ppermute | solution.py:532
  34.0 2.9 %shard_map.97 = (f32[128,256]{1,0:T(8,128)S(1)}, f32[8,256]{1,0:T(8,128)S(1)}) custom-call(f32[16,1024]{1,0:T(8,128)S(1)} %get-tuple-element.47.table, f32[264,128]{1,0:T(8,128)S(1)} %shard_map.94.e0.packed, f32[128,256]{1,0:T(8,128)S(1)} %get-tuple-element.54.p0, f32[128,256]{1,0:T(8,128)S(1)} %collective-permute-done.6.p1, ...), custom_call_target="tpu_custom_call" | custom-call | tf_op jit(solution)/shard_map/pallas_call | solution.py:525
  36.9 5.6 %shard_map.95 = (bf16[28,256,256]{2,1,0:T(8,128)(2,1)S(1)}, bf16[28,256,256]{2,1,0:T(8,128)(2,1)S(1)}, f32[4,256,256]{2,1,0:T(8,128)S(1)}, f32[256,256]{1,0:T(8,128)S(1)}) custom-call(s32[4]{0:T(128)S(1)} %pad_add_fusion.place, f32[264,128]{1,0:T(8,128)S(1)} %shard_map.94.e0.packed, f32[264,128]{1,0:T(8,128)S(1)} %collective-permute-done.3.e1, ...), custom_call_target="tpu_custom_call" | custom-call | tf_op jit(solution)/shard_map/pallas_call | solution.py:525
  42.5 1.9 %collective-permute-start.9 = (f32[256,256]{1,0:T(8,128)S(1)}, f32[256,256]{1,0:T(8,128)S(1)}, u32[]{:S(2)}, u32[]{:S(2)}) collective-permute-start(f32[256,256]{1,0:T(8,128)S(1)} %get-tuple-element.59.mine), channel_id=1, source_target_pairs={{0,4},{4,0},{1,5},{5,1},{2,6},{6,2},{3,7},{7,3},{8,12},{12,8},{9,1... | collective-permute-start | bytes 786440 | tf_op jit(solution)/shard_map/ppermute | solution.py:541
  44.4 2.5 %collective-permute-start.12 = (f32[8,256]{1,0:T(8,128)S(1)}, f32[8,256]{1,0:T(8,128)S(1)}, u32[]{:S(2)}, u32[]{:S(2)}) collective-permute-start(f32[8,256]{1,0:T(8,128)S(1)} %get-tuple-element.61.v0), channel_id=1, source_target_pairs={{0,3},{1,0},{2,1},{3,2},{4,7},{5,4},{6,5},{7,6},{8,11},{9,8},{10,9... | collective-permute-start | bytes 24584 | tf_op jit(solution)/shard_map/ppermute | solution.py:532
  47.7 3.2 %collective-permute-done.11.v2 = f32[8,256]{1,0:T(8,128)S(1)} collective-permute-done((f32[8,256]{1,0:T(8,128)S(1)}, f32[8,256]{1,0:T(8,128)S(1)}, u32[]{:S(2)}, u32[]{:S(2)}) %collective-permute-start.11) | collective-permute-done | bytes 8224 | tf_op jit(solution)/shard_map/ppermute | solution.py:532
  50.9 0.9 shard_map.98
  51.9 2.0 %collective-permute-start.13 = (f32[8,256]{1,0:T(8,128)S(1)}, f32[8,256]{1,0:T(8,128)S(1)}, u32[]{:S(2)}, u32[]{:S(2)}) collective-permute-start(f32[8,256]{1,0:T(8,128)S(1)} %get-tuple-element.62.v_mine), channel_id=1, source_target_pairs={{0,4},{4,0},{1,5},{5,1},{2,6},{6,2},{3,7},{7,3},{8,12},{12,8},{9,1... | collective-permute-start | bytes 24584 | tf_op jit(solution)/shard_map/ppermute | solution.py:541
  53.9 0.8 collective-permute-done.13.v_other
  54.7 0.9 shard_map.99
  55.6 2.6 %collective-permute-start.16 = (f32[136,256]{1,0:T(8,128)S(1)}, f32[136,256]{1,0:T(8,128)S(1)}, u32[]{:S(2)}, u32[]{:S(2)}) collective-permute-start(f32[136,256]{1,0:T(8,128)S(1)} %get-tuple-element.64), channel_id=1, source_target_pairs={{0,24},{8,0},{16,8},{24,16},{1,25},{9,1},{17,9},{25,17},{2,26},{10... | collective-permute-start | bytes 417800 | tf_op jit(solution)/shard_map/ppermute | solution.py:532
  59.2 4.4 %collective-permute-done.16.m3 = f32[136,256]{1,0:T(8,128)S(1)} collective-permute-done((f32[136,256]{1,0:T(8,128)S(1)}, f32[136,256]{1,0:T(8,128)S(1)}, u32[]{:S(2)}, u32[]{:S(2)}) %collective-permute-start.16) | collective-permute-done | bytes 139296 | tf_op jit(solution)/shard_map/ppermute | solution.py:532
  63.6 1.4 collective-permute-start.19
  65.0 1.8 %collective-permute-start.18 = (f32[136,256]{1,0:T(8,128)S(1)}, f32[136,256]{1,0:T(8,128)S(1)}, u32[]{:S(2)}, u32[]{:S(2)}) collective-permute-start(f32[136,256]{1,0:T(8,128)S(1)} %collective-permute-done.15.m2), channel_id=1, source_target_pairs={{0,4},{4,0},{1,5},{5,1},{2,6},{6,2},{3,7},{7,3},{8,12},{12,8},{9,1... | collective-permute-start | bytes 417800 | tf_op jit(solution)/shard_map/ppermute | solution.py:541
  66.8 1.4 collective-permute-done.14.m1
  68.7 1.0 collective-permute-done.17.o1
  69.7 1.5 shard_map.100
  71.2 2.8 %collective-permute-start.22 = (f32[136,256]{1,0:T(8,128)S(1)}, f32[136,256]{1,0:T(8,128)S(1)}, u32[]{:S(2)}, u32[]{:S(2)}) collective-permute-start(f32[136,256]{1,0:T(8,128)S(1)} %get-tuple-element.66), channel_id=1, source_target_pairs={{0,96},{32,0},{64,32},{96,64},{1,97},{33,1},{65,33},{97,65},{2,98}... | collective-permute-start | bytes 417800 | tf_op jit(solution)/shard_map/ppermute | solution.py:532
  75.2 4.4 %collective-permute-done.22.m3 = f32[136,256]{1,0:T(8,128)S(1)} collective-permute-done((f32[136,256]{1,0:T(8,128)S(1)}, f32[136,256]{1,0:T(8,128)S(1)}, u32[]{:S(2)}, u32[]{:S(2)}) %collective-permute-start.22) | collective-permute-done | bytes 139296 | tf_op jit(solution)/shard_map/ppermute | solution.py:532
  79.5 1.3 collective-permute-start.25
  80.9 1.9 %collective-permute-start.24 = (f32[136,256]{1,0:T(8,128)S(1)}, f32[136,256]{1,0:T(8,128)S(1)}, u32[]{:S(2)}, u32[]{:S(2)}) collective-permute-start(f32[136,256]{1,0:T(8,128)S(1)} %collective-permute-done.21.m2), channel_id=1, source_target_pairs={{0,4},{4,0},{1,5},{5,1},{2,6},{6,2},{3,7},{7,3},{8,12},{12,8},{9,1... | collective-permute-start | bytes 417800 | tf_op jit(solution)/shard_map/ppermute | solution.py:541
  82.7 1.4 collective-permute-done.20.m1
  84.6 1.5 collective-permute-start.27
  86.1 3.0 %shard_map.101 = (f32[4,264,256]{2,1,0:T(8,128)S(1)}, f32[4,256,256]{2,1,0:T(8,128)S(1)}) custom-call(s32[4]{0:T(128)S(1)} %pad_add_fusion.place, f32[4,264,256]{2,1,0:T(8,128)S(1)} %get-tuple-element.67.xs, f32[256,256]{1,0:T(8,128)S(1)} %collective-permute-done.9.other, f32[8,256]{1,0:T(8,128)S(1)} %collective-permute-done.13.v_other, ...), custom_call_target="tpu_custom_call" | custom-call | tf_op jit(solution)/shard_map/pallas_call | solution.py:525
  89.0 2.1 %collective-permute-done.27.p2 = f32[128,256]{1,0:T(8,128)S(1)} collective-permute-done((f32[128,256]{1,0:T(8,128)S(1)}, f32[128,256]{1,0:T(8,128)S(1)}, u32[]{:S(2)}, u32[]{:S(2)}) %collective-permute-start.27) | collective-permute-done | bytes 131104 | tf_op jit(solution)/shard_map/ppermute | solution.py:532
  91.1 3.2 %collective-permute-done.26.p1 = f32[128,256]{1,0:T(8,128)S(1)} collective-permute-done((f32[128,256]{1,0:T(8,128)S(1)}, f32[128,256]{1,0:T(8,128)S(1)}, u32[]{:S(2)}, u32[]{:S(2)}) %collective-permute-start.26) | collective-permute-done | bytes 131104 | tf_op jit(solution)/shard_map/ppermute | solution.py:532
  94.3 4.8 %shard_map.102 = (f32[4,128,256]{2,1,0:T(8,128)S(1)}, f32[4,128,256]{2,1,0:T(8,128)S(1)}, f32[4,8,256]{2,1,0:T(8,128)S(1)}, f32[8,256]{1,0:T(8,128)S(1)}, f32[4,264,256]{2,1,0:T(8,128)S(1)}) custom-call(s32[4]{0:T(128)S(1)} %pad_add_fusion.place, f32[16,1024]{1,0:T(8,128)S(1)} %get-tuple-element.47.table, f32[264,256]{1,0:T(8,128)S(1)} %get-tuple-element.65.own, ...), custom_call_target="tpu_custom_call" | custom-call | tf_op jit(solution)/shard_map/pallas_call | solution.py:525
  99.7 0.8 collective-permute-done.29.far
  102.7 1.0 collective-permute-done.32.q3
  103.8 1.8 %collective-permute-done.31.q2 = f32[8,256]{1,0:T(8,128)S(1)} collective-permute-done((f32[8,256]{1,0:T(8,128)S(1)}, f32[8,256]{1,0:T(8,128)S(1)}, u32[]{:S(2)}, u32[]{:S(2)}) %collective-permute-start.31) | collective-permute-done | bytes 8224 | tf_op jit(solution)/shard_map/ppermute | solution.py:532
  106.2 1.0 shard_map.104
  107.1 0.9 collective-permute-start.35
  108.7 1.7 %shard_map.105.offsets = f32[4,8,256]{2,1,0:T(8,128)S(1)} custom-call(s32[4]{0:T(128)S(1)} %pad_add_fusion.place, f32[4,8,256]{2,1,0:T(8,128)S(1)} %get-tuple-element.77.qs, f32[4,264,256]{2,1,0:T(8,128)S(1)} %get-tuple-element.67.xs, f32[8,256]{1,0:T(8,128)S(1)} %collective-permute-done.29.far, f32[256,256]{1,0:T(8,128)S(1)} %collective-permute-done.9.other, ...), custom_call_target="tpu_custom_call" | custom-call | tf_op jit(solution)/shard_map/pallas_call | solution.py:525
  110.4 1.6 collective-permute-done.34.gy2
  112.1 4.8 %shard_map.106 = (f32[512,256]{1,0:T(8,128)}, bf16[512,256]{1,0:T(8,128)(2,1)S(1)}, bf16[512,256]{1,0:T(8,128)(2,1)S(1)}, f32[136,128]{1,0:T(8,128)S(1)}, f32[136,128]{1,0:T(8,128)S(1)}) custom-call(s32[4]{0:T(128)S(1)} %pad_add_fusion.place, f32[16,1024]{1,0:T(8,128)S(1)} %get-tuple-element.47.table, f32[8,256]{1,0:T(8,128)S(1)} %get-tuple-element.74.gy0, ...), custom_call_target="tpu_custom_call" | custom-call | tf_op jit(solution)/shard_map/pallas_call | solution.py:525
  116.9 1.3 shard_map.107
  118.2 3.3 %collective-permute-start.36 = (f32[16,64,128]{2,1,0:T(8,128)S(1)}, f32[16,64,128]{2,1,0:T(8,128)S(1)}, u32[]{:S(2)}, u32[]{:S(2)}) collective-permute-start(f32[16,64,128]{2,1,0:T(8,128)S(1)} %get-tuple-element.85), channel_id=1, source_target_pairs={{0,4},{4,0},{1,5},{5,1},{2,6},{6,2},{3,7},{7,3},{8,12},{12,8},{9,1... | collective-permute-start | bytes 1572872 | tf_op jit(solution)/shard_map/ppermute | solution.py:541
  121.5 1.5 collective-permute-done.36.b
  123.1 0.9 shard_map.108
  123.9 4.2 %all-to-all-start = ((f32[16,64,128]{2,1,0:T(8,128)}), f32[16,64,128]{2,1,0:T(8,128)S(1)}, u32[]{:S(2)}, u32[]{:S(2)}) async-start(f32[16,64,128]{2,1,0:T(8,128)} %shard_map.108), calls=%async_computation | async-start | bytes 1048576 | tf_op jit(solution)/shard_map/all_to_all | solution.py:626
  129.1 1.3 shard_map.111.s
  130.6 1.2 collective-permute-done.38.s_far
  131.7 2.8 %collective-permute-start.41 = (f32[144,128]{1,0:T(8,128)S(1)}, f32[144,128]{1,0:T(8,128)S(1)}, u32[]{:S(2)}, u32[]{:S(2)}) collective-permute-start(f32[144,128]{1,0:T(8,128)S(1)} %shard_map.112.a), channel_id=1, source_target_pairs={{0,24},{8,0},{16,8},{24,16},{1,25},{9,1},{17,9},{25,17},{2,26},{10... | collective-permute-start | bytes 221192 | tf_op jit(solution)/shard_map/ppermute | solution.py:532
  135.7 1.4 collective-permute-done.41.d
  137.2 2.4 %collective-permute-done.40.c = f32[144,128]{1,0:T(8,128)S(1)} collective-permute-done((f32[144,128]{1,0:T(8,128)S(1)}, f32[144,128]{1,0:T(8,128)S(1)}, u32[]{:S(2)}, u32[]{:S(2)}) %collective-permute-start.40) | collective-permute-done | bytes 73760 | tf_op jit(solution)/shard_map/ppermute | solution.py:532
  139.6 2.0 %collective-permute-done.39.b = f32[144,128]{1,0:T(8,128)S(1)} collective-permute-done((f32[144,128]{1,0:T(8,128)S(1)}, f32[144,128]{1,0:T(8,128)S(1)}, u32[]{:S(2)}, u32[]{:S(2)}) %collective-permute-start.39) | collective-permute-done | bytes 73760 | tf_op jit(solution)/shard_map/ppermute | solution.py:532
  141.6 2.5 %collective-permute-start.44 = (f32[144,128]{1,0:T(8,128)S(1)}, f32[144,128]{1,0:T(8,128)S(1)}, u32[]{:S(2)}, u32[]{:S(2)}) collective-permute-start(f32[144,128]{1,0:T(8,128)S(1)} %shard_map.113.a), channel_id=1, source_target_pairs={{0,96},{32,0},{64,32},{96,64},{1,97},{33,1},{65,33},{97,65},{2,98}... | collective-permute-start | bytes 221192 | tf_op jit(solution)/shard_map/ppermute | solution.py:532
  145.4 3.4 %collective-permute-done.43.c = f32[144,128]{1,0:T(8,128)S(1)} collective-permute-done((f32[144,128]{1,0:T(8,128)S(1)}, f32[144,128]{1,0:T(8,128)S(1)}, u32[]{:S(2)}, u32[]{:S(2)}) %collective-permute-start.43) | collective-permute-done | bytes 73760 | tf_op jit(solution)/shard_map/ppermute | solution.py:532
  148.8 1.1 collective-permute-done.42.b
  150.2 1.6 collective-permute-start.47
  152.3 2.8 %collective-permute-start.45 = (f32[136,128]{1,0:T(8,128)S(1)}, f32[136,128]{1,0:T(8,128)S(1)}, u32[]{:S(2)}, u32[]{:S(2)}) collective-permute-start(f32[136,128]{1,0:T(8,128)S(1)} %get-tuple-element.88.mine), channel_id=1, source_target_pairs={{0,4},{4,0},{1,5},{5,1},{2,6},{6,2},{3,7},{7,3},{8,12},{12,8},{9,1... | collective-permute-start | bytes 208904 | tf_op jit(solution)/shard_map/ppermute | solution.py:541
  156.0 1.4 shard_map.115
  (74 shorter events, 18.1 us)
Async XLA Ops:
  1.4 1.0 copy-start.2
  2.5 0.7 copy-start.3
  5.0 9.9 %collective-permute-start = (f32[264,128]{1,0:T(8,128)S(1)}, f32[264,128]{1,0:T(8,128)S(1)}, u32[]{:S(2)}, u32[]{:S(2)}) collective-permute-start(f32[264,128]{1,0:T(8,128)S(1)} %get-tuple-element.49), channel_id=1, source_target_pairs={{0,1},{1,2},{2,3},{3,0},{4,5},{5,6},{6,7},{7,4},{8,9},{9,10},{10,1... | collective-permute-start | bytes 405512 | tf_op jit(solution)/shard_map/ppermute | solution.py:532
  7.6 9.2 %collective-permute-start.1 = (f32[264,128]{1,0:T(8,128)S(1)}, f32[264,128]{1,0:T(8,128)S(1)}, u32[]{:S(2)}, u32[]{:S(2)}) collective-permute-start(f32[264,128]{1,0:T(8,128)S(1)} %get-tuple-element.50), channel_id=1, source_target_pairs={{0,2},{1,3},{2,0},{3,1},{4,6},{5,7},{6,4},{7,5},{8,10},{9,11},{10,... | collective-permute-start | bytes 405512 | tf_op jit(solution)/shard_map/ppermute | solution.py:532
  10.9 5.9 %collective-permute-start.2 = (f32[264,128]{1,0:T(8,128)S(1)}, f32[264,128]{1,0:T(8,128)S(1)}, u32[]{:S(2)}, u32[]{:S(2)}) collective-permute-start(f32[264,128]{1,0:T(8,128)S(1)} %get-tuple-element.51), channel_id=1, source_target_pairs={{0,3},{1,0},{2,1},{3,2},{4,7},{5,4},{6,5},{7,6},{8,11},{9,8},{10,9... | collective-permute-start | bytes 405512 | tf_op jit(solution)/shard_map/ppermute | solution.py:532
  11.6 1.2 copy-start
  14.1 11.5 %collective-permute-start.6 = (f32[128,256]{1,0:T(8,128)S(1)}, f32[128,256]{1,0:T(8,128)S(1)}, u32[]{:S(2)}, u32[]{:S(2)}) collective-permute-start(f32[128,256]{1,0:T(8,128)S(1)} %get-tuple-element.55), channel_id=1, source_target_pairs={{0,1},{1,2},{2,3},{3,0},{4,5},{5,6},{6,7},{7,4},{8,9},{9,10},{10,1... | collective-permute-start | bytes 393224 | tf_op jit(solution)/shard_map/ppermute | solution.py:532
  20.1 16.8 %collective-permute-start.5 = (f32[264,128]{1,0:T(8,128)S(1)}, f32[264,128]{1,0:T(8,128)S(1)}, u32[]{:S(2)}, u32[]{:S(2)}) collective-permute-start(f32[264,128]{1,0:T(8,128)S(1)} %shard_map.94.e0.packed), channel_id=1, source_target_pairs={{0,3},{1,0},{2,1},{3,2},{4,7},{5,4},{6,5},{7,6},{8,11},{9,8},{10,9... | collective-permute-start | bytes 405512 | tf_op jit(solution)/shard_map/ppermute | solution.py:532
  22.6 14.3 %collective-permute-start.4 = (f32[264,128]{1,0:T(8,128)S(1)}, f32[264,128]{1,0:T(8,128)S(1)}, u32[]{:S(2)}, u32[]{:S(2)}) collective-permute-start(f32[264,128]{1,0:T(8,128)S(1)} %shard_map.94.e0.packed), channel_id=1, source_target_pairs={{0,2},{1,3},{2,0},{3,1},{4,6},{5,7},{6,4},{7,5},{8,10},{9,11},{10,... | collective-permute-start | bytes 405512 | tf_op jit(solution)/shard_map/ppermute | solution.py:532
  23.6 13.3 %collective-permute-start.3 = (f32[264,128]{1,0:T(8,128)S(1)}, f32[264,128]{1,0:T(8,128)S(1)}, u32[]{:S(2)}, u32[]{:S(2)}) collective-permute-start(f32[264,128]{1,0:T(8,128)S(1)} %shard_map.94.e0.packed), channel_id=1, source_target_pairs={{0,1},{1,2},{2,3},{3,0},{4,5},{5,6},{6,7},{7,4},{8,9},{9,10},{10,1... | collective-permute-start | bytes 405512 | tf_op jit(solution)/shard_map/ppermute | solution.py:532
  23.6 9.7 %collective-permute-start.7 = (f32[128,256]{1,0:T(8,128)S(1)}, f32[128,256]{1,0:T(8,128)S(1)}, u32[]{:S(2)}, u32[]{:S(2)}) collective-permute-start(f32[128,256]{1,0:T(8,128)S(1)} %get-tuple-element.56), channel_id=1, source_target_pairs={{0,2},{1,3},{2,0},{3,1},{4,6},{5,7},{6,4},{7,5},{8,10},{9,11},{10,... | collective-permute-start | bytes 393224 | tf_op jit(solution)/shard_map/ppermute | solution.py:532
  25.5 8.4 %collective-permute-start.8 = (f32[128,256]{1,0:T(8,128)S(1)}, f32[128,256]{1,0:T(8,128)S(1)}, u32[]{:S(2)}, u32[]{:S(2)}) collective-permute-start(f32[128,256]{1,0:T(8,128)S(1)} %get-tuple-element.57), channel_id=1, source_target_pairs={{0,3},{1,0},{2,1},{3,2},{4,7},{5,4},{6,5},{7,6},{8,11},{9,8},{10,9... | collective-permute-start | bytes 393224 | tf_op jit(solution)/shard_map/ppermute | solution.py:532
  42.5 12.2 %collective-permute-start.9 = (f32[256,256]{1,0:T(8,128)S(1)}, f32[256,256]{1,0:T(8,128)S(1)}, u32[]{:S(2)}, u32[]{:S(2)}) collective-permute-start(f32[256,256]{1,0:T(8,128)S(1)} %get-tuple-element.59.mine), channel_id=1, source_target_pairs={{0,4},{4,0},{1,5},{5,1},{2,6},{6,2},{3,7},{7,3},{8,12},{12,8},{9,1... | collective-permute-start | bytes 786440 | tf_op jit(solution)/shard_map/ppermute | solution.py:541
  44.4 3.3 %collective-permute-start.12 = (f32[8,256]{1,0:T(8,128)S(1)}, f32[8,256]{1,0:T(8,128)S(1)}, u32[]{:S(2)}, u32[]{:S(2)}) collective-permute-start(f32[8,256]{1,0:T(8,128)S(1)} %get-tuple-element.61.v0), channel_id=1, source_target_pairs={{0,3},{1,0},{2,1},{3,2},{4,7},{5,4},{6,5},{7,6},{8,11},{9,8},{10,9... | collective-permute-start | bytes 24584 | tf_op jit(solution)/shard_map/ppermute | solution.py:532
  46.9 4.0 %collective-permute-start.11 = (f32[8,256]{1,0:T(8,128)S(1)}, f32[8,256]{1,0:T(8,128)S(1)}, u32[]{:S(2)}, u32[]{:S(2)}) collective-permute-start(f32[8,256]{1,0:T(8,128)S(1)} %get-tuple-element.61.v0), channel_id=1, source_target_pairs={{0,2},{1,3},{2,0},{3,1},{4,6},{5,7},{6,4},{7,5},{8,10},{9,11},{10,... | collective-permute-start | bytes 24584 | tf_op jit(solution)/shard_map/ppermute | solution.py:532
  47.1 3.8 %collective-permute-start.10 = (f32[8,256]{1,0:T(8,128)S(1)}, f32[8,256]{1,0:T(8,128)S(1)}, u32[]{:S(2)}, u32[]{:S(2)}) collective-permute-start(f32[8,256]{1,0:T(8,128)S(1)} %get-tuple-element.61.v0), channel_id=1, source_target_pairs={{0,1},{1,2},{2,3},{3,0},{4,5},{5,6},{6,7},{7,4},{8,9},{9,10},{10,1... | collective-permute-start | bytes 24584 | tf_op jit(solution)/shard_map/ppermute | solution.py:532
  51.9 2.8 %collective-permute-start.13 = (f32[8,256]{1,0:T(8,128)S(1)}, f32[8,256]{1,0:T(8,128)S(1)}, u32[]{:S(2)}, u32[]{:S(2)}) collective-permute-start(f32[8,256]{1,0:T(8,128)S(1)} %get-tuple-element.62.v_mine), channel_id=1, source_target_pairs={{0,4},{4,0},{1,5},{5,1},{2,6},{6,2},{3,7},{7,3},{8,12},{12,8},{9,1... | collective-permute-start | bytes 24584 | tf_op jit(solution)/shard_map/ppermute | solution.py:541
  55.6 8.1 %collective-permute-start.16 = (f32[136,256]{1,0:T(8,128)S(1)}, f32[136,256]{1,0:T(8,128)S(1)}, u32[]{:S(2)}, u32[]{:S(2)}) collective-permute-start(f32[136,256]{1,0:T(8,128)S(1)} %get-tuple-element.64), channel_id=1, source_target_pairs={{0,24},{8,0},{16,8},{24,16},{1,25},{9,1},{17,9},{25,17},{2,26},{10... | collective-permute-start | bytes 417800 | tf_op jit(solution)/shard_map/ppermute | solution.py:532
  58.1 6.9 %collective-permute-start.15 = (f32[136,256]{1,0:T(8,128)S(1)}, f32[136,256]{1,0:T(8,128)S(1)}, u32[]{:S(2)}, u32[]{:S(2)}) collective-permute-start(f32[136,256]{1,0:T(8,128)S(1)} %get-tuple-element.64), channel_id=1, source_target_pairs={{0,16},{8,24},{16,0},{24,8},{1,17},{9,25},{17,1},{25,9},{2,18},{10... | collective-permute-start | bytes 417800 | tf_op jit(solution)/shard_map/ppermute | solution.py:532
  58.6 9.6 %collective-permute-start.14 = (f32[136,256]{1,0:T(8,128)S(1)}, f32[136,256]{1,0:T(8,128)S(1)}, u32[]{:S(2)}, u32[]{:S(2)}) collective-permute-start(f32[136,256]{1,0:T(8,128)S(1)} %get-tuple-element.64), channel_id=1, source_target_pairs={{0,8},{8,16},{16,24},{24,0},{1,9},{9,17},{17,25},{25,1},{2,10},{10... | collective-permute-start | bytes 417800 | tf_op jit(solution)/shard_map/ppermute | solution.py:532
  63.6 5.1 %collective-permute-start.19 = (f32[136,256]{1,0:T(8,128)S(1)}, f32[136,256]{1,0:T(8,128)S(1)}, u32[]{:S(2)}, u32[]{:S(2)}) collective-permute-start(f32[136,256]{1,0:T(8,128)S(1)} %collective-permute-done.16.m3), channel_id=1, source_target_pairs={{0,4},{4,0},{1,5},{5,1},{2,6},{6,2},{3,7},{7,3},{8,12},{12,8},{9,1... | collective-permute-start | bytes 417800 | tf_op jit(solution)/shard_map/ppermute | solution.py:541
  65.0 3.7 %collective-permute-start.18 = (f32[136,256]{1,0:T(8,128)S(1)}, f32[136,256]{1,0:T(8,128)S(1)}, u32[]{:S(2)}, u32[]{:S(2)}) collective-permute-start(f32[136,256]{1,0:T(8,128)S(1)} %collective-permute-done.15.m2), channel_id=1, source_target_pairs={{0,4},{4,0},{1,5},{5,1},{2,6},{6,2},{3,7},{7,3},{8,12},{12,8},{9,1... | collective-permute-start | bytes 417800 | tf_op jit(solution)/shard_map/ppermute | solution.py:541
  68.2 1.5 collective-permute-start.17
  71.2 8.4 %collective-permute-start.22 = (f32[136,256]{1,0:T(8,128)S(1)}, f32[136,256]{1,0:T(8,128)S(1)}, u32[]{:S(2)}, u32[]{:S(2)}) collective-permute-start(f32[136,256]{1,0:T(8,128)S(1)} %get-tuple-element.66), channel_id=1, source_target_pairs={{0,96},{32,0},{64,32},{96,64},{1,97},{33,1},{65,33},{97,65},{2,98}... | collective-permute-start | bytes 417800 | tf_op jit(solution)/shard_map/ppermute | solution.py:532
  74.0 6.9 %collective-permute-start.21 = (f32[136,256]{1,0:T(8,128)S(1)}, f32[136,256]{1,0:T(8,128)S(1)}, u32[]{:S(2)}, u32[]{:S(2)}) collective-permute-start(f32[136,256]{1,0:T(8,128)S(1)} %get-tuple-element.66), channel_id=1, source_target_pairs={{0,64},{32,96},{64,0},{96,32},{1,65},{33,97},{65,1},{97,33},{2,66}... | collective-permute-start | bytes 417800 | tf_op jit(solution)/shard_map/ppermute | solution.py:532
  74.3 9.7 %collective-permute-start.20 = (f32[136,256]{1,0:T(8,128)S(1)}, f32[136,256]{1,0:T(8,128)S(1)}, u32[]{:S(2)}, u32[]{:S(2)}) collective-permute-start(f32[136,256]{1,0:T(8,128)S(1)} %get-tuple-element.66), channel_id=1, source_target_pairs={{0,32},{32,64},{64,96},{96,0},{1,33},{33,65},{65,97},{97,1},{2,34}... | collective-permute-start | bytes 417800 | tf_op jit(solution)/shard_map/ppermute | solution.py:532
  75.0 11.0 %collective-permute-start.28 = (f32[128,256]{1,0:T(8,128)S(1)}, f32[128,256]{1,0:T(8,128)S(1)}, u32[]{:S(2)}, u32[]{:S(2)}) collective-permute-start(f32[128,256]{1,0:T(8,128)S(1)} %get-tuple-element.70.p0), channel_id=1, source_target_pairs={{0,3},{1,0},{2,1},{3,2},{4,7},{5,4},{6,5},{7,6},{8,11},{9,8},{10,9... | collective-permute-start | bytes 393224 | tf_op jit(solution)/shard_map/ppermute | solution.py:532
  79.5 14.8 %collective-permute-start.25 = (f32[136,256]{1,0:T(8,128)S(1)}, f32[136,256]{1,0:T(8,128)S(1)}, u32[]{:S(2)}, u32[]{:S(2)}) collective-permute-start(f32[136,256]{1,0:T(8,128)S(1)} %collective-permute-done.22.m3), channel_id=1, source_target_pairs={{0,4},{4,0},{1,5},{5,1},{2,6},{6,2},{3,7},{7,3},{8,12},{12,8},{9,1... | collective-permute-start | bytes 417800 | tf_op jit(solution)/shard_map/ppermute | solution.py:541
  80.9 13.5 %collective-permute-start.24 = (f32[136,256]{1,0:T(8,128)S(1)}, f32[136,256]{1,0:T(8,128)S(1)}, u32[]{:S(2)}, u32[]{:S(2)}) collective-permute-start(f32[136,256]{1,0:T(8,128)S(1)} %collective-permute-done.21.m2), channel_id=1, source_target_pairs={{0,4},{4,0},{1,5},{5,1},{2,6},{6,2},{3,7},{7,3},{8,12},{12,8},{9,1... | collective-permute-start | bytes 417800 | tf_op jit(solution)/shard_map/ppermute | solution.py:541
  84.1 10.3 %collective-permute-start.23 = (f32[136,256]{1,0:T(8,128)S(1)}, f32[136,256]{1,0:T(8,128)S(1)}, u32[]{:S(2)}, u32[]{:S(2)}) collective-permute-start(f32[136,256]{1,0:T(8,128)S(1)} %collective-permute-done.20.m1), channel_id=1, source_target_pairs={{0,4},{4,0},{1,5},{5,1},{2,6},{6,2},{3,7},{7,3},{8,12},{12,8},{9,1... | collective-permute-start | bytes 417800 | tf_op jit(solution)/shard_map/ppermute | solution.py:541
  84.6 6.5 %collective-permute-start.27 = (f32[128,256]{1,0:T(8,128)S(1)}, f32[128,256]{1,0:T(8,128)S(1)}, u32[]{:S(2)}, u32[]{:S(2)}) collective-permute-start(f32[128,256]{1,0:T(8,128)S(1)} %get-tuple-element.70.p0), channel_id=1, source_target_pairs={{0,2},{1,3},{2,0},{3,1},{4,6},{5,7},{6,4},{7,5},{8,10},{9,11},{10,... | collective-permute-start | bytes 393224 | tf_op jit(solution)/shard_map/ppermute | solution.py:532
  86.1 8.2 %collective-permute-start.26 = (f32[128,256]{1,0:T(8,128)S(1)}, f32[128,256]{1,0:T(8,128)S(1)}, u32[]{:S(2)}, u32[]{:S(2)}) collective-permute-start(f32[128,256]{1,0:T(8,128)S(1)} %get-tuple-element.70.p0), channel_id=1, source_target_pairs={{0,1},{1,2},{2,3},{3,0},{4,5},{5,6},{6,7},{7,4},{8,9},{9,10},{10,1... | collective-permute-start | bytes 393224 | tf_op jit(solution)/shard_map/ppermute | solution.py:532
  99.2 1.4 collective-permute-start.29
  101.3 2.5 %collective-permute-start.32 = (f32[8,256]{1,0:T(8,128)S(1)}, f32[8,256]{1,0:T(8,128)S(1)}, u32[]{:S(2)}, u32[]{:S(2)}) collective-permute-start(f32[8,256]{1,0:T(8,128)S(1)} %shard_map.103.q0), channel_id=1, source_target_pairs={{0,24},{8,0},{16,8},{24,16},{1,25},{9,1},{17,9},{25,17},{2,26},{10... | collective-permute-start | bytes 24584 | tf_op jit(solution)/shard_map/ppermute | solution.py:532
  101.6 4.0 %collective-permute-start.31 = (f32[8,256]{1,0:T(8,128)S(1)}, f32[8,256]{1,0:T(8,128)S(1)}, u32[]{:S(2)}, u32[]{:S(2)}) collective-permute-start(f32[8,256]{1,0:T(8,128)S(1)} %shard_map.103.q0), channel_id=1, source_target_pairs={{0,16},{8,24},{16,0},{24,8},{1,17},{9,25},{17,1},{25,9},{2,18},{10... | collective-permute-start | bytes 24584 | tf_op jit(solution)/shard_map/ppermute | solution.py:532
  102.1 4.1 %collective-permute-start.30 = (f32[8,256]{1,0:T(8,128)S(1)}, f32[8,256]{1,0:T(8,128)S(1)}, u32[]{:S(2)}, u32[]{:S(2)}) collective-permute-start(f32[8,256]{1,0:T(8,128)S(1)} %shard_map.103.q0), channel_id=1, source_target_pairs={{0,8},{8,16},{16,24},{24,0},{1,9},{9,17},{17,25},{25,1},{2,10},{10... | collective-permute-start | bytes 24584 | tf_op jit(solution)/shard_map/ppermute | solution.py:532
  107.1 3.3 %collective-permute-start.35 = (f32[8,256]{1,0:T(8,128)S(1)}, f32[8,256]{1,0:T(8,128)S(1)}, u32[]{:S(2)}, u32[]{:S(2)}) collective-permute-start(f32[8,256]{1,0:T(8,128)S(1)} %get-tuple-element.74.gy0), channel_id=1, source_target_pairs={{0,96},{32,0},{64,32},{96,64},{1,97},{33,1},{65,33},{97,65},{2,98}... | collective-permute-start | bytes 24584 | tf_op jit(solution)/shard_map/ppermute | solution.py:532
  108.0 4.0 %collective-permute-start.34 = (f32[8,256]{1,0:T(8,128)S(1)}, f32[8,256]{1,0:T(8,128)S(1)}, u32[]{:S(2)}, u32[]{:S(2)}) collective-permute-start(f32[8,256]{1,0:T(8,128)S(1)} %get-tuple-element.74.gy0), channel_id=1, source_target_pairs={{0,64},{32,96},{64,0},{96,32},{1,65},{33,97},{65,1},{97,33},{2,66}... | collective-permute-start | bytes 24584 | tf_op jit(solution)/shard_map/ppermute | solution.py:532
  108.0 4.1 %collective-permute-start.33 = (f32[8,256]{1,0:T(8,128)S(1)}, f32[8,256]{1,0:T(8,128)S(1)}, u32[]{:S(2)}, u32[]{:S(2)}) collective-permute-start(f32[8,256]{1,0:T(8,128)S(1)} %get-tuple-element.74.gy0), channel_id=1, source_target_pairs={{0,32},{32,64},{64,96},{96,0},{1,33},{33,65},{65,97},{97,1},{2,34}... | collective-permute-start | bytes 24584 | tf_op jit(solution)/shard_map/ppermute | solution.py:532
  112.1 4.8 %copy-start.1 = (bf16[512,1024]{1,0:T(8,128)(2,1)S(1)}, bf16[512,1024]{1,0:T(8,128)(2,1)}, u32[]{:S(2)}) copy-start(bf16[512,1024]{1,0:T(8,128)(2,1)} %observed.5) | copy-start | bytes 3145732
  118.2 4.8 %collective-permute-start.36 = (f32[16,64,128]{2,1,0:T(8,128)S(1)}, f32[16,64,128]{2,1,0:T(8,128)S(1)}, u32[]{:S(2)}, u32[]{:S(2)}) collective-permute-start(f32[16,64,128]{2,1,0:T(8,128)S(1)} %get-tuple-element.85), channel_id=1, source_target_pairs={{0,4},{4,0},{1,5},{5,1},{2,6},{6,2},{3,7},{7,3},{8,12},{12,8},{9,1... | collective-permute-start | bytes 1572872 | tf_op jit(solution)/shard_map/ppermute | solution.py:541
  123.9 5.2 %copy-start.4 = (s32[8]{0:T(128)S(1)}, s32[8]{0:T(128)}, u32[]{:S(2)}) copy-start(s32[8]{0:T(128)} %panel_of.1) | copy-start | bytes 100
  123.9 33.4 %all-to-all-start = ((f32[16,64,128]{2,1,0:T(8,128)}), f32[16,64,128]{2,1,0:T(8,128)S(1)}, u32[]{:S(2)}, u32[]{:S(2)}) async-start(f32[16,64,128]{2,1,0:T(8,128)} %shard_map.108), calls=%async_computation | async-start | bytes 1048576 | tf_op jit(solution)/shard_map/all_to_all | solution.py:626
  128.2 3.5 %collective-permute-start.37 = (f32[136,128]{1,0:T(8,128)S(1)}, f32[136,128]{1,0:T(8,128)S(1)}, u32[]{:S(2)}, u32[]{:S(2)}) collective-permute-start(f32[136,128]{1,0:T(8,128)S(1)} %get-tuple-element.87), channel_id=1, source_target_pairs={{0,4},{4,0},{1,5},{5,1},{2,6},{6,2},{3,7},{7,3},{8,12},{12,8},{9,1... | collective-permute-start | bytes 208904 | tf_op jit(solution)/shard_map/ppermute | solution.py:541
  130.5 1.2 collective-permute-start.38
  131.7 5.4 %collective-permute-start.41 = (f32[144,128]{1,0:T(8,128)S(1)}, f32[144,128]{1,0:T(8,128)S(1)}, u32[]{:S(2)}, u32[]{:S(2)}) collective-permute-start(f32[144,128]{1,0:T(8,128)S(1)} %shard_map.112.a), channel_id=1, source_target_pairs={{0,24},{8,0},{16,8},{24,16},{1,25},{9,1},{17,9},{25,17},{2,26},{10... | collective-permute-start | bytes 221192 | tf_op jit(solution)/shard_map/ppermute | solution.py:532
  134.6 5.0 %collective-permute-start.40 = (f32[144,128]{1,0:T(8,128)S(1)}, f32[144,128]{1,0:T(8,128)S(1)}, u32[]{:S(2)}, u32[]{:S(2)}) collective-permute-start(f32[144,128]{1,0:T(8,128)S(1)} %shard_map.112.a), channel_id=1, source_target_pairs={{0,16},{8,24},{16,0},{24,8},{1,17},{9,25},{17,1},{25,9},{2,18},{10... | collective-permute-start | bytes 221192 | tf_op jit(solution)/shard_map/ppermute | solution.py:532
  135.2 6.4 %collective-permute-start.39 = (f32[144,128]{1,0:T(8,128)S(1)}, f32[144,128]{1,0:T(8,128)S(1)}, u32[]{:S(2)}, u32[]{:S(2)}) collective-permute-start(f32[144,128]{1,0:T(8,128)S(1)} %shard_map.112.a), channel_id=1, source_target_pairs={{0,8},{8,16},{16,24},{24,0},{1,9},{9,17},{17,25},{25,1},{2,10},{10... | collective-permute-start | bytes 221192 | tf_op jit(solution)/shard_map/ppermute | solution.py:532
  141.6 3.9 %collective-permute-start.44 = (f32[144,128]{1,0:T(8,128)S(1)}, f32[144,128]{1,0:T(8,128)S(1)}, u32[]{:S(2)}, u32[]{:S(2)}) collective-permute-start(f32[144,128]{1,0:T(8,128)S(1)} %shard_map.113.a), channel_id=1, source_target_pairs={{0,96},{32,0},{64,32},{96,64},{1,97},{33,1},{65,33},{97,65},{2,98}... | collective-permute-start | bytes 221192 | tf_op jit(solution)/shard_map/ppermute | solution.py:532
  144.0 4.8 %collective-permute-start.43 = (f32[144,128]{1,0:T(8,128)S(1)}, f32[144,128]{1,0:T(8,128)S(1)}, u32[]{:S(2)}, u32[]{:S(2)}) collective-permute-start(f32[144,128]{1,0:T(8,128)S(1)} %shard_map.113.a), channel_id=1, source_target_pairs={{0,64},{32,96},{64,0},{96,32},{1,65},{33,97},{65,1},{97,33},{2,66}... | collective-permute-start | bytes 221192 | tf_op jit(solution)/shard_map/ppermute | solution.py:532
  144.6 5.3 %collective-permute-start.42 = (f32[144,128]{1,0:T(8,128)S(1)}, f32[144,128]{1,0:T(8,128)S(1)}, u32[]{:S(2)}, u32[]{:S(2)}) collective-permute-start(f32[144,128]{1,0:T(8,128)S(1)} %shard_map.113.a), channel_id=1, source_target_pairs={{0,32},{32,64},{64,96},{96,0},{1,33},{33,65},{65,97},{97,1},{2,34}... | collective-permute-start | bytes 221192 | tf_op jit(solution)/shard_map/ppermute | solution.py:532
  149.9 5.2 %collective-permute-start.48 = (f32[8,128]{1,0:T(8,128)S(1)}, f32[8,128]{1,0:T(8,128)S(1)}, u32[]{:S(2)}, u32[]{:S(2)}) collective-permute-start(f32[8,128]{1,0:T(8,128)S(1)} %get-tuple-element.89.s0), channel_id=1, source_target_pairs={{0,3},{1,0},{2,1},{3,2},{4,7},{5,4},{6,5},{7,6},{8,11},{9,8},{10,9... | collective-permute-start | bytes 12296 | tf_op jit(solution)/shard_map/ppermute | solution.py:532
  150.2 4.8 %collective-permute-start.47 = (f32[8,128]{1,0:T(8,128)S(1)}, f32[8,128]{1,0:T(8,128)S(1)}, u32[]{:S(2)}, u32[]{:S(2)}) collective-permute-start(f32[8,128]{1,0:T(8,128)S(1)} %get-tuple-element.89.s0), channel_id=1, source_target_pairs={{0,2},{1,3},{2,0},{3,1},{4,6},{5,7},{6,4},{7,5},{8,10},{9,11},{10,... | collective-permute-start | bytes 12296 | tf_op jit(solution)/shard_map/ppermute | solution.py:532
  151.8 3.7 %collective-permute-start.46 = (f32[8,128]{1,0:T(8,128)S(1)}, f32[8,128]{1,0:T(8,128)S(1)}, u32[]{:S(2)}, u32[]{:S(2)}) collective-permute-start(f32[8,128]{1,0:T(8,128)S(1)} %get-tuple-element.89.s0), channel_id=1, source_target_pairs={{0,1},{1,2},{2,3},{3,0},{4,5},{5,6},{6,7},{7,4},{8,9},{9,10},{10,1... | collective-permute-start | bytes 12296 | tf_op jit(solution)/shard_map/ppermute | solution.py:532
  152.3 3.7 %collective-permute-start.45 = (f32[136,128]{1,0:T(8,128)S(1)}, f32[136,128]{1,0:T(8,128)S(1)}, u32[]{:S(2)}, u32[]{:S(2)}) collective-permute-start(f32[136,128]{1,0:T(8,128)S(1)} %get-tuple-element.88.mine), channel_id=1, source_target_pairs={{0,4},{4,0},{1,5},{5,1},{2,6},{6,2},{3,7},{7,3},{8,12},{12,8},{9,1... | collective-permute-start | bytes 208904 | tf_op jit(solution)/shard_map/ppermute | solution.py:541
